TPU v7x, 768 devices: a whole 4x8x12 slice. The times are simulated.
768 devices in a mesh: blk: 64 (over x, y, core), sub: 12 (over z).
Axes of the slice: x: 4, y: 8, z: 12, core: 2. Of those that a mesh axis runs over, the one named last changes fastest.
Arguments:
- flow_state: float32 [6, 512, 8, 1536], P(None, 'blk', None, 'sub'), may hold values from -6 to 6
- timestep: float32 [512, 8, 1536], P('blk', None, 'sub'), may hold values from 0.05 to 0.3
- coupling: float32 [3, 6, 6], replicated, may hold values from -2.5 to 2.5
- face_type: int32 [64, 2], P('blk'), may hold values from 0 to 3
- face_rot: int32 [64, 2], P('blk'), may hold values from 0 to 3
Outputs:
- updated: float32 [6, 512, 8, 1536], P(None, 'blk', None, 'sub')
- fine_residual: float32 [6, 512, 8, 1536], P(None, 'blk', None, 'sub')
All inputs are finite; a program needn't handle non-finite values.
Results may differ from a plain program's by a relative error of at most 0.0003.
Values sent between devices are 32-bit elements; how exact they have to be, the bound alone decides.
No kernel may reach another device: no remote copies, remote signals or barrier semaphores. Data moves between devices by JAX's collectives and lax.ppermute only.
A program may use at most 64 MiB of HBM per device.

v0:
```python
import jax
import jax.numpy as jnp
from jax import lax
from jax.sharding import PartitionSpec as P

DAMP_TWO = 0.05
DAMP_FOUR = 0.02
SECTION_COEFFS = (0.4, 1.0)
PRECISE = lax.Precision.HIGHEST


def padded_2(x, sides, width):
    edges = {}
    for axis, dim in sides:
        peers, length = (lax.axis_size(axis), x.shape[dim])
        up = [(i, (i + 1) % peers) for i in range(peers)]
        last = lax.slice_in_dim(x, length - width, length, axis=dim)
        leading = lax.slice_in_dim(x, 0, width, axis=dim)
        edges[dim] = (
            lax.ppermute(last, axis, up),
            lax.ppermute(leading, axis, [(b, a) for a, b in up]),
        )
    done = []
    for _, dim in sides:
        low, high = edges[dim]
        around = [(width, width) if d in done else (0, 0) for d in range(x.ndim)]
        x = jnp.concatenate([jnp.pad(low, around), x, jnp.pad(high, around)], axis=dim)
        done.append(dim)
    return x


def rotate_plane(plane, rot_code):
    flipped = jnp.where(rot_code % 2 == 1, plane[:, :, ::-1, :], plane)
    turned = jnp.stack([flipped[0], flipped[1], -flipped[3], flipped[2], flipped[4], flipped[5]])
    return jnp.where(rot_code // 2 % 2 == 1, turned, flipped)


def mirrored(rows_in, negated):
    sign_row = jnp.where(jnp.arange(6) == negated, -1.0, 1.0).astype(jnp.float32)
    return rows_in * sign_row[:, None, None, None]


def lower_ghosts(block_cells, prev_last, next_first, kind_code, rot_code):
    wall_rows = mirrored(block_cells[:, :2][:, ::-1], 1)
    picked = jnp.where(
        kind_code == 0,
        prev_last,
        jnp.where(
            kind_code == 1,
            next_first[:, ::-1],
            jnp.where(kind_code == 2, wall_rows, jnp.zeros_like(wall_rows)),
        ),
    )
    return rotate_plane(picked, rot_code)


def upper_ghosts(block_cells, prev_last, next_first, kind_code, rot_code):
    wall_rows = mirrored(block_cells[:, -2:][:, ::-1], 1)
    picked = jnp.where(
        kind_code == 0,
        next_first,
        jnp.where(
            kind_code == 1,
            prev_last[:, ::-1],
            jnp.where(kind_code == 2, wall_rows, jnp.zeros_like(wall_rows)),
        ),
    )
    return rotate_plane(picked, rot_code)


def flux_of(padded, coupling, direction):
    mixed = jnp.einsum("uv,vijk->uijk", coupling[direction], padded, precision=PRECISE)
    return mixed + 0.5 * padded[1 + direction][None] * padded


def divergence(padded, coupling, direction):
    axis_pos = direction + 1
    length = padded.shape[axis_pos] - 4
    fluxes = flux_of(padded, coupling, direction)
    face_count = length + 1

    def cut_axis(array, offset, amount):
        return lax.slice_in_dim(array, offset, offset + amount, axis=axis_pos)

    near_left = cut_axis(padded, 1, face_count)
    near_right = cut_axis(padded, 2, face_count)
    far_left = cut_axis(padded, 0, face_count)
    far_right = cut_axis(padded, 3, face_count)
    face_flux = (
        0.5 * (cut_axis(fluxes, 1, face_count) + cut_axis(fluxes, 2, face_count))
        - DAMP_TWO * (near_right - near_left)
        + DAMP_FOUR * (far_right - 3.0 * near_right + 3.0 * near_left - far_left)
    )
    return cut_axis(face_flux, 1, length) - cut_axis(face_flux, 0, length)


def cell_residual(along_i, along_k, block_cells, coupling):
    low_j = mirrored(block_cells[:, :, :2][:, :, ::-1], 2)
    high_j = mirrored(block_cells[:, :, -2:][:, :, ::-1], 2)
    along_j = jnp.concatenate([low_j, block_cells, high_j], axis=2)
    return (
        divergence(along_i, coupling, 0)
        + divergence(along_j, coupling, 1)
        + divergence(along_k, coupling, 2)
    )


def from_halo(raw_i, along_k, block_cells, coupling, face_type, face_rot):
    prev_last = raw_i[:, :2]
    next_first = raw_i[:, -2:]
    low_ghost = lower_ghosts(block_cells, prev_last, next_first, face_type[0, 0], face_rot[0, 0])
    high_ghost = upper_ghosts(block_cells, prev_last, next_first, face_type[0, 1], face_rot[0, 1])
    along_i = jnp.concatenate([low_ghost, block_cells, high_ghost], axis=1)
    return cell_residual(along_i, along_k, block_cells, coupling)


def clear_ends(padded, width):
    final_index = lax.axis_size("sub") - 1
    position = lax.axis_index("sub")
    columns = jnp.arange(padded.shape[3])
    outside = (columns < width) & (position == 0) | (columns >= padded.shape[3] - width) & (
        position == final_index
    )
    return jnp.where(outside[None, None, None, :], 0.0, padded)


def restrict(array):
    shape_of = array.shape
    leading = shape_of[:-3]
    reshaped = array.reshape(
        leading + (shape_of[-3] // 2, 2, shape_of[-2] // 2, 2, shape_of[-1] // 2, 2)
    )
    return reshaped.mean(axis=(-5, -3, -1))


def prolong(array):
    return jnp.repeat(jnp.repeat(jnp.repeat(array, 2, axis=-3), 2, axis=-2), 2, axis=-1)


def body(flow_state, timestep, coupling, face_type, face_rot):
    fine_state = flow_state
    for section_alpha in SECTION_COEFFS:
        fine_padded = padded_2(fine_state, (("blk", 1), ("sub", 3)), 2)
        fine_padded = clear_ends(fine_padded, 2)
        fine_state = flow_state - section_alpha * timestep[None] * from_halo(
            fine_padded[:, :, :, 2:-2],
            fine_padded[:, 2:-2],
            fine_state,
            coupling,
            face_type,
            face_rot,
        )
    coarse_start = restrict(fine_state)
    coarse_step = restrict(timestep)
    padded = padded_2(fine_state, (("blk", 1), ("sub", 3)), 2)
    padded = clear_ends(padded, 2)
    residual_now = from_halo(
        padded[:, :, :, 2:-2], padded[:, 2:-2], fine_state, coupling, face_type, face_rot
    )
    coarse_pad = padded_2(coarse_start, (("blk", 1), ("sub", 3)), 2)
    coarse_pad = clear_ends(coarse_pad, 2)
    start_residual = from_halo(
        coarse_pad[:, :, :, 2:-2], coarse_pad[:, 2:-2], coarse_start, coupling, face_type, face_rot
    )
    forcing = start_residual - restrict(residual_now)
    coarse = coarse_start
    for section_alpha in SECTION_COEFFS:
        coarse_padded = padded_2(coarse, (("blk", 1), ("sub", 3)), 2)
        coarse_padded = clear_ends(coarse_padded, 2)
        coarse = coarse_start - section_alpha * coarse_step[None] * (
            from_halo(
                coarse_padded[:, :, :, 2:-2],
                coarse_padded[:, 2:-2],
                coarse,
                coupling,
                face_type,
                face_rot,
            )
            - forcing
        )
    updated = fine_state + prolong(coarse - coarse_start)
    return (updated, residual_now)


def solution(mesh):
    return jax.shard_map(
        body,
        mesh=mesh,
        in_specs=(
            P(None, "blk", None, "sub"),
            P("blk", None, "sub"),
            P(),
            P("blk", None),
            P("blk", None),
        ),
        out_specs=(P(None, "blk", None, "sub"), P(None, "blk", None, "sub")),
        check_vma=False,
    )
```

profile of v0, /device:TPU:192, one launch (start us, length us, event | category | flops | bytes accessed | tf_op | source)
XLA Modules:
  0.0 149.6 jit_solution(24085971179929819)
XLA Ops:
  0.7 1.0 copy.137
  1.7 1.9 %collective-permute-start.1 = (f32[6,2,8,128]{3,1,2,0:T(2,128)S(1)}, f32[6,2,8,128]{3,1,2,0:T(2,128)S(1)}, u32[]{:S(2)}, u32[]{:S(2)}) collective-permute-start(f32[6,2,8,128]{3,1,2,0:T(2,128)S(1)} %get-tuple-element.40), channel_id=1, source_target_pairs={{0,12},{12,24},{24,36},{36,48},{48,60},{60,72},{72,84},{84,96},{96... | collective-permute-start | bytes 147464 | tf_op jit(solution)/shard_map/ppermute | solution.py:20
  3.6 7.0 %collective-permute-start.2 = (f32[6,2,8,128]{3,1,2,0:T(2,128)S(1)}, f32[6,2,8,128]{3,1,2,0:T(2,128)}, u32[]{:S(2)}, u32[]{:S(2)}) collective-permute-start(f32[6,2,8,128]{3,1,2,0:T(2,128)S(1)} %get-tuple-element.41), channel_id=1, source_target_pairs={{12,0},{24,12},{36,24},{48,36},{60,48},{72,60},{84,72},{96,84},{10... | collective-permute-start | bytes 147464 | tf_op jit(solution)/shard_map/ppermute | solution.py:21
  10.7 5.5 %collective-permute-start = (f32[6,8,8,2]{3,1,2,0:T(8,128)S(1)}, f32[6,8,8,2]{3,1,2,0:T(8,128)S(1)}, u32[]{:S(2)}, u32[]{:S(2)}) collective-permute-start(f32[6,8,8,2]{3,1,2,0:T(8,128)S(1)} %get-tuple-element.42), channel_id=1, source_target_pairs={{0,1},{1,2},{2,3},{3,4},{4,5},{5,6},{6,7},{7,8},{8,9},{9,10},{10,1... | collective-permute-start | bytes 9224 | tf_op jit(solution)/shard_map/ppermute | solution.py:20
  16.2 1.9 %collective-permute-start.3 = (f32[6,8,8,2]{3,1,2,0:T(8,128)S(1)}, f32[6,8,8,2]{3,1,2,0:T(8,128)S(1)}, u32[]{:S(2)}, u32[]{:S(2)}) collective-permute-start(f32[6,8,8,2]{3,1,2,0:T(8,128)S(1)} %get-tuple-element.43), channel_id=1, source_target_pairs={{1,0},{2,1},{3,2},{4,3},{5,4},{6,5},{7,6},{8,7},{9,8},{10,9},{11,1... | collective-permute-start | bytes 9224 | tf_op jit(solution)/shard_map/ppermute | solution.py:21
  18.2 0.8 broadcast_multiply_fusion.1
  19.0 2.8 %reshape.73 = f32[4,2,4,2,64,2]{5,4,3,2,1,0:T(8,128)S(1)} reshape(f32[8,8,128]{2,1,0:T(8,128)} %param.6) | data formatting | bytes 65536 | tf_op jit(solution)/shard_map/reshape | solution.py:130
  22.5 0.6 fusion.224
  23.2 0.6 fusion.59
  33.7 1.4 fusion.8
  36.0 0.6 fusion.61
  37.3 0.8 fusion.13
  39.4 0.6 fusion.55
  40.1 1.9 %collective-permute-start.5 = (f32[6,2,8,128]{3,1,2,0:T(2,128)S(1)}, f32[6,2,8,128]{3,1,2,0:T(2,128)S(1)}, u32[]{:S(2)}, u32[]{:S(2)}) collective-permute-start(f32[6,2,8,128]{3,1,2,0:T(2,128)S(1)} %get-tuple-element.34), channel_id=1, source_target_pairs={{0,12},{12,24},{24,36},{36,48},{48,60},{60,72},{72,84},{84,96},{96... | collective-permute-start | bytes 147464 | tf_op jit(solution)/shard_map/ppermute | solution.py:20
  42.0 7.0 %collective-permute-start.6 = (f32[6,2,8,128]{3,1,2,0:T(2,128)S(1)}, f32[6,2,8,128]{3,1,2,0:T(2,128)S(1)}, u32[]{:S(2)}, u32[]{:S(2)}) collective-permute-start(f32[6,2,8,128]{3,1,2,0:T(2,128)S(1)} %get-tuple-element.35), channel_id=1, source_target_pairs={{12,0},{24,12},{36,24},{48,36},{60,48},{72,60},{84,72},{96,84},{10... | collective-permute-start | bytes 147464 | tf_op jit(solution)/shard_map/ppermute | solution.py:21
  49.0 5.1 %collective-permute-start.4 = (f32[6,8,8,2]{3,1,2,0:T(8,128)S(1)}, f32[6,8,8,2]{3,1,2,0:T(8,128)S(1)}, u32[]{:S(2)}, u32[]{:S(2)}) collective-permute-start(f32[6,8,8,2]{3,1,2,0:T(8,128)S(1)} %get-tuple-element.36), channel_id=1, source_target_pairs={{0,1},{1,2},{2,3},{3,4},{4,5},{5,6},{6,7},{7,8},{8,9},{9,10},{10,1... | collective-permute-start | bytes 9224 | tf_op jit(solution)/shard_map/ppermute | solution.py:20
  54.2 2.1 %collective-permute-start.7 = (f32[6,8,8,2]{3,1,2,0:T(8,128)S(1)}, f32[6,8,8,2]{3,1,2,0:T(8,128)S(1)}, u32[]{:S(2)}, u32[]{:S(2)}) collective-permute-start(f32[6,8,8,2]{3,1,2,0:T(8,128)S(1)} %get-tuple-element.37), channel_id=1, source_target_pairs={{1,0},{2,1},{3,2},{4,3},{5,4},{6,5},{7,6},{8,7},{9,8},{10,9},{11,1... | collective-permute-start | bytes 9224 | tf_op jit(solution)/shard_map/ppermute | solution.py:21
  57.3 5.6 %collective-permute-done.7 = f32[6,8,8,2]{3,1,2,0:T(8,128)S(1)} collective-permute-done((f32[6,8,8,2]{3,1,2,0:T(8,128)S(1)}, f32[6,8,8,2]{3,1,2,0:T(8,128)S(1)}, u32[]{:S(2)}, u32[]{:S(2)}) %collective-permute-start.7) | collective-permute-done | bytes 3104 | tf_op jit(solution)/shard_map/ppermute | solution.py:21
  62.9 0.6 fusion.7
  64.5 0.6 fusion.57
  65.8 0.8 fusion.11
  67.8 1.9 %collective-permute-start.13 = (f32[6,2,8,128]{3,1,2,0:T(2,128)S(1)}, f32[6,2,8,128]{3,1,2,0:T(2,128)S(1)}, u32[]{:S(2)}, u32[]{:S(2)}) collective-permute-start(f32[6,2,8,128]{3,1,2,0:T(2,128)S(1)} %get-tuple-element.28), channel_id=1, source_target_pairs={{0,12},{12,24},{24,36},{36,48},{48,60},{60,72},{72,84},{84,96},{96... | collective-permute-start | bytes 147464 | tf_op jit(solution)/shard_map/ppermute | solution.py:20
  69.8 0.6 fusion.51
  70.5 2.7 %copy.138 = f32[6,8,8,128]{0,3,2,1:T(8,128)} copy(f32[6,8,8,128]{3,1,2,0:T(8,128)S(1)} %fusion.94) | data formatting | bytes 393216 | tf_op jit(solution)/shard_map/sub | solution.py:145
  73.1 4.8 %reduce_sum.27 = f32[6,4,4,64]{0,3,2,1:T(8,128)S(1)} reduce(f32[6,4,2,4,2,64,2]{0,6,5,4,3,2,1:T(2,128)} %bitcast.127, f32[]{:T(128)} %constant.168.clone.1), dimensions={2,4,6}, to_apply=%region_0.1 | reduce | flops 43008 | bytes 221188 | tf_op jit(solution)/shard_map/reduce_sum | solution.py:133
  78.6 1.9 %collective-permute-start.9 = (f32[6,2,4,64]{3,0,2,1:T(8,128)S(1)}, f32[6,2,4,64]{3,0,2,1:T(8,128)S(1)}, u32[]{:S(2)}, u32[]{:S(2)}) collective-permute-start(f32[6,2,4,64]{3,0,2,1:T(8,128)S(1)} %get-tuple-element.60), channel_id=1, source_target_pairs={{0,12},{12,24},{24,36},{36,48},{48,60},{60,72},{72,84},{84,96},{96... | collective-permute-start | bytes 36872 | tf_op jit(solution)/shard_map/ppermute | solution.py:20
  80.5 7.0 %collective-permute-start.10 = (f32[6,2,4,64]{3,0,2,1:T(8,128)S(1)}, f32[6,2,4,64]{3,0,2,1:T(8,128)S(1)}, u32[]{:S(2)}, u32[]{:S(2)}) collective-permute-start(f32[6,2,4,64]{3,0,2,1:T(8,128)S(1)} %get-tuple-element.61), channel_id=1, source_target_pairs={{12,0},{24,12},{36,24},{48,36},{60,48},{72,60},{84,72},{96,84},{10... | collective-permute-start | bytes 36872 | tf_op jit(solution)/shard_map/ppermute | solution.py:21
  88.0 2.3 %collective-permute-start.8 = (f32[6,4,4,2]{3,0,2,1:T(8,128)S(1)}, f32[6,4,4,2]{3,0,2,1:T(8,128)S(1)}, u32[]{:S(2)}, u32[]{:S(2)}) collective-permute-start(f32[6,4,4,2]{3,0,2,1:T(8,128)S(1)} %get-tuple-element.62), channel_id=1, source_target_pairs={{0,1},{1,2},{2,3},{3,4},{4,5},{5,6},{6,7},{7,8},{8,9},{9,10},{10,1... | collective-permute-start | bytes 2312 | tf_op jit(solution)/shard_map/ppermute | solution.py:20
  90.2 3.6 %collective-permute-start.11 = (f32[6,4,4,2]{3,0,2,1:T(8,128)S(1)}, f32[6,4,4,2]{3,0,2,1:T(8,128)S(1)}, u32[]{:S(2)}, u32[]{:S(2)}) collective-permute-start(f32[6,4,4,2]{3,0,2,1:T(8,128)S(1)} %get-tuple-element.63), channel_id=1, source_target_pairs={{1,0},{2,1},{3,2},{4,3},{5,4},{6,5},{7,6},{8,7},{9,8},{10,9},{11,1... | collective-permute-start | bytes 2312 | tf_op jit(solution)/shard_map/ppermute | solution.py:21
  94.1 1.9 %collective-permute-start.14 = (f32[6,2,8,128]{3,1,2,0:T(2,128)S(1)}, f32[6,2,8,128]{3,1,2,0:T(2,128)S(1)}, u32[]{:S(2)}, u32[]{:S(2)}) collective-permute-start(f32[6,2,8,128]{3,1,2,0:T(2,128)S(1)} %get-tuple-element.29), channel_id=1, source_target_pairs={{12,0},{24,12},{36,24},{48,36},{60,48},{72,60},{84,72},{96,84},{10... | collective-permute-start | bytes 147464 | tf_op jit(solution)/shard_map/ppermute | solution.py:21
  96.0 1.6 %collective-permute-done.11 = f32[6,4,4,2]{3,0,2,1:T(8,128)S(1)} collective-permute-done((f32[6,4,4,2]{3,0,2,1:T(8,128)S(1)}, f32[6,4,4,2]{3,0,2,1:T(8,128)S(1)}, u32[]{:S(2)}, u32[]{:S(2)}) %collective-permute-start.11) | collective-permute-done | bytes 800 | tf_op jit(solution)/shard_map/ppermute | solution.py:21
  97.6 3.4 %collective-permute-start.12 = (f32[6,8,8,2]{3,1,2,0:T(8,128)S(1)}, f32[6,8,8,2]{3,1,2,0:T(8,128)S(1)}, u32[]{:S(2)}, u32[]{:S(2)}) collective-permute-start(f32[6,8,8,2]{3,1,2,0:T(8,128)S(1)} %get-tuple-element.30), channel_id=1, source_target_pairs={{0,1},{1,2},{2,3},{3,4},{4,5},{5,6},{6,7},{7,8},{8,9},{9,10},{10,1... | collective-permute-start | bytes 9224 | tf_op jit(solution)/shard_map/ppermute | solution.py:20
  101.0 2.7 %collective-permute-start.15 = (f32[6,8,8,2]{3,1,2,0:T(8,128)S(1)}, f32[6,8,8,2]{3,1,2,0:T(8,128)S(1)}, u32[]{:S(2)}, u32[]{:S(2)}) collective-permute-start(f32[6,8,8,2]{3,1,2,0:T(8,128)S(1)} %get-tuple-element.31), channel_id=1, source_target_pairs={{1,0},{2,1},{3,2},{4,3},{5,4},{6,5},{7,6},{8,7},{9,8},{10,9},{11,1... | collective-permute-start | bytes 9224 | tf_op jit(solution)/shard_map/ppermute | solution.py:21
  105.2 4.5 %collective-permute-done.15 = f32[6,8,8,2]{3,1,2,0:T(8,128)S(1)} collective-permute-done((f32[6,8,8,2]{3,1,2,0:T(8,128)S(1)}, f32[6,8,8,2]{3,1,2,0:T(8,128)S(1)}, u32[]{:S(2)}, u32[]{:S(2)}) %collective-permute-start.15) | collective-permute-done | bytes 3104 | tf_op jit(solution)/shard_map/ppermute | solution.py:21
  111.3 0.6 fusion.53
  112.6 0.8 fusion.9
  114.4 2.7 %copy.146 = f32[6,8,8,128]{0,3,2,1:T(8,128)} copy(f32[6,8,8,128]{3,1,2,0:T(8,128)S(1)} %fusion.90) | data formatting | bytes 393216 | tf_op jit(solution)/shard_map/add | solution.py:102
  117.1 4.8 %reduce_sum.29 = f32[6,4,4,64]{0,3,2,1:T(8,128)S(1)} reduce(f32[6,4,2,4,2,64,2]{0,6,5,4,3,2,1:T(2,128)} %bitcast.126, f32[]{:T(128)} %constant.168.clone.1), dimensions={2,4,6}, to_apply=%region_2.3 | reduce | flops 43008 | bytes 221188 | tf_op jit(solution)/shard_map/reduce_sum | solution.py:133
  122.4 1.9 %collective-permute-start.17 = (f32[6,2,4,64]{3,0,2,1:T(8,128)S(1)}, f32[6,2,4,64]{3,0,2,1:T(8,128)S(1)}, u32[]{:S(2)}, u32[]{:S(2)}) collective-permute-start(f32[6,2,4,64]{3,0,2,1:T(8,128)S(1)} %get-tuple-element.54), channel_id=1, source_target_pairs={{0,12},{12,24},{24,36},{36,48},{48,60},{60,72},{72,84},{84,96},{96... | collective-permute-start | bytes 36872 | tf_op jit(solution)/shard_map/ppermute | solution.py:20
  124.3 7.0 %collective-permute-start.18 = (f32[6,2,4,64]{3,0,2,1:T(8,128)S(1)}, f32[6,2,4,64]{3,0,2,1:T(8,128)S(1)}, u32[]{:S(2)}, u32[]{:S(2)}) collective-permute-start(f32[6,2,4,64]{3,0,2,1:T(8,128)S(1)} %get-tuple-element.55), channel_id=1, source_target_pairs={{12,0},{24,12},{36,24},{48,36},{60,48},{72,60},{84,72},{96,84},{10... | collective-permute-start | bytes 36872 | tf_op jit(solution)/shard_map/ppermute | solution.py:21
  131.7 3.9 %collective-permute-start.16 = (f32[6,4,4,2]{3,0,2,1:T(8,128)S(1)}, f32[6,4,4,2]{3,0,2,1:T(8,128)S(1)}, u32[]{:S(2)}, u32[]{:S(2)}) collective-permute-start(f32[6,4,4,2]{3,0,2,1:T(8,128)S(1)} %get-tuple-element.56), channel_id=1, source_target_pairs={{0,1},{1,2},{2,3},{3,4},{4,5},{5,6},{6,7},{7,8},{8,9},{9,10},{10,1... | collective-permute-start | bytes 2312 | tf_op jit(solution)/shard_map/ppermute | solution.py:20
  135.6 1.9 %collective-permute-start.19 = (f32[6,4,4,2]{3,0,2,1:T(8,128)S(1)}, f32[6,4,4,2]{3,0,2,1:T(8,128)S(1)}, u32[]{:S(2)}, u32[]{:S(2)}) collective-permute-start(f32[6,4,4,2]{3,0,2,1:T(8,128)S(1)} %get-tuple-element.57), channel_id=1, source_target_pairs={{1,0},{2,1},{3,2},{4,3},{5,4},{6,5},{7,6},{8,7},{9,8},{10,9},{11,1... | collective-permute-start | bytes 2312 | tf_op jit(solution)/shard_map/ppermute | solution.py:21
  137.6 0.7 copy.152
  138.3 4.7 %collective-permute-done.19 = f32[6,4,4,2]{3,0,2,1:T(8,128)S(1)} collective-permute-done((f32[6,4,4,2]{3,0,2,1:T(8,128)S(1)}, f32[6,4,4,2]{3,0,2,1:T(8,128)S(1)}, u32[]{:S(2)}, u32[]{:S(2)}) %collective-permute-start.19) | collective-permute-done | bytes 800 | tf_op jit(solution)/shard_map/ppermute | solution.py:21
  144.4 1.7 %copy.149 = f32[6,8,8,64]{2,1,3,0:T(8,128)} copy(f32[6,8,8,64]{3,1,2,0:T(8,128)S(1)} %bitcast.129) | data formatting | bytes 196608 | tf_op jit(solution)/shard_map/reshape | solution.py:137
  146.1 1.6 %broadcast_in_dim.145 = f32[6,8,8,64,2]{2,1,4,3,0:T(8,128)S(1)} broadcast(f32[6,8,8,64]{2,1,3,0:T(8,128)} %copy.149), dimensions={0,1,2,3} | broadcast | bytes 294912 | tf_op jit(solution)/shard_map/broadcast_in_dim | solution.py:137
  147.7 1.1 copy.150
  148.9 0.7 copy.151
  (193 shorter events, 16.1 us)
Async XLA Ops:
  0.6 21.2 %copy-start.5 = (s32[1,2]{1,0:T(1,128)S(1)}, s32[1,2]{1,0:T(1,128)}, u32[]{:S(2)}) copy-start(s32[1,2]{1,0:T(1,128)} %param.8) | copy-start | bytes 28
  0.6 21.8 %copy-start.6 = (s32[1,2]{1,0:T(1,128)S(1)}, s32[1,2]{1,0:T(1,128)}, u32[]{:S(2)}) copy-start(s32[1,2]{1,0:T(1,128)} %param.9) | copy-start | bytes 28
  0.7 22.5 %copy-start.1 = (f32[3,6,6]{2,1,0:T(8,128)S(1)}, f32[3,6,6]{2,1,0:T(8,128)}, u32[]{:S(2)}) copy-start(f32[3,6,6]{2,1,0:T(8,128)} %param.7) | copy-start | bytes 1300
  1.7 32.0 %collective-permute-start.1 = (f32[6,2,8,128]{3,1,2,0:T(2,128)S(1)}, f32[6,2,8,128]{3,1,2,0:T(2,128)S(1)}, u32[]{:S(2)}, u32[]{:S(2)}) collective-permute-start(f32[6,2,8,128]{3,1,2,0:T(2,128)S(1)} %get-tuple-element.40), channel_id=1, source_target_pairs={{0,12},{12,24},{24,36},{36,48},{48,60},{60,72},{72,84},{84,96},{96... | collective-permute-start | bytes 147464 | tf_op jit(solution)/shard_map/ppermute | solution.py:20
  3.6 30.1 %collective-permute-start.2 = (f32[6,2,8,128]{3,1,2,0:T(2,128)S(1)}, f32[6,2,8,128]{3,1,2,0:T(2,128)}, u32[]{:S(2)}, u32[]{:S(2)}) collective-permute-start(f32[6,2,8,128]{3,1,2,0:T(2,128)S(1)} %get-tuple-element.41), channel_id=1, source_target_pairs={{12,0},{24,12},{36,24},{48,36},{60,48},{72,60},{84,72},{96,84},{10... | collective-permute-start | bytes 147464 | tf_op jit(solution)/shard_map/ppermute | solution.py:21
  10.7 22.9 %collective-permute-start = (f32[6,8,8,2]{3,1,2,0:T(8,128)S(1)}, f32[6,8,8,2]{3,1,2,0:T(8,128)S(1)}, u32[]{:S(2)}, u32[]{:S(2)}) collective-permute-start(f32[6,8,8,2]{3,1,2,0:T(8,128)S(1)} %get-tuple-element.42), channel_id=1, source_target_pairs={{0,1},{1,2},{2,3},{3,4},{4,5},{5,6},{6,7},{7,8},{8,9},{9,10},{10,1... | collective-permute-start | bytes 9224 | tf_op jit(solution)/shard_map/ppermute | solution.py:20
  16.2 17.4 %collective-permute-start.3 = (f32[6,8,8,2]{3,1,2,0:T(8,128)S(1)}, f32[6,8,8,2]{3,1,2,0:T(8,128)S(1)}, u32[]{:S(2)}, u32[]{:S(2)}) collective-permute-start(f32[6,8,8,2]{3,1,2,0:T(8,128)S(1)} %get-tuple-element.43), channel_id=1, source_target_pairs={{1,0},{2,1},{3,2},{4,3},{5,4},{6,5},{7,6},{8,7},{9,8},{10,9},{11,1... | collective-permute-start | bytes 9224 | tf_op jit(solution)/shard_map/ppermute | solution.py:21
  18.2 5.8 %copy-start.3 = (f32[6]{0:T(128)}, f32[6]{0:T(128)S(1)}, u32[]{:S(2)}) copy-start(f32[6]{0:T(128)S(1)} %compare_select_fusion) | copy-start | bytes 76
  21.8 11.5 %copy-start.2 = (f32[8,8,128]{2,1,0:T(8,128)S(1)}, f32[8,8,128]{2,1,0:T(8,128)}, u32[]{:S(2)}) copy-start(f32[8,8,128]{2,1,0:T(8,128)} %param.6) | copy-start | bytes 98308
  37.0 2.1 %copy-start = (f32[6,8,8,128]{3,2,1,0:T(8,128)S(1)}, f32[6,8,8,128]{3,2,1,0:T(8,128)}, u32[]{:S(2)}) copy-start(f32[6,8,8,128]{3,2,1,0:T(8,128)} %param.5) | copy-start | bytes 589828
  38.2 1.1 copy-start.4
  40.1 22.8 %collective-permute-start.5 = (f32[6,2,8,128]{3,1,2,0:T(2,128)S(1)}, f32[6,2,8,128]{3,1,2,0:T(2,128)S(1)}, u32[]{:S(2)}, u32[]{:S(2)}) collective-permute-start(f32[6,2,8,128]{3,1,2,0:T(2,128)S(1)} %get-tuple-element.34), channel_id=1, source_target_pairs={{0,12},{12,24},{24,36},{36,48},{48,60},{60,72},{72,84},{84,96},{96... | collective-permute-start | bytes 147464 | tf_op jit(solution)/shard_map/ppermute | solution.py:20
  42.0 20.9 %collective-permute-start.6 = (f32[6,2,8,128]{3,1,2,0:T(2,128)S(1)}, f32[6,2,8,128]{3,1,2,0:T(2,128)S(1)}, u32[]{:S(2)}, u32[]{:S(2)}) collective-permute-start(f32[6,2,8,128]{3,1,2,0:T(2,128)S(1)} %get-tuple-element.35), channel_id=1, source_target_pairs={{12,0},{24,12},{36,24},{48,36},{60,48},{72,60},{84,72},{96,84},{10... | collective-permute-start | bytes 147464 | tf_op jit(solution)/shard_map/ppermute | solution.py:21
  49.0 8.3 %collective-permute-start.4 = (f32[6,8,8,2]{3,1,2,0:T(8,128)S(1)}, f32[6,8,8,2]{3,1,2,0:T(8,128)S(1)}, u32[]{:S(2)}, u32[]{:S(2)}) collective-permute-start(f32[6,8,8,2]{3,1,2,0:T(8,128)S(1)} %get-tuple-element.36), channel_id=1, source_target_pairs={{0,1},{1,2},{2,3},{3,4},{4,5},{5,6},{6,7},{7,8},{8,9},{9,10},{10,1... | collective-permute-start | bytes 9224 | tf_op jit(solution)/shard_map/ppermute | solution.py:20
  54.2 8.8 %collective-permute-start.7 = (f32[6,8,8,2]{3,1,2,0:T(8,128)S(1)}, f32[6,8,8,2]{3,1,2,0:T(8,128)S(1)}, u32[]{:S(2)}, u32[]{:S(2)}) collective-permute-start(f32[6,8,8,2]{3,1,2,0:T(8,128)S(1)} %get-tuple-element.37), channel_id=1, source_target_pairs={{1,0},{2,1},{3,2},{4,3},{5,4},{6,5},{7,6},{8,7},{9,8},{10,9},{11,1... | collective-permute-start | bytes 9224 | tf_op jit(solution)/shard_map/ppermute | solution.py:21
  67.8 42.0 %collective-permute-start.13 = (f32[6,2,8,128]{3,1,2,0:T(2,128)S(1)}, f32[6,2,8,128]{3,1,2,0:T(2,128)S(1)}, u32[]{:S(2)}, u32[]{:S(2)}) collective-permute-start(f32[6,2,8,128]{3,1,2,0:T(2,128)S(1)} %get-tuple-element.28), channel_id=1, source_target_pairs={{0,12},{12,24},{24,36},{36,48},{48,60},{60,72},{72,84},{84,96},{96... | collective-permute-start | bytes 147464 | tf_op jit(solution)/shard_map/ppermute | solution.py:20
  78.6 22.4 %collective-permute-start.9 = (f32[6,2,4,64]{3,0,2,1:T(8,128)S(1)}, f32[6,2,4,64]{3,0,2,1:T(8,128)S(1)}, u32[]{:S(2)}, u32[]{:S(2)}) collective-permute-start(f32[6,2,4,64]{3,0,2,1:T(8,128)S(1)} %get-tuple-element.60), channel_id=1, source_target_pairs={{0,12},{12,24},{24,36},{36,48},{48,60},{60,72},{72,84},{84,96},{96... | collective-permute-start | bytes 36872 | tf_op jit(solution)/shard_map/ppermute | solution.py:20
  80.5 23.1 %collective-permute-start.10 = (f32[6,2,4,64]{3,0,2,1:T(8,128)S(1)}, f32[6,2,4,64]{3,0,2,1:T(8,128)S(1)}, u32[]{:S(2)}, u32[]{:S(2)}) collective-permute-start(f32[6,2,4,64]{3,0,2,1:T(8,128)S(1)} %get-tuple-element.61), channel_id=1, source_target_pairs={{12,0},{24,12},{36,24},{48,36},{60,48},{72,60},{84,72},{96,84},{10... | collective-permute-start | bytes 36872 | tf_op jit(solution)/shard_map/ppermute | solution.py:21
  88.0 6.2 %collective-permute-start.8 = (f32[6,4,4,2]{3,0,2,1:T(8,128)S(1)}, f32[6,4,4,2]{3,0,2,1:T(8,128)S(1)}, u32[]{:S(2)}, u32[]{:S(2)}) collective-permute-start(f32[6,4,4,2]{3,0,2,1:T(8,128)S(1)} %get-tuple-element.62), channel_id=1, source_target_pairs={{0,1},{1,2},{2,3},{3,4},{4,5},{5,6},{6,7},{7,8},{8,9},{9,10},{10,1... | collective-permute-start | bytes 2312 | tf_op jit(solution)/shard_map/ppermute | solution.py:20
  90.2 7.4 %collective-permute-start.11 = (f32[6,4,4,2]{3,0,2,1:T(8,128)S(1)}, f32[6,4,4,2]{3,0,2,1:T(8,128)S(1)}, u32[]{:S(2)}, u32[]{:S(2)}) collective-permute-start(f32[6,4,4,2]{3,0,2,1:T(8,128)S(1)} %get-tuple-element.63), channel_id=1, source_target_pairs={{1,0},{2,1},{3,2},{4,3},{5,4},{6,5},{7,6},{8,7},{9,8},{10,9},{11,1... | collective-permute-start | bytes 2312 | tf_op jit(solution)/shard_map/ppermute | solution.py:21
  94.1 15.7 %collective-permute-start.14 = (f32[6,2,8,128]{3,1,2,0:T(2,128)S(1)}, f32[6,2,8,128]{3,1,2,0:T(2,128)S(1)}, u32[]{:S(2)}, u32[]{:S(2)}) collective-permute-start(f32[6,2,8,128]{3,1,2,0:T(2,128)S(1)} %get-tuple-element.29), channel_id=1, source_target_pairs={{12,0},{24,12},{36,24},{48,36},{60,48},{72,60},{84,72},{96,84},{10... | collective-permute-start | bytes 147464 | tf_op jit(solution)/shard_map/ppermute | solution.py:21
  97.6 7.6 %collective-permute-start.12 = (f32[6,8,8,2]{3,1,2,0:T(8,128)S(1)}, f32[6,8,8,2]{3,1,2,0:T(8,128)S(1)}, u32[]{:S(2)}, u32[]{:S(2)}) collective-permute-start(f32[6,8,8,2]{3,1,2,0:T(8,128)S(1)} %get-tuple-element.30), channel_id=1, source_target_pairs={{0,1},{1,2},{2,3},{3,4},{4,5},{5,6},{6,7},{7,8},{8,9},{9,10},{10,1... | collective-permute-start | bytes 9224 | tf_op jit(solution)/shard_map/ppermute | solution.py:20
  101.0 8.8 %collective-permute-start.15 = (f32[6,8,8,2]{3,1,2,0:T(8,128)S(1)}, f32[6,8,8,2]{3,1,2,0:T(8,128)S(1)}, u32[]{:S(2)}, u32[]{:S(2)}) collective-permute-start(f32[6,8,8,2]{3,1,2,0:T(8,128)S(1)} %get-tuple-element.31), channel_id=1, source_target_pairs={{1,0},{2,1},{3,2},{4,3},{5,4},{6,5},{7,6},{8,7},{9,8},{10,9},{11,1... | collective-permute-start | bytes 9224 | tf_op jit(solution)/shard_map/ppermute | solution.py:21
  122.4 20.6 %collective-permute-start.17 = (f32[6,2,4,64]{3,0,2,1:T(8,128)S(1)}, f32[6,2,4,64]{3,0,2,1:T(8,128)S(1)}, u32[]{:S(2)}, u32[]{:S(2)}) collective-permute-start(f32[6,2,4,64]{3,0,2,1:T(8,128)S(1)} %get-tuple-element.54), channel_id=1, source_target_pairs={{0,12},{12,24},{24,36},{36,48},{48,60},{60,72},{72,84},{84,96},{96... | collective-permute-start | bytes 36872 | tf_op jit(solution)/shard_map/ppermute | solution.py:20
  124.3 18.7 %collective-permute-start.18 = (f32[6,2,4,64]{3,0,2,1:T(8,128)S(1)}, f32[6,2,4,64]{3,0,2,1:T(8,128)S(1)}, u32[]{:S(2)}, u32[]{:S(2)}) collective-permute-start(f32[6,2,4,64]{3,0,2,1:T(8,128)S(1)} %get-tuple-element.55), channel_id=1, source_target_pairs={{12,0},{24,12},{36,24},{48,36},{60,48},{72,60},{84,72},{96,84},{10... | collective-permute-start | bytes 36872 | tf_op jit(solution)/shard_map/ppermute | solution.py:21
  131.7 6.6 %collective-permute-start.16 = (f32[6,4,4,2]{3,0,2,1:T(8,128)S(1)}, f32[6,4,4,2]{3,0,2,1:T(8,128)S(1)}, u32[]{:S(2)}, u32[]{:S(2)}) collective-permute-start(f32[6,4,4,2]{3,0,2,1:T(8,128)S(1)} %get-tuple-element.56), channel_id=1, source_target_pairs={{0,1},{1,2},{2,3},{3,4},{4,5},{5,6},{6,7},{7,8},{8,9},{9,10},{10,1... | collective-permute-start | bytes 2312 | tf_op jit(solution)/shard_map/ppermute | solution.py:20
  135.6 7.4 %collective-permute-start.19 = (f32[6,4,4,2]{3,0,2,1:T(8,128)S(1)}, f32[6,4,4,2]{3,0,2,1:T(8,128)S(1)}, u32[]{:S(2)}, u32[]{:S(2)}) collective-permute-start(f32[6,4,4,2]{3,0,2,1:T(8,128)S(1)} %get-tuple-element.57), channel_id=1, source_target_pairs={{1,0},{2,1},{3,2},{4,3},{5,4},{6,5},{7,6},{8,7},{9,8},{10,9},{11,1... | collective-permute-start | bytes 2312 | tf_op jit(solution)/shard_map/ppermute | solution.py:21
where the time goes:
time: 151 us; the launch traced here: 150 us
  starting transfers between devices  71.8 us (48%)
  other arithmetic  22.2 us (15%)
  local copies, waits for them, and re-layouts  19.6 us (13%)
  waiting for transfers between devices  17.3 us (11%)
  between operations  11.1 us (7%)
  matrix products  7.59 us (5%)
    ppermute x10, starting transfers between devices, padded_2(): lax.ppermute(leading, axis, [(b, a) for a, b in up])  42 us
    ppermute x10, starting transfers between devices, padded_2(): lax.ppermute(last, axis, up)  29.8 us
    ppermute x10, waiting for transfers between devices, padded_2(): lax.ppermute(leading, axis, [(b, a) for a, b in up])  16.4 us
    reduce_sum x3, other arithmetic, restrict(): return reshaped.mean(axis=(-5, -3, -1))  9.89 us
    dot_general x15, matrix products, flux_of(): jnp.einsum('uv,vijk->uijk', coupling[direction], padded, precision=PRECISE)  7.59 us
    add x15, other arithmetic, divergence(): 0.5 * (cut_axis(fluxes, 1, face_count) + cut_axis(fluxes, 2, face_count))  3.57 us
  transfers between devices with their start and end apart: 20, of which 7 were waited for; matrix products, arithmetic and copies ran while one was open for 12% of the time, Pallas kernels for 0%

commit v1 on v0

v1 whole, which is shorter than its diff:
```python
import functools

import jax
import jax.numpy as jnp
from jax import lax
from jax.experimental import pallas as pl
from jax.experimental.pallas import tpu as pltpu
from jax.sharding import PartitionSpec as P

NV = 6
NI = 8
HALO = 10
PER = 12
VMEM_LIMIT = 12 * 1024 * 1024

C0, C1, C2 = 0.44, -0.26, 0.04


def iota_j():
    return lax.broadcasted_iota(jnp.int32, (8, 128), 0)


def iota_k():
    return lax.broadcasted_iota(jnp.int32, (8, 128), 1)


def rotl(x, shift):
    return pltpu.roll(x, shift % 128, 1)


def rots(x, shift):
    return pltpu.roll(x, shift % 8, 0)


def reverse_j(x):
    j = iota_j()
    x = rots(x, 4)
    x = jnp.where((j // 2) % 2 == 0, rots(x, -2), rots(x, 2))
    return jnp.where(j % 2 == 0, rots(x, -1), rots(x, 1))


def ghost_rows(own2, prev2, next2, kind, rot):
    nearest = []
    for r in range(2):
        picked = []
        for v in range(NV):
            wall = -own2[r][v] if v == 1 else own2[r][v]
            x = jnp.where(kind == 2, wall, 0.0)
            x = jnp.where(kind == 1, next2[r][v], x)
            x = jnp.where(kind == 0, prev2[r][v], x)
            picked.append(jnp.where(rot % 2 == 1, reverse_j(x), x))
        turn = rot // 2 % 2 == 1
        a, b = picked[2], picked[3]
        picked[2], picked[3] = jnp.where(turn, -b, a), jnp.where(turn, a, b)
        nearest.append(picked)
    return nearest


def with_ghosts(rows, below, above, meta):
    t_lo, t_hi, r_lo, r_hi = meta
    lo = ghost_rows([rows[0], rows[1]], [below[1], below[0]], [above[0], above[1]], t_lo, r_lo)
    hi = ghost_rows([rows[-1], rows[-2]], [above[0], above[1]], [below[1], below[0]], t_hi, r_hi)
    return [lo[1], lo[0]] + rows + [hi[0], hi[1]]


def flux(q, a, d):
    half = 0.5 * q[1 + d]
    out = []
    for u in range(NV):
        acc = (a[d][u][u] + half) * q[u]
        for v in range(NV):
            if v != u:
                acc = acc + a[d][u][v] * q[v]
        out.append(acc)
    return out


def flux_j(q, a):
    out, mirrored = [], []
    for u in range(NV):
        even = None
        for v in range(NV):
            if v != 2:
                term = a[1][u][v] * q[v]
                even = term if even is None else even + term
        if u == 2:
            even = even + 0.5 * (q[2] * q[2])
            odd = a[1][2][2] * q[2]
        else:
            odd = q[2] * (a[1][u][2] + 0.5 * q[u])
        out.append(even + odd)
        mirrored.append(even - odd)
    return out, mirrored


def j_weights(unit):
    j = iota_j() // unit
    n = 8 // unit
    out = []
    for sign in (1.0, -1.0):
        end = (j == 0) | (j == n - 1)
        centre = jnp.where(end, C0 + sign * C1, C0) + 2 * C0
        near = C1 + sign * C2
        below = jnp.where(j == 0, 0.0, jnp.where((j == 1) | (j == n - 1), near, C1))
        above = jnp.where(j == n - 1, 0.0, jnp.where((j == 0) | (j == n - 2), near, C1))
        if n == 4:
            two = None
        else:
            two = (jnp.where(j >= 2, C2, 0.0), jnp.where(j <= n - 3, C2, 0.0))
        out.append((centre, below, above, two))
    return out


def residual2(padded, side, a, unit):
    n = len(padded) - 4
    k = iota_k()
    j = iota_j()
    weights = j_weights(unit)
    first_j, last_j = j < unit, j >= 8 - unit
    low1, low2 = k < unit, k < 2 * unit
    high1, high2 = k >= 128 - unit, k >= 128 - 2 * unit
    fi = {m: flux(padded[m], a, 0) for m in range(1, n + 3)}
    result = []
    for i in range(n):
        m = i + 2
        q = padded[m]
        fj, gj = flux_j(q, a)
        fk = flux(q, a, 2)
        fs = flux(side[i], a, 2)
        row = []
        for u in range(NV):
            x = q[u]
            s = side[i][u]
            centre, below, above, two = weights[1 if u == 2 else 0]
            acc = fi[m + 1][u] - fi[m - 1][u]
            acc = acc + C1 * (padded[m + 1][u] + padded[m - 1][u]) + C2 * (padded[m + 2][u] + padded[m - 2][u])
            acc = acc + centre * x
            acc = acc + below * rots(x, unit) + above * rots(x, -unit)
            if two is None:
                acc = acc + C2 * rots(x, 4)
            else:
                acc = acc + two[0] * rots(x, 2) + two[1] * rots(x, -2)
            up = jnp.where(last_j, gj[u], rots(fj[u], -unit))
            down = jnp.where(first_j, gj[u], rots(fj[u], unit))
            acc = acc + (up - down)
            tx, ts = C1 * x, C1 * s
            acc = acc + rotl(jnp.where(low1, fs[u] + ts, fk[u] + tx), -unit)
            acc = acc - rotl(jnp.where(high1, fs[u] - ts, fk[u] - tx), unit)
            acc = acc + C2 * (rotl(jnp.where(low2, s, x), -2 * unit) + rotl(jnp.where(high2, s, x), 2 * unit))
            row.append(acc)
        result.append(row)
    return result


def pair_mean(a, b):
    x = a + b
    x = x + jnp.where(iota_j() % 2 == 0, rots(x, -1), rots(x, 1))
    x = x + jnp.where(iota_k() % 2 == 0, rotl(x, -1), rotl(x, 1))
    return 0.125 * x


def restrict_rows(rows):
    return [[pair_mean(rows[2 * c][v], rows[2 * c + 1][v]) for v in range(len(rows[0]))] for c in range(len(rows) // 2)]


def load(ref, first, count):
    return [[ref[v, first + r] for v in range(NV)] for r in range(count)]


def store(ref, first, rows):
    for r, row in enumerate(rows):
        for v in range(NV):
            ref[v, first + r] = row[v]


def coefficients(a_ref):
    return [[[a_ref[d, u, v] for v in range(NV)] for u in range(NV)] for d in range(3)]


def meta_of(type_ref, rot_ref):
    return (type_ref[0, 0], type_ref[0, 1], rot_ref[0, 0], rot_ref[0, 1])


def halo_mask():
    k = iota_k()
    s = lax.axis_index("sub")
    last = lax.axis_size("sub") - 1
    return ((k < HALO) & (s != last)) | ((k >= 128 - HALO) & (s != 0))


def neighbours(ga, gb, first):
    even = lax.axis_index("blk") % 2 == 0
    a, b = load(ga, first, 2), load(gb, first, 2)
    below = [[jnp.where(even, b[r][v], a[r][v]) for v in range(NV)] for r in range(2)]
    above = [[jnp.where(even, a[r][v], b[r][v]) for v in range(NV)] for r in range(2)]
    return below, above


def send(ma, mb, first, rows):
    even = lax.axis_index("blk") % 2 == 0
    for r in range(2):
        for v in range(NV):
            lo, hi = rows[r][v], rows[len(rows) - 2 + r][v]
            ma[v, first + r] = jnp.where(even, hi, lo)
            mb[v, first + r] = jnp.where(even, lo, hi)


def pack_kernel(q_ref, dt_ref, ma, mb, to_left, to_right):
    k = iota_k()
    send(ma, mb, 0, load(q_ref, 0, NI))
    tiles = [q_ref[v, i] for v in range(NV) for i in range(NI)] + [dt_ref[i] for i in range(NI)]
    for g in range(-(-len(tiles) // PER)):
        left = right = jnp.zeros((8, 128), jnp.float32)
        for n, x in enumerate(tiles[g * PER : (g + 1) * PER]):
            at = n * HALO
            inside = (k >= at) & (k < at + HALO)
            left = jnp.where(inside, rotl(x, at), left)
            right = jnp.where(inside, rotl(x, at + HALO), right)
        to_left[g] = left
        to_right[g] = right


def unpack(from_right, from_left):
    k = iota_k()
    tiles = []
    for n in range(NV * NI + NI):
        g, at = n // PER, n % PER * HALO
        low = rotl(from_right[g], -at)
        high = rotl(from_left[g], -at - HALO)
        tiles.append(jnp.where(k < HALO, low, jnp.where(k >= 128 - HALO, high, 0.0)))
    return [[tiles[v * NI + i] for v in range(NV)] for i in range(NI)], tiles[NV * NI :]


def advance(start, dt, twice, factor):
    return [[start[i][v] - (0.5 * factor * dt[i]) * twice[i][v] for v in range(NV)] for i in range(len(start))]


def masked(rows):
    inside = halo_mask()
    return [[jnp.where(inside, x, 0.0) for x in row] for row in rows]


def first_kernel(a_ref, type_ref, rot_ref, q_ref, dt_ref, ga, gb, from_right, from_left, t1_ref, h0_ref, dth_ref, ma, mb):
    a, meta = coefficients(a_ref), meta_of(type_ref, rot_ref)
    h0, dth = unpack(from_right, from_left)
    store(h0_ref, 0, h0)
    for i in range(NI):
        dth_ref[i] = dth[i]
    send(ma, mb, 2, h0)
    t0 = load(q_ref, 0, NI)
    below, above = neighbours(ga, gb, 0)
    twice = residual2(with_ghosts(t0, below, above, meta), h0, a, 1)
    t1 = advance(t0, [dt_ref[i] for i in range(NI)], twice, 0.4)
    store(t1_ref, 0, t1)
    send(ma, mb, 0, t1)


def second_kernel(a_ref, type_ref, rot_ref, q_ref, t1_ref, h0_ref, dt_ref, dth_ref, ga, gb, t2_ref, h1_ref, ma, mb):
    a, meta = coefficients(a_ref), meta_of(type_ref, rot_ref)
    t0, h0 = load(q_ref, 0, NI), load(h0_ref, 0, NI)
    below, above = neighbours(ga, gb, 2)
    twice = residual2(with_ghosts(h0, below, above, meta), t0, a, 1)
    h1 = masked(advance(h0, [dth_ref[i] for i in range(NI)], twice, 0.4))
    store(h1_ref, 0, h1)
    send(ma, mb, 2, h1)
    t1 = load(t1_ref, 0, NI)
    below, above = neighbours(ga, gb, 0)
    twice = residual2(with_ghosts(t1, below, above, meta), h1, a, 1)
    t2 = advance(t0, [dt_ref[i] for i in range(NI)], twice, 1.0)
    store(t2_ref, 0, t2)
    send(ma, mb, 0, t2)


def third_kernel(
    a_ref, type_ref, rot_ref, t1_ref, t2_ref, h0_ref, h1_ref, dt_ref, dth_ref, ga, gb, res_ref, h2_ref, c1_ref, ma, mb
):
    a, meta = coefficients(a_ref), meta_of(type_ref, rot_ref)
    h0, h1, t1 = load(h0_ref, 0, NI), load(h1_ref, 0, NI), load(t1_ref, 0, NI)
    below, above = neighbours(ga, gb, 2)
    twice = residual2(with_ghosts(h1, below, above, meta), t1, a, 1)
    h2 = masked(advance(h0, [dth_ref[i] for i in range(NI)], twice, 1.0))
    store(h2_ref, 0, h2)
    send(ma, mb, 4, h2)
    t2 = load(t2_ref, 0, NI)
    below, above = neighbours(ga, gb, 0)
    twice = residual2(with_ghosts(t2, below, above, meta), h2, a, 1)
    res = [[0.5 * x for x in row] for row in twice]
    store(res_ref, 0, res)
    start = restrict_rows(t2)
    mean = restrict_rows(res)
    step = [pair_mean(dt_ref[2 * c], dt_ref[2 * c + 1]) for c in range(NI // 2)]
    c1 = [[start[c][v] - (0.4 * step[c]) * mean[c][v] for v in range(NV)] for c in range(NI // 2)]
    store(c1_ref, 0, c1)
    send(ma, mb, 0, c1)
    send(ma, mb, 2, start)


def fourth_kernel(a_ref, type_ref, rot_ref, t2_ref, h2_ref, res_ref, c1_ref, dt_ref, dth_ref, ga, gb, out_ref):
    a, meta = coefficients(a_ref), meta_of(type_ref, rot_ref)
    half = NI // 2
    h2, t2 = load(h2_ref, 0, NI), load(t2_ref, 0, NI)
    below, above = neighbours(ga, gb, 4)
    twice = residual2(with_ghosts(h2, below, above, meta), t2, a, 1)
    mean = restrict_rows(twice)
    start_h = restrict_rows(h2)
    step_h = [pair_mean(dth_ref[2 * c], dth_ref[2 * c + 1]) for c in range(half)]
    c1_h = masked([[start_h[c][v] - (0.2 * step_h[c]) * mean[c][v] for v in range(NV)] for c in range(half)])
    start = restrict_rows(t2)
    below, above = neighbours(ga, gb, 2)
    twice_start = residual2(with_ghosts(start, below, above, meta), start_h, a, 2)
    c1 = load(c1_ref, 0, half)
    below, above = neighbours(ga, gb, 0)
    twice_c1 = residual2(with_ghosts(c1, below, above, meta), c1_h, a, 2)
    for c in range(half):
        step = pair_mean(dt_ref[2 * c], dt_ref[2 * c + 1])
        for v in range(NV):
            mean_res = pair_mean(res_ref[v, 2 * c], res_ref[v, 2 * c + 1])
            change = -step * (0.5 * (twice_c1[c][v] - twice_start[c][v]) + mean_res)
            out_ref[v, 2 * c] = t2[2 * c][v] + change
            out_ref[v, 2 * c + 1] = t2[2 * c + 1][v] + change


def field(rows):
    return (NV, rows, 8, 128)


def call(kernel, scalars, arrays, outs):
    smem, vmem = pl.BlockSpec(memory_space=pltpu.SMEM), pl.BlockSpec(memory_space=pltpu.VMEM)
    return pl.pallas_call(
        kernel,
        out_shape=[jax.ShapeDtypeStruct(shape, jnp.float32) for shape in outs],
        in_specs=[smem] * len(scalars) + [vmem] * len(arrays),
        out_specs=[vmem] * len(outs),
        compiler_params=pltpu.CompilerParams(vmem_limit_bytes=VMEM_LIMIT),
    )(*scalars, *arrays)


def body(flow_state, timestep, coupling, face_type, face_rot):
    blocks, parts = lax.axis_size("blk"), lax.axis_size("sub")
    chip = [(b, b ^ 1) for b in range(blocks)]
    link = [(b, (b + 1) % blocks if b % 2 else (b - 1) % blocks) for b in range(blocks)]
    ahead = [(s, s + 1) for s in range(parts - 1)]
    back = [(s + 1, s) for s in range(parts - 1)]
    groups = -(-(NV * NI + NI) // PER)
    scalars = (coupling, face_type, face_rot)

    ma, mb, to_left, to_right = call(
        pack_kernel, (), (flow_state, timestep), (field(2), field(2), (groups, 8, 128), (groups, 8, 128))
    )
    ga, gb = lax.ppermute(ma, "blk", chip), lax.ppermute(mb, "blk", link)
    from_right, from_left = lax.ppermute(to_left, "sub", back), lax.ppermute(to_right, "sub", ahead)

    t1, h0, dth, ma, mb = call(
        first_kernel,
        scalars,
        (flow_state, timestep, ga, gb, from_right, from_left),
        (field(NI), field(NI), (NI, 8, 128), field(4), field(4)),
    )
    ga, gb = lax.ppermute(ma, "blk", chip), lax.ppermute(mb, "blk", link)

    t2, h1, ma, mb = call(
        second_kernel,
        scalars,
        (flow_state, t1, h0, timestep, dth, ga, gb),
        (field(NI), field(NI), field(4), field(4)),
    )
    ga, gb = lax.ppermute(ma, "blk", chip), lax.ppermute(mb, "blk", link)

    res, h2, c1, ma, mb = call(
        third_kernel,
        scalars,
        (t1, t2, h0, h1, timestep, dth, ga, gb),
        (field(NI), field(NI), field(NI // 2), field(6), field(6)),
    )
    ga, gb = lax.ppermute(ma, "blk", chip), lax.ppermute(mb, "blk", link)

    (updated,) = call(
        fourth_kernel, scalars, (t2, h2, res, c1, timestep, dth, ga, gb), (field(NI),)
    )
    return (updated, res)


def solution(mesh):
    return jax.shard_map(
        body,
        mesh=mesh,
        in_specs=(
            P(None, "blk", None, "sub"),
            P("blk", None, "sub"),
            P(),
            P("blk", None),
            P("blk", None),
        ),
        out_specs=(P(None, "blk", None, "sub"), P(None, "blk", None, "sub")),
        check_vma=False,
    )
```

time: 151 us -> 68.5 us (0.45)
  the two profiles are of different devices: /device:TPU:192 before, /device:TPU:512 now
where the time goes in v1:
time: 68.5 us; the launch traced here: 68 us
  starting transfers between devices  31.3 us (46%)
  waiting for transfers between devices  22.9 us (33%)
  Pallas kernels  10.4 us (15%)
  local copies, waits for them, and re-layouts  2.62 us (4%)
  between operations  0.8 us (1%)
    ppermute x8, starting transfers between devices, body(): ga, gb = (lax.ppermute(ma, 'blk', chip), lax.ppermute(mb, 'blk', link))  25.4 us
    ppermute x8, waiting for transfers between devices, body(): ga, gb = (lax.ppermute(ma, 'blk', chip), lax.ppermute(mb, 'blk', link))  18.2 us
    pallas_call x5, Pallas kernels, call(): pl.pallas_call(kernel, out_shape=[jax.ShapeDtypeStruct(shape, jnp.float32...  10.4 us
    ppermute x1, waiting for transfers between devices, body(): lax.ppermute(to_right, 'sub', ahead)  4.7 us
    ppermute x1, starting transfers between devices, body(): lax.ppermute(to_left, 'sub', back)  3.67 us
    unnamed x14, local copies, waits for them, and re-layouts  2.62 us
    ppermute x1, starting transfers between devices, body(): lax.ppermute(to_right, 'sub', ahead)  2.17 us
  transfers between devices with their start and end apart: 10, of which 4 were waited for; matrix products, arithmetic and copies ran while one was open for 0% of the time, Pallas kernels for 0%

profile of v1, /device:TPU:512, one launch (start us, length us, event | category | flops | bytes accessed | tf_op | source)
XLA Modules:
  0.0 68.0 jit_solution(7068668413686170669)
XLA Ops:
  0.6 0.0 copy-start
  0.6 0.9 %copy-done = f32[6,8,8,128]{3,2,1,0:T(8,128)S(1)} copy-done((f32[6,8,8,128]{3,2,1,0:T(8,128)S(1)}, f32[6,8,8,128]{3,2,1,0:T(8,128)}, u32[]{:S(2)}) %copy-start) | copy-done | bytes 196632
  1.6 0.0 copy-start.1
  1.6 0.8 %copy-done.1 = f32[8,8,128]{2,1,0:T(8,128)S(1)} copy-done((f32[8,8,128]{2,1,0:T(8,128)S(1)}, f32[8,8,128]{2,1,0:T(8,128)}, u32[]{:S(2)}) %copy-start.1) | copy-done | bytes 32792
  2.3 0.0 copy-start.3
  2.3 0.2 shard_map.68
  2.5 1.9 %collective-permute-start = (f32[6,2,8,128]{3,2,1,0:T(8,128)S(1)}, f32[6,2,8,128]{3,2,1,0:T(8,128)S(1)}, u32[]{:S(2)}, u32[]{:S(2)}) collective-permute-start(f32[6,2,8,128]{3,2,1,0:T(8,128)S(1)} %get-tuple-element.20), channel_id=1, source_target_pairs={{0,12},{12,0},{24,36},{36,24},{48,60},{60,48},{72,84},{84,72},{96,... | collective-permute-start | bytes 147464 | tf_op jit(solution)/shard_map/ppermute | solution.py:350
  4.4 7.7 %collective-permute-start.1 = (f32[6,2,8,128]{3,2,1,0:T(8,128)S(1)}, f32[6,2,8,128]{3,2,1,0:T(8,128)S(1)}, u32[]{:S(2)}, u32[]{:S(2)}) collective-permute-start(f32[6,2,8,128]{3,2,1,0:T(8,128)S(1)} %get-tuple-element.21), channel_id=1, source_target_pairs={{0,756},{12,24},{24,12},{36,48},{48,36},{60,72},{72,60},{84,96},{9... | collective-permute-start | bytes 147464 | tf_op jit(solution)/shard_map/ppermute | solution.py:350
  12.1 0.0 copy-start.5
  12.1 0.0 copy-start.6
  12.1 3.7 %collective-permute-start.2 = (f32[5,8,128]{2,1,0:T(8,128)S(1)}, f32[5,8,128]{2,1,0:T(8,128)S(1)}, u32[]{:S(2)}, u32[]{:S(2)}) collective-permute-start(f32[5,8,128]{2,1,0:T(8,128)S(1)} %get-tuple-element.22), channel_id=1, source_target_pairs={{1,0},{2,1},{3,2},{4,3},{5,4},{6,5},{7,6},{8,7},{9,8},{10,9},{11,1... | collective-permute-start | bytes 61448 | tf_op jit(solution)/shard_map/ppermute | solution.py:351
  15.8 2.2 %collective-permute-start.3 = (f32[5,8,128]{2,1,0:T(8,128)S(1)}, f32[5,8,128]{2,1,0:T(8,128)S(1)}, u32[]{:S(2)}, u32[]{:S(2)}) collective-permute-start(f32[5,8,128]{2,1,0:T(8,128)S(1)} %get-tuple-element.23), channel_id=1, source_target_pairs={{0,1},{1,2},{2,3},{3,4},{4,5},{5,6},{6,7},{7,8},{8,9},{9,10},{10,1... | collective-permute-start | bytes 61448 | tf_op jit(solution)/shard_map/ppermute | solution.py:351
  18.0 0.0 collective-permute-done.2.from_right
  18.0 4.7 %collective-permute-done.3.from_left = f32[5,8,128]{2,1,0:T(8,128)S(1)} collective-permute-done((f32[5,8,128]{2,1,0:T(8,128)S(1)}, f32[5,8,128]{2,1,0:T(8,128)S(1)}, u32[]{:S(2)}, u32[]{:S(2)}) %collective-permute-start.3) | collective-permute-done | bytes 20512 | tf_op jit(solution)/shard_map/ppermute | solution.py:351
  22.7 0.0 collective-permute-done.ga
  22.7 0.0 collective-permute-done.1.gb
  22.7 0.0 copy-done.3
  22.7 0.0 copy-done.5
  22.7 0.0 copy-done.6
  22.7 1.6 %shard_map.69 = (f32[6,8,8,128]{3,2,1,0:T(8,128)S(1)}, f32[6,8,8,128]{3,2,1,0:T(8,128)S(1)}, f32[8,8,128]{2,1,0:T(8,128)S(1)}, f32[6,4,8,128]{3,2,1,0:T(8,128)S(1)}, f32[6,4,8,128]{3,2,1,0:T(8,128)S(1)}) custom-call(f32[3,6,6]{2,1,0:T(8,128)S(1)} %copy-done.3, s32[1,2]{1,0:T(1,128)S(1)} %copy-done.5, s32[1,2]{1,0:T(1,128)S(1)} %copy-done.6, ...), custom_call_target="tpu_custom_call" | custom-call | tf_op jit(solution)/shard_map/pallas_call | solution.py:329
  24.3 1.9 %collective-permute-start.4 = (f32[6,4,8,128]{3,2,1,0:T(8,128)S(1)}, f32[6,4,8,128]{3,2,1,0:T(8,128)S(1)}, u32[]{:S(2)}, u32[]{:S(2)}) collective-permute-start(f32[6,4,8,128]{3,2,1,0:T(8,128)S(1)} %get-tuple-element.27), channel_id=1, source_target_pairs={{0,12},{12,0},{24,36},{36,24},{48,60},{60,48},{72,84},{84,72},{96,... | collective-permute-start | bytes 294920 | tf_op jit(solution)/shard_map/ppermute | solution.py:359
  26.3 3.4 %collective-permute-start.5 = (f32[6,4,8,128]{3,2,1,0:T(8,128)S(1)}, f32[6,4,8,128]{3,2,1,0:T(8,128)S(1)}, u32[]{:S(2)}, u32[]{:S(2)}) collective-permute-start(f32[6,4,8,128]{3,2,1,0:T(8,128)S(1)} %get-tuple-element.28), channel_id=1, source_target_pairs={{0,756},{12,24},{24,12},{36,48},{48,36},{60,72},{72,60},{84,96},{9... | collective-permute-start | bytes 294920 | tf_op jit(solution)/shard_map/ppermute | solution.py:359
  29.6 0.0 collective-permute-done.4.ga
  29.6 5.9 %collective-permute-done.5.gb = f32[6,4,8,128]{3,2,1,0:T(8,128)S(1)} collective-permute-done((f32[6,4,8,128]{3,2,1,0:T(8,128)S(1)}, f32[6,4,8,128]{3,2,1,0:T(8,128)S(1)}, u32[]{:S(2)}, u32[]{:S(2)}) %collective-permute-start.5) | collective-permute-done | bytes 98336 | tf_op jit(solution)/shard_map/ppermute | solution.py:359
  35.5 0.0 copy-start.2
  35.5 2.3 %shard_map.70 = (f32[6,8,8,128]{3,2,1,0:T(8,128)S(1)}, f32[6,8,8,128]{3,2,1,0:T(8,128)S(1)}, f32[6,4,8,128]{3,2,1,0:T(8,128)S(1)}, f32[6,4,8,128]{3,2,1,0:T(8,128)S(1)}) custom-call(f32[3,6,6]{2,1,0:T(8,128)S(1)} %copy-done.3, s32[1,2]{1,0:T(1,128)S(1)} %copy-done.5, s32[1,2]{1,0:T(1,128)S(1)} %copy-done.6, f32[6,8,8,128]{3,2,1,0:T(8,128)S(1)} %copy-done, ...), custom_call_target="tpu_custom_call" | custom-call | tf_op jit(solution)/shard_map/pallas_call | solution.py:329
  37.9 1.9 %collective-permute-start.6 = (f32[6,4,8,128]{3,2,1,0:T(8,128)S(1)}, f32[6,4,8,128]{3,2,1,0:T(8,128)S(1)}, u32[]{:S(2)}, u32[]{:S(2)}) collective-permute-start(f32[6,4,8,128]{3,2,1,0:T(8,128)S(1)} %get-tuple-element.31), channel_id=1, source_target_pairs={{0,12},{12,0},{24,36},{36,24},{48,60},{60,48},{72,84},{84,72},{96,... | collective-permute-start | bytes 294920 | tf_op jit(solution)/shard_map/ppermute | solution.py:367
  39.8 3.4 %collective-permute-start.7 = (f32[6,4,8,128]{3,2,1,0:T(8,128)S(1)}, f32[6,4,8,128]{3,2,1,0:T(8,128)S(1)}, u32[]{:S(2)}, u32[]{:S(2)}) collective-permute-start(f32[6,4,8,128]{3,2,1,0:T(8,128)S(1)} %get-tuple-element.32), channel_id=1, source_target_pairs={{0,756},{12,24},{24,12},{36,48},{48,36},{60,72},{72,60},{84,96},{9... | collective-permute-start | bytes 294920 | tf_op jit(solution)/shard_map/ppermute | solution.py:367
  43.2 0.0 collective-permute-done.6.ga
  43.2 5.9 %collective-permute-done.7.gb = f32[6,4,8,128]{3,2,1,0:T(8,128)S(1)} collective-permute-done((f32[6,4,8,128]{3,2,1,0:T(8,128)S(1)}, f32[6,4,8,128]{3,2,1,0:T(8,128)S(1)}, u32[]{:S(2)}, u32[]{:S(2)}) %collective-permute-start.7) | collective-permute-done | bytes 98336 | tf_op jit(solution)/shard_map/ppermute | solution.py:367
  49.1 0.0 copy-done.2
  49.1 3.0 %shard_map.71 = (f32[6,8,8,128]{3,2,1,0:T(8,128)}, f32[6,8,8,128]{3,2,1,0:T(8,128)S(1)}, f32[6,4,8,128]{3,2,1,0:T(8,128)S(1)}, f32[6,6,8,128]{3,2,1,0:T(8,128)S(1)}, f32[6,6,8,128]{3,2,1,0:T(8,128)S(1)}) custom-call(f32[3,6,6]{2,1,0:T(8,128)S(1)} %copy-done.3, s32[1,2]{1,0:T(1,128)S(1)} %copy-done.5, s32[1,2]{1,0:T(1,128)S(1)} %copy-done.6, ...), custom_call_target="tpu_custom_call" | custom-call | tf_op jit(solution)/shard_map/pallas_call | solution.py:329
  52.1 1.9 %collective-permute-start.8 = (f32[6,6,8,128]{3,2,1,0:T(8,128)S(1)}, f32[6,6,8,128]{3,2,1,0:T(8,128)S(1)}, u32[]{:S(2)}, u32[]{:S(2)}) collective-permute-start(f32[6,6,8,128]{3,2,1,0:T(8,128)S(1)} %get-tuple-element.36), channel_id=1, source_target_pairs={{0,12},{12,0},{24,36},{36,24},{48,60},{60,48},{72,84},{84,72},{96,... | collective-permute-start | bytes 442376 | tf_op jit(solution)/shard_map/ppermute | solution.py:375
  54.0 3.4 %collective-permute-start.9 = (f32[6,6,8,128]{3,2,1,0:T(8,128)S(1)}, f32[6,6,8,128]{3,2,1,0:T(8,128)S(1)}, u32[]{:S(2)}, u32[]{:S(2)}) collective-permute-start(f32[6,6,8,128]{3,2,1,0:T(8,128)S(1)} %get-tuple-element.37), channel_id=1, source_target_pairs={{0,756},{12,24},{24,12},{36,48},{48,36},{60,72},{72,60},{84,96},{9... | collective-permute-start | bytes 442376 | tf_op jit(solution)/shard_map/ppermute | solution.py:375
  57.3 0.0 collective-permute-done.8.ga
  57.4 6.4 %collective-permute-done.9.gb = f32[6,6,8,128]{3,2,1,0:T(8,128)S(1)} collective-permute-done((f32[6,6,8,128]{3,2,1,0:T(8,128)S(1)}, f32[6,6,8,128]{3,2,1,0:T(8,128)S(1)}, u32[]{:S(2)}, u32[]{:S(2)}) %collective-permute-start.9) | collective-permute-done | bytes 147488 | tf_op jit(solution)/shard_map/ppermute | solution.py:375
  63.8 0.0 copy-start.4
  63.8 0.9 %copy-done.4 = f32[6,8,8,128]{3,2,1,0:T(8,128)S(1)} copy-done((f32[6,8,8,128]{3,2,1,0:T(8,128)S(1)}, f32[6,8,8,128]{3,2,1,0:T(8,128)}, u32[]{:S(2)}) %copy-start.4) | copy-done | bytes 196632
  64.7 3.3 %shard_map.72 = f32[6,8,8,128]{3,2,1,0:T(8,128)} custom-call(f32[3,6,6]{2,1,0:T(8,128)S(1)} %copy-done.3, s32[1,2]{1,0:T(1,128)S(1)} %copy-done.5, s32[1,2]{1,0:T(1,128)S(1)} %copy-done.6, f32[6,8,8,128]{3,2,1,0:T(8,128)S(1)} %get-tuple-element.29.t2_ref, f32[6,8,8,128]{3,2,1,0:T(8,128)S(1)} %get-tuple-element.33.h2_ref, f32[6,8,8,128]{3,2,1,0:T(8,128)S(1)} %copy-done.4, ...), custom_call_target="tpu_custom_call" | custom-call | tf_op jit(solution)/shard_map/pallas_call | solution.py:329
Async XLA Ops:
  0.6 0.9 %copy-start = (f32[6,8,8,128]{3,2,1,0:T(8,128)S(1)}, f32[6,8,8,128]{3,2,1,0:T(8,128)}, u32[]{:S(2)}) copy-start(f32[6,8,8,128]{3,2,1,0:T(8,128)} %q_ref.5) | copy-start | bytes 589828
  1.6 0.8 %copy-start.1 = (f32[8,8,128]{2,1,0:T(8,128)S(1)}, f32[8,8,128]{2,1,0:T(8,128)}, u32[]{:S(2)}) copy-start(f32[8,8,128]{2,1,0:T(8,128)} %dt_ref.9) | copy-start | bytes 98308
  2.3 20.4 %copy-start.3 = (f32[3,6,6]{2,1,0:T(8,128)S(1)}, f32[3,6,6]{2,1,0:T(8,128)}, u32[]{:S(2)}) copy-start(f32[3,6,6]{2,1,0:T(8,128)} %a_ref.7) | copy-start | bytes 1300
  2.5 20.2 %collective-permute-start = (f32[6,2,8,128]{3,2,1,0:T(8,128)S(1)}, f32[6,2,8,128]{3,2,1,0:T(8,128)S(1)}, u32[]{:S(2)}, u32[]{:S(2)}) collective-permute-start(f32[6,2,8,128]{3,2,1,0:T(8,128)S(1)} %get-tuple-element.20), channel_id=1, source_target_pairs={{0,12},{12,0},{24,36},{36,24},{48,60},{60,48},{72,84},{84,72},{96,... | collective-permute-start | bytes 147464 | tf_op jit(solution)/shard_map/ppermute | solution.py:350
  4.4 18.3 %collective-permute-start.1 = (f32[6,2,8,128]{3,2,1,0:T(8,128)S(1)}, f32[6,2,8,128]{3,2,1,0:T(8,128)S(1)}, u32[]{:S(2)}, u32[]{:S(2)}) collective-permute-start(f32[6,2,8,128]{3,2,1,0:T(8,128)S(1)} %get-tuple-element.21), channel_id=1, source_target_pairs={{0,756},{12,24},{24,12},{36,48},{48,36},{60,72},{72,60},{84,96},{9... | collective-permute-start | bytes 147464 | tf_op jit(solution)/shard_map/ppermute | solution.py:350
  12.1 10.6 %copy-start.5 = (s32[1,2]{1,0:T(1,128)S(1)}, s32[1,2]{1,0:T(1,128)}, u32[]{:S(2)}) copy-start(s32[1,2]{1,0:T(1,128)} %type_ref.7) | copy-start | bytes 28
  12.1 10.6 %copy-start.6 = (s32[1,2]{1,0:T(1,128)S(1)}, s32[1,2]{1,0:T(1,128)}, u32[]{:S(2)}) copy-start(s32[1,2]{1,0:T(1,128)} %rot_ref.7) | copy-start | bytes 28
  12.1 5.9 %collective-permute-start.2 = (f32[5,8,128]{2,1,0:T(8,128)S(1)}, f32[5,8,128]{2,1,0:T(8,128)S(1)}, u32[]{:S(2)}, u32[]{:S(2)}) collective-permute-start(f32[5,8,128]{2,1,0:T(8,128)S(1)} %get-tuple-element.22), channel_id=1, source_target_pairs={{1,0},{2,1},{3,2},{4,3},{5,4},{6,5},{7,6},{8,7},{9,8},{10,9},{11,1... | collective-permute-start | bytes 61448 | tf_op jit(solution)/shard_map/ppermute | solution.py:351
  15.8 6.9 %collective-permute-start.3 = (f32[5,8,128]{2,1,0:T(8,128)S(1)}, f32[5,8,128]{2,1,0:T(8,128)S(1)}, u32[]{:S(2)}, u32[]{:S(2)}) collective-permute-start(f32[5,8,128]{2,1,0:T(8,128)S(1)} %get-tuple-element.23), channel_id=1, source_target_pairs={{0,1},{1,2},{2,3},{3,4},{4,5},{5,6},{6,7},{7,8},{8,9},{9,10},{10,1... | collective-permute-start | bytes 61448 | tf_op jit(solution)/shard_map/ppermute | solution.py:351
  24.3 5.3 %collective-permute-start.4 = (f32[6,4,8,128]{3,2,1,0:T(8,128)S(1)}, f32[6,4,8,128]{3,2,1,0:T(8,128)S(1)}, u32[]{:S(2)}, u32[]{:S(2)}) collective-permute-start(f32[6,4,8,128]{3,2,1,0:T(8,128)S(1)} %get-tuple-element.27), channel_id=1, source_target_pairs={{0,12},{12,0},{24,36},{36,24},{48,60},{60,48},{72,84},{84,72},{96,... | collective-permute-start | bytes 294920 | tf_op jit(solution)/shard_map/ppermute | solution.py:359
  26.3 9.3 %collective-permute-start.5 = (f32[6,4,8,128]{3,2,1,0:T(8,128)S(1)}, f32[6,4,8,128]{3,2,1,0:T(8,128)S(1)}, u32[]{:S(2)}, u32[]{:S(2)}) collective-permute-start(f32[6,4,8,128]{3,2,1,0:T(8,128)S(1)} %get-tuple-element.28), channel_id=1, source_target_pairs={{0,756},{12,24},{24,12},{36,48},{48,36},{60,72},{72,60},{84,96},{9... | collective-permute-start | bytes 294920 | tf_op jit(solution)/shard_map/ppermute | solution.py:359
  35.5 13.5 %copy-start.2 = (f32[8,8,128]{2,1,0:T(8,128)S(1)}, f32[8,8,128]{2,1,0:T(8,128)}, u32[]{:S(2)}) copy-start(f32[8,8,128]{2,1,0:T(8,128)} %dt_ref.9) | copy-start | bytes 98308
  37.9 5.3 %collective-permute-start.6 = (f32[6,4,8,128]{3,2,1,0:T(8,128)S(1)}, f32[6,4,8,128]{3,2,1,0:T(8,128)S(1)}, u32[]{:S(2)}, u32[]{:S(2)}) collective-permute-start(f32[6,4,8,128]{3,2,1,0:T(8,128)S(1)} %get-tuple-element.31), channel_id=1, source_target_pairs={{0,12},{12,0},{24,36},{36,24},{48,60},{60,48},{72,84},{84,72},{96,... | collective-permute-start | bytes 294920 | tf_op jit(solution)/shard_map/ppermute | solution.py:367
  39.8 9.3 %collective-permute-start.7 = (f32[6,4,8,128]{3,2,1,0:T(8,128)S(1)}, f32[6,4,8,128]{3,2,1,0:T(8,128)S(1)}, u32[]{:S(2)}, u32[]{:S(2)}) collective-permute-start(f32[6,4,8,128]{3,2,1,0:T(8,128)S(1)} %get-tuple-element.32), channel_id=1, source_target_pairs={{0,756},{12,24},{24,12},{36,48},{48,36},{60,72},{72,60},{84,96},{9... | collective-permute-start | bytes 294920 | tf_op jit(solution)/shard_map/ppermute | solution.py:367
  52.1 5.3 %collective-permute-start.8 = (f32[6,6,8,128]{3,2,1,0:T(8,128)S(1)}, f32[6,6,8,128]{3,2,1,0:T(8,128)S(1)}, u32[]{:S(2)}, u32[]{:S(2)}) collective-permute-start(f32[6,6,8,128]{3,2,1,0:T(8,128)S(1)} %get-tuple-element.36), channel_id=1, source_target_pairs={{0,12},{12,0},{24,36},{36,24},{48,60},{60,48},{72,84},{84,72},{96,... | collective-permute-start | bytes 442376 | tf_op jit(solution)/shard_map/ppermute | solution.py:375
  54.0 9.8 %collective-permute-start.9 = (f32[6,6,8,128]{3,2,1,0:T(8,128)S(1)}, f32[6,6,8,128]{3,2,1,0:T(8,128)S(1)}, u32[]{:S(2)}, u32[]{:S(2)}) collective-permute-start(f32[6,6,8,128]{3,2,1,0:T(8,128)S(1)} %get-tuple-element.37), channel_id=1, source_target_pairs={{0,756},{12,24},{24,12},{36,48},{48,36},{60,72},{72,60},{84,96},{9... | collective-permute-start | bytes 442376 | tf_op jit(solution)/shard_map/ppermute | solution.py:375
  63.8 0.9 %copy-start.4 = (f32[6,8,8,128]{3,2,1,0:T(8,128)S(1)}, f32[6,8,8,128]{3,2,1,0:T(8,128)}, u32[]{:S(2)}) copy-start(f32[6,8,8,128]{3,2,1,0:T(8,128)} %get-tuple-element.19.res_ref) | copy-start | bytes 589828

commit v2 on v1

v2 whole, which is shorter than its diff:
```python
import jax
import jax.numpy as jnp
from jax import lax
from jax.experimental import pallas as pl
from jax.experimental.pallas import tpu as pltpu
from jax.sharding import PartitionSpec as P


NV = 6
NI = 8
HALO = 10
SEG = 32
VMEM_LIMIT = 12 * 1024 * 1024

C0, C1, C2 = 0.44, -0.26, 0.04


def iota_j():
    return lax.broadcasted_iota(jnp.int32, (8, 128), 0)


def iota_k():
    return lax.broadcasted_iota(jnp.int32, (8, 128), 1)


def rotl(x, shift):
    return pltpu.roll(x, shift % 128, 1)


def rots(x, shift):
    return pltpu.roll(x, shift % 8, 0)


def reverse_j(x):
    j = iota_j()
    x = rots(x, 4)
    x = jnp.where((j // 2) % 2 == 0, rots(x, -2), rots(x, 2))
    return jnp.where(j % 2 == 0, rots(x, -1), rots(x, 1))


def ghost_rows(own2, prev2, next2, kind, rot):
    nearest = []
    for r in range(2):
        picked = []
        for v in range(NV):
            wall = -own2[r][v] if v == 1 else own2[r][v]
            x = jnp.where(kind == 2, wall, 0.0)
            x = jnp.where(kind == 1, next2[r][v], x)
            x = jnp.where(kind == 0, prev2[r][v], x)
            picked.append(jnp.where(rot % 2 == 1, reverse_j(x), x))
        turn = rot // 2 % 2 == 1
        a, b = picked[2], picked[3]
        picked[2], picked[3] = jnp.where(turn, -b, a), jnp.where(turn, a, b)
        nearest.append(picked)
    return nearest


def with_ghosts(rows, below, above, meta):
    t_lo, t_hi, r_lo, r_hi = meta
    lo = ghost_rows([rows[0], rows[1]], [below[1], below[0]], [above[0], above[1]], t_lo, r_lo)
    hi = ghost_rows([rows[-1], rows[-2]], [above[0], above[1]], [below[1], below[0]], t_hi, r_hi)
    return [lo[1], lo[0]] + rows + [hi[0], hi[1]]


def flux(q, a, d):
    half = 0.5 * q[1 + d]
    out = []
    for u in range(NV):
        acc = (a[d][u][u] + half) * q[u]
        for v in range(NV):
            if v != u:
                acc = acc + a[d][u][v] * q[v]
        out.append(acc)
    return out


def flux_j(q, a):
    out, mirrored = [], []
    for u in range(NV):
        even = None
        for v in range(NV):
            if v != 2:
                term = a[1][u][v] * q[v]
                even = term if even is None else even + term
        if u == 2:
            even = even + 0.5 * (q[2] * q[2])
            odd = a[1][2][2] * q[2]
        else:
            odd = q[2] * (a[1][u][2] + 0.5 * q[u])
        out.append(even + odd)
        mirrored.append(even - odd)
    return out, mirrored


def j_weights(unit):
    j = iota_j() // unit
    n = 8 // unit
    out = []
    for sign in (1.0, -1.0):
        end = (j == 0) | (j == n - 1)
        centre = jnp.where(end, C0 + sign * C1, C0) + 2 * C0
        near = C1 + sign * C2
        below = jnp.where(j == 0, 0.0, jnp.where((j == 1) | (j == n - 1), near, C1))
        above = jnp.where(j == n - 1, 0.0, jnp.where((j == 0) | (j == n - 2), near, C1))
        if n == 4:
            two = None
        else:
            two = (jnp.where(j >= 2, C2, 0.0), jnp.where(j <= n - 3, C2, 0.0))
        out.append((centre, below, above, two))
    return out


def seg():
    return iota_k() // SEG


def place():
    return iota_k() % SEG


def second_index(fj, gj, q, u, unit, weights, ends):
    centre, below, above, two = weights[1 if u == 2 else 0]
    x = q[u]
    acc = centre * x + below * rots(x, unit) + above * rots(x, -unit)
    if two is None:
        acc = acc + C2 * rots(x, 4)
    else:
        acc = acc + two[0] * rots(x, 2) + two[1] * rots(x, -2)
    up = jnp.where(ends[1], gj[u], rots(fj[u], -unit))
    down = jnp.where(ends[0], gj[u], rots(fj[u], unit))
    return acc + (up - down)


def residual2(padded, halo, a, unit):
    n = len(padded) - 4
    k, j = iota_k(), iota_j()
    weights = j_weights(unit)
    ends = (j < unit, j >= 8 - unit)
    low1, low2 = k < unit, k < 2 * unit
    high1, high2 = k >= 128 - unit, k >= 128 - 2 * unit
    upper = place() >= HALO
    edge = []
    for tile in halo:
        f = flux(tile, a, 2)
        edge.append([jnp.where(upper, f[u] + C1 * tile[u], f[u] - C1 * tile[u]) for u in range(NV)])
    fi = {m: flux(padded[m], a, 0) for m in range(1, n + 3)}
    result = []
    for i in range(n):
        m = i + 2
        q = padded[m]
        fj, gj = flux_j(q, a)
        fk = flux(q, a, 2)
        g, first = unit * i // 4, unit * i % 4 * SEG + HALO
        row = []
        for u in range(NV):
            x = q[u]
            s, e = rotl(halo[g][u], -first), rotl(edge[g][u], -first)
            acc = second_index(fj, gj, q, u, unit, weights, ends)
            acc = acc + (fi[m + 1][u] - fi[m - 1][u])
            acc = acc + C1 * (padded[m + 1][u] + padded[m - 1][u]) + C2 * (padded[m + 2][u] + padded[m - 2][u])
            t = C1 * x
            acc = acc + rotl(jnp.where(low1, e, fk[u] + t), -unit)
            acc = acc - rotl(jnp.where(high1, e, fk[u] - t), unit)
            acc = acc + C2 * (rotl(jnp.where(low2, s, x), -2 * unit) + rotl(jnp.where(high2, s, x), 2 * unit))
            row.append(acc)
        result.append(row)
    return result


def halo_residual2(halo, ghost, own, a):
    r, o = seg(), place()
    j = iota_j()
    weights = j_weights(1)
    ends = (j < 1, j >= 7)
    first, last, low, high = r == 0, r == 3, r < 2, r >= 2
    tiles = [halo[0], halo[1], ghost]
    up_i, down_i = [], []
    for t in tiles:
        f = flux(t, a, 0)
        up_i.append([f[u] + C1 * t[u] for u in range(NV)])
        down_i.append([f[u] - C1 * t[u] for u in range(NV)])
    upper = o >= HALO
    after1, after2 = o == HALO, (o == HALO) | (o == HALO + 1)
    before1, before2 = o == HALO - 1, (o == HALO - 1) | (o == HALO - 2)
    result = []
    for g in range(2):
        q, nxt, prv = tiles[g], (g + 1) % 3, (g + 2) % 3
        fj, gj = flux_j(q, a)
        fk = flux(q, a, 2)
        fo = flux(own[g], a, 2)
        row = []
        for u in range(NV):
            x, y = q[u], own[g][u]
            acc = second_index(fj, gj, q, u, 1, weights, ends)
            acc = acc + rotl(jnp.where(first, up_i[nxt][u], up_i[g][u]), -SEG)
            acc = acc - rotl(jnp.where(last, down_i[prv][u], down_i[g][u]), SEG)
            acc = acc + C2 * rotl(jnp.where(low, tiles[nxt][u], x) + jnp.where(high, tiles[prv][u], x), 2 * SEG)
            t = C1 * x
            e = jnp.where(upper, fo[u] + C1 * y, fo[u] - C1 * y)
            acc = acc + rotl(jnp.where(after1, e, fk[u] + t), -1)
            acc = acc - rotl(jnp.where(before1, e, fk[u] - t), 1)
            acc = acc + C2 * (rotl(jnp.where(after2, y, x), -2) + rotl(jnp.where(before2, y, x), 2))
            row.append(acc)
        result.append(row)
    return result


def pack_ends(rows):
    r = seg()
    out = []
    for g in range(2):
        tile = []
        for v in range(NV):
            acc = rotl(rows[4 * g][v], HALO)
            for p in range(1, 4):
                acc = jnp.where(r == p, rotl(rows[4 * g + p][v], HALO + p * SEG), acc)
            tile.append(acc)
        out.append(tile)
    return out


def halo_ghost(halo, below, above, meta):
    t_lo, t_hi, r_lo, r_hi = meta
    r = seg()
    high_side = r < 2
    even_part = r % 2 == 0

    def turned(x):
        return jnp.where(even_part, rotl(x, SEG), rotl(x, -SEG))

    picked = []
    for v in range(NV):
        wall_lo, wall_hi = turned(halo[0][v]), turned(halo[1][v])
        if v == 1:
            wall_lo, wall_hi = -wall_lo, -wall_hi
        hi = jnp.where(t_hi == 2, wall_hi, 0.0)
        hi = jnp.where(t_hi == 1, turned(below[v]), hi)
        hi = jnp.where(t_hi == 0, above[v], hi)
        lo = jnp.where(t_lo == 2, wall_lo, 0.0)
        lo = jnp.where(t_lo == 1, turned(above[v]), lo)
        lo = jnp.where(t_lo == 0, below[v], lo)
        x = jnp.where(high_side, hi, lo)
        code = jnp.where(high_side, r_hi, r_lo)
        picked.append(jnp.where(code % 2 == 1, reverse_j(x), x))
    turn = jnp.where(high_side, r_hi, r_lo) // 2 % 2 == 1
    b, c = picked[2], picked[3]
    picked[2], picked[3] = jnp.where(turn, -c, b), jnp.where(turn, b, c)
    return picked


def cell_mean(x):
    x = x + jnp.where(iota_j() % 2 == 0, rots(x, -1), rots(x, 1))
    x = x + jnp.where(iota_k() % 2 == 0, rotl(x, -1), rotl(x, 1))
    return 0.125 * x


def restrict_rows(rows):
    return [[cell_mean(rows[2 * c][v] + rows[2 * c + 1][v]) for v in range(len(rows[0]))] for c in range(len(rows) // 2)]


def halo_mean(x):
    return cell_mean(x + jnp.where(seg() % 2 == 0, rotl(x, -SEG), rotl(x, SEG)))


def load(ref, first, count):
    return [[ref[v, first + r] for v in range(NV)] for r in range(count)]


def store(ref, first, rows):
    for r, row in enumerate(rows):
        for v in range(NV):
            ref[v, first + r] = row[v]


def load_tiles(ref):
    return [[ref[g, v] for v in range(NV)] for g in range(2)]


def store_tiles(ref, tiles):
    for g in range(2):
        for v in range(NV):
            ref[g, v] = tiles[g][v]


def coefficients(a_ref):
    return [[[a_ref[d, u, v] for v in range(NV)] for u in range(NV)] for d in range(3)]


def meta_of(type_ref, rot_ref):
    return (type_ref[0, 0], type_ref[0, 1], rot_ref[0, 0], rot_ref[0, 1])


def masked(tiles):
    o = place()
    s = lax.axis_index("sub")
    final = lax.axis_size("sub") - 1
    inside = ((o < HALO) & (s != 0)) | ((o >= HALO) & (o < 2 * HALO) & (s != final))
    return [[jnp.where(inside, x, 0.0) for x in tile] for tile in tiles]


def is_even():
    return lax.axis_index("blk") % 2 == 0


def send(ma, mb, at, first, last):
    even = is_even()
    for n, (lo, hi) in enumerate(zip(first, last)):
        ma[at + n] = jnp.where(even, hi, lo)
        mb[at + n] = jnp.where(even, lo, hi)


def receive(ga, gb, at, count):
    even = is_even()
    below, above = [], []
    for n in range(at, at + count):
        a, b = ga[n], gb[n]
        below.append(jnp.where(even, b, a))
        above.append(jnp.where(even, a, b))
    return below, above


def send_rows(ma, mb, at, rows):
    send(ma, mb, at, rows[0] + rows[1], rows[-2] + rows[-1])


def receive_rows(ga, gb, at):
    below, above = receive(ga, gb, at, 2 * NV)
    return [below[:NV], below[NV:]], [above[:NV], above[NV:]]


def send_halo(ma, mb, at, halo):
    low = seg() < 2
    first = [jnp.where(low, halo[0][p], rotl(halo[0][p + 1], 64)) for p in range(0, NV, 2)]
    last = [jnp.where(low, rotl(halo[1][p + 1], 64), halo[1][p]) for p in range(0, NV, 2)]
    send(ma, mb, at, first, last)


def receive_halo(ga, gb, at):
    below, above = receive(ga, gb, at, NV // 2)

    def spread(tiles):
        return [y for x in tiles for y in (x, rotl(x, 64))]

    return spread(below), spread(above)


def send_coarse(ma, mb, at, first, second):
    j_even, k_even = iota_j() % 2 == 0, iota_k() % 2 == 0

    def joined(r0, r1):
        out = []
        for v in range(NV):
            x, y = (jnp.where(j_even, first[r][v], second[r][v]) for r in (r0, r1))
            out.append(jnp.where(k_even, x, y))
        return out

    send(ma, mb, at, joined(0, 1), joined(-2, -1))


def receive_coarse(ga, gb, at):
    j_even, k_even = iota_j() % 2 == 0, iota_k() % 2 == 0
    fields = ([], [])
    for tiles in receive(ga, gb, at, NV):
        rows = ([], [])
        for x in tiles:
            rows[0].append(jnp.where(k_even, x, rotl(x, 1)))
            rows[1].append(jnp.where(k_even, rotl(x, -1), x))
        fields[0].append([[jnp.where(j_even, x, rots(x, 1)) for x in row] for row in rows])
        fields[1].append([[jnp.where(j_even, rots(x, -1), x) for x in row] for row in rows])
    return fields


def pack_kernel(q_hbm, dt_hbm, ends_ref, ma, mb, to_left, to_right, q_ref, dt_ref, sems):
    copies = (
        pltpu.make_async_copy(q_hbm, q_ref, sems.at[0]),
        pltpu.make_async_copy(dt_hbm, dt_ref, sems.at[1]),
    )
    for copy in copies:
        copy.start()
    for copy in copies:
        copy.wait()
    rows = load(q_ref, 0, NI)
    send_rows(ma, mb, 0, rows)
    ends = pack_ends(rows)
    store_tiles(ends_ref, ends)
    r, lower = seg(), place() < HALO
    tiles = ends[0] + ends[1]
    for g in range(2):
        acc = rotl(dt_ref[4 * g], HALO)
        for p in range(1, 4):
            acc = jnp.where(r == p, rotl(dt_ref[4 * g + p], HALO + p * SEG), acc)
        tiles.append(acc)
    for n in range(NV + 1):
        x, y = tiles[2 * n], tiles[2 * n + 1]
        to_right[n] = jnp.where(lower, x, rotl(y, HALO))
        to_left[n] = jnp.where(lower, rotl(y, -HALO), x)


def unpack(from_right, from_left):
    lower = place() < HALO
    tiles = []
    for n in range(NV + 1):
        x, y = from_left[n], from_right[n]
        tiles.append(jnp.where(lower, x, y))
        tiles.append(jnp.where(lower, rotl(x, -HALO), rotl(y, HALO)))
    halo = masked([tiles[:NV], tiles[NV : 2 * NV]])
    return halo, tiles[2 * NV :]


def advance(start, dt, twice, factor):
    return [[start[i][v] - (0.5 * factor * dt[i]) * twice[i][v] for v in range(NV)] for i in range(len(start))]


def first_kernel(a_ref, type_ref, rot_ref, q_ref, dt_ref, ga, gb, from_right, from_left, t1_ref, h0_ref, dth_ref, ma, mb):
    a, meta = coefficients(a_ref), meta_of(type_ref, rot_ref)
    h0, dth = unpack(from_right, from_left)
    store_tiles(h0_ref, h0)
    for g in range(2):
        dth_ref[g] = dth[g]
    send_halo(ma, mb, 2 * NV, h0)
    t0 = load(q_ref, 0, NI)
    below, above = receive_rows(ga, gb, 0)
    twice = residual2(with_ghosts(t0, below, above, meta), h0, a, 1)
    t1 = advance(t0, [dt_ref[i] for i in range(NI)], twice, 0.4)
    store(t1_ref, 0, t1)
    send_rows(ma, mb, 0, t1)


def second_kernel(
    a_ref, type_ref, rot_ref, q_ref, t1_ref, h0_ref, ends_ref, dt_ref, dth_ref, ga, gb, t2_ref, h1_ref, ma, mb
):
    a, meta = coefficients(a_ref), meta_of(type_ref, rot_ref)
    h0 = load_tiles(h0_ref)
    below, above = receive_halo(ga, gb, 2 * NV)
    twice = halo_residual2(h0, halo_ghost(h0, below, above, meta), load_tiles(ends_ref), a)
    h1 = masked(advance(h0, [dth_ref[g] for g in range(2)], twice, 0.4))
    store_tiles(h1_ref, h1)
    send_halo(ma, mb, 2 * NV, h1)
    t0, t1 = load(q_ref, 0, NI), load(t1_ref, 0, NI)
    below, above = receive_rows(ga, gb, 0)
    twice = residual2(with_ghosts(t1, below, above, meta), h1, a, 1)
    t2 = advance(t0, [dt_ref[i] for i in range(NI)], twice, 1.0)
    store(t2_ref, 0, t2)
    send_rows(ma, mb, 0, t2)


def third_kernel(
    a_ref, type_ref, rot_ref, t1_ref, t2_ref, h0_ref, h1_ref, dt_ref, dth_ref, ga, gb, res_ref, h2_ref, c1_ref, mean_ref, ma, mb
):
    a, meta = coefficients(a_ref), meta_of(type_ref, rot_ref)
    h0, h1 = load_tiles(h0_ref), load_tiles(h1_ref)
    below, above = receive_halo(ga, gb, 2 * NV)
    twice = halo_residual2(h1, halo_ghost(h1, below, above, meta), pack_ends(load(t1_ref, 0, NI)), a)
    h2 = masked(advance(h0, [dth_ref[g] for g in range(2)], twice, 1.0))
    store_tiles(h2_ref, h2)
    send_halo(ma, mb, NV, h2)
    t2 = load(t2_ref, 0, NI)
    below, above = receive_rows(ga, gb, 0)
    twice = residual2(with_ghosts(t2, below, above, meta), h2, a, 1)
    res = [[0.5 * x for x in row] for row in twice]
    store(res_ref, 0, res)
    start, mean = restrict_rows(t2), restrict_rows(res)
    store(mean_ref, 0, mean)
    c1 = []
    for c in range(NI // 2):
        step = cell_mean(dt_ref[2 * c] + dt_ref[2 * c + 1])
        c1.append([start[c][v] - (0.4 * step) * mean[c][v] for v in range(NV)])
    store(c1_ref, 0, c1)
    send_coarse(ma, mb, 0, c1, start)


def fourth_kernel(a_ref, type_ref, rot_ref, t2_ref, h2_ref, c1_ref, mean_ref, dt_ref, dth_ref, ga, gb, out_ref):
    a, meta = coefficients(a_ref), meta_of(type_ref, rot_ref)
    half = NI // 2
    h2, t2 = load_tiles(h2_ref), load(t2_ref, 0, NI)
    below, above = receive_halo(ga, gb, NV)
    twice = halo_residual2(h2, halo_ghost(h2, below, above, meta), pack_ends(t2), a)
    start_h = [[halo_mean(x) for x in tile] for tile in h2]
    c1_h = []
    for g in range(2):
        step = halo_mean(dth_ref[g])
        c1_h.append([start_h[g][v] - (0.2 * step) * halo_mean(twice[g][v]) for v in range(NV)])
    c1_h = masked(c1_h)
    start, c1 = restrict_rows(t2), load(c1_ref, 0, half)
    (below1, above1), (below0, above0) = receive_coarse(ga, gb, 0)
    twice0 = residual2(with_ghosts(start, below0, above0, meta), start_h, a, 2)
    twice1 = residual2(with_ghosts(c1, below1, above1, meta), c1_h, a, 2)
    for c in range(half):
        step = cell_mean(dt_ref[2 * c] + dt_ref[2 * c + 1])
        for v in range(NV):
            change = -step * (0.5 * (twice1[c][v] - twice0[c][v]) + mean_ref[v, c])
            out_ref[v, 2 * c] = t2[2 * c][v] + change
            out_ref[v, 2 * c + 1] = t2[2 * c + 1][v] + change


def field(rows):
    return (NV, rows, 8, 128)


def tiles_of(*count):
    return (*count, 8, 128)


def call(kernel, scalars, arrays, outs, in_hbm=False, scratch=()):
    smem, vmem = pl.BlockSpec(memory_space=pltpu.SMEM), pl.BlockSpec(memory_space=pltpu.VMEM)
    given = pl.BlockSpec(memory_space=pltpu.HBM) if in_hbm else vmem
    return pl.pallas_call(
        kernel,
        out_shape=[jax.ShapeDtypeStruct(shape, jnp.float32) for shape in outs],
        in_specs=[smem] * len(scalars) + [given] * len(arrays),
        out_specs=[vmem] * len(outs),
        scratch_shapes=scratch,
        compiler_params=pltpu.CompilerParams(vmem_limit_bytes=VMEM_LIMIT),
    )(*scalars, *arrays)


def cycle(flow_state, timestep, coupling, face_type, face_rot):
    blocks, parts = lax.axis_size("blk"), lax.axis_size("sub")
    chip = [(b, b ^ 1) for b in range(blocks)]
    link = [(b, (b + 1) % blocks if b % 2 else (b - 1) % blocks) for b in range(blocks)]
    ahead = [(s, s + 1) for s in range(parts - 1)]
    back = [(s + 1, s) for s in range(parts - 1)]
    scalars = (coupling, face_type, face_rot)
    pair = tiles_of(2, NV)

    def exchange(ma, mb):
        gb = lax.ppermute(mb, "blk", link)
        ga = lax.ppermute(ma, "blk", chip)
        return ga, gb

    ends, ma, mb, to_left, to_right = call(
        pack_kernel,
        (),
        (flow_state, timestep),
        (pair, tiles_of(2 * NV), tiles_of(2 * NV), tiles_of(NV + 1), tiles_of(NV + 1)),
        in_hbm=True,
        scratch=(
            pltpu.VMEM(field(NI), jnp.float32),
            pltpu.VMEM(tiles_of(NI), jnp.float32),
            pltpu.SemaphoreType.DMA((2,)),
        ),
    )
    ga, gb = exchange(ma, mb)
    from_right = lax.ppermute(to_left, "sub", back)
    from_left = lax.ppermute(to_right, "sub", ahead)

    message = tiles_of(2 * NV + NV // 2)
    t1, h0, dth, ma, mb = call(
        first_kernel,
        scalars,
        (flow_state, timestep, ga, gb, from_right, from_left),
        (field(NI), pair, tiles_of(2), message, message),
    )
    ga, gb = exchange(ma, mb)

    t2, h1, ma, mb = call(
        second_kernel,
        scalars,
        (flow_state, t1, h0, ends, timestep, dth, ga, gb),
        (field(NI), pair, message, message),
    )
    ga, gb = exchange(ma, mb)

    message = tiles_of(NV + NV // 2)
    res, h2, c1, mean, ma, mb = call(
        third_kernel,
        scalars,
        (t1, t2, h0, h1, timestep, dth, ga, gb),
        (field(NI), pair, field(NI // 2), field(NI // 2), message, message),
    )
    ga, gb = exchange(ma, mb)

    (updated,) = call(
        fourth_kernel, scalars, (t2, h2, c1, mean, timestep, dth, ga, gb), (field(NI),)
    )
    return (updated, res)


def solution(mesh):
    return jax.shard_map(
        cycle,
        mesh=mesh,
        in_specs=(
            P(None, "blk", None, "sub"),
            P("blk", None, "sub"),
            P(),
            P("blk", None),
            P("blk", None),
        ),
        out_specs=(P(None, "blk", None, "sub"), P(None, "blk", None, "sub")),
        check_vma=False,
    )
```

time: 68.5 us -> 69.4 us (1.013)
  Pallas kernels: 10.4 us -> 14.2 us
  waiting for transfers between devices: 22.9 us -> 21 us
  local copies, waits for them, and re-layouts: 2.62 us -> 1.7 us
    pallas_call x5, Pallas kernels: 10.4 us -> 14.2 us  [call(): pl.pallas_call(kernel, out_shape=[jax.ShapeDtypeStruct(shape, jnp.float32...]
    ppermute x10, waiting for transfers between devices: 22.9 us -> 21 us  [the longest x4 16.2 us: exchange(): gb = lax.ppermute(mb, 'blk', link)]
    unnamed x14 -> x12, local copies, waits for them, and re-layouts: 2.62 us -> 1.7 us
where the time goes in v2:
time: 69.4 us; the launch traced here: 68.9 us
  starting transfers between devices  31.3 us (45%)
  waiting for transfers between devices  21 us (30%)
  Pallas kernels  14.2 us (20%)
  local copies, waits for them, and re-layouts  1.7 us (2%)
  between operations  0.81 us (1%)
    ppermute x4, starting transfers between devices, exchange(): gb = lax.ppermute(mb, 'blk', link)  17.8 us
    ppermute x4, waiting for transfers between devices, exchange(): gb = lax.ppermute(mb, 'blk', link)  16.2 us
    pallas_call x5, Pallas kernels, call(): pl.pallas_call(kernel, out_shape=[jax.ShapeDtypeStruct(shape, jnp.float32...  14.2 us
    ppermute x4, starting transfers between devices, exchange(): ga = lax.ppermute(ma, 'blk', chip)  7.67 us
    ppermute x1, waiting for transfers between devices, cycle(): from_left = lax.ppermute(to_right, 'sub', ahead)  4.79 us
    ppermute x1, starting transfers between devices, cycle(): from_right = lax.ppermute(to_left, 'sub', back)  3.67 us
    ppermute x1, starting transfers between devices, cycle(): from_left = lax.ppermute(to_right, 'sub', ahead)  2.17 us
    unnamed x12, local copies, waits for them, and re-layouts  1.7 us
  transfers between devices with their start and end apart: 10, of which 4 were waited for; matrix products, arithmetic and copies ran while one was open for 0% of the time, Pallas kernels for 0%

profile of v2, /device:TPU:512, one launch (start us, length us, event | category | flops | bytes accessed | tf_op | source)
XLA Modules:
  0.0 68.9 jit_solution(18276148415540111257)
XLA Ops:
  0.6 0.0 copy-start
  0.6 0.9 %copy-done = f32[6,8,8,128]{3,2,1,0:T(8,128)S(1)} copy-done((f32[6,8,8,128]{3,2,1,0:T(8,128)S(1)}, f32[6,8,8,128]{3,2,1,0:T(8,128)}, u32[]{:S(2)}) %copy-start) | copy-done | bytes 196632
  1.6 0.0 copy-start.1
  1.6 0.8 %copy-done.1 = f32[8,8,128]{2,1,0:T(8,128)S(1)} copy-done((f32[8,8,128]{2,1,0:T(8,128)S(1)}, f32[8,8,128]{2,1,0:T(8,128)}, u32[]{:S(2)}) %copy-start.1) | copy-done | bytes 32792
  2.3 0.0 copy-start.3
  2.3 0.5 shard_map.68
  2.8 1.9 %collective-permute-start = (f32[12,8,128]{2,1,0:T(8,128)S(1)}, f32[12,8,128]{2,1,0:T(8,128)S(1)}, u32[]{:S(2)}, u32[]{:S(2)}) collective-permute-start(f32[12,8,128]{2,1,0:T(8,128)S(1)} %get-tuple-element.22), channel_id=1, source_target_pairs={{0,12},{12,0},{24,36},{36,24},{48,60},{60,48},{72,84},{84,72},{96,... | collective-permute-start | bytes 147464 | tf_op jit(solution)/shard_map/ppermute | solution.py:528
  4.7 7.7 %collective-permute-start.1 = (f32[12,8,128]{2,1,0:T(8,128)S(1)}, f32[12,8,128]{2,1,0:T(8,128)S(1)}, u32[]{:S(2)}, u32[]{:S(2)}) collective-permute-start(f32[12,8,128]{2,1,0:T(8,128)S(1)} %get-tuple-element.23), channel_id=1, source_target_pairs={{0,756},{12,24},{24,12},{36,48},{48,36},{60,72},{72,60},{84,96},{9... | collective-permute-start | bytes 147464 | tf_op jit(solution)/shard_map/ppermute | solution.py:527
  12.4 0.0 copy-start.4
  12.4 0.0 copy-start.5
  12.4 3.7 %collective-permute-start.2 = (f32[7,8,128]{2,1,0:T(8,128)S(1)}, f32[7,8,128]{2,1,0:T(8,128)S(1)}, u32[]{:S(2)}, u32[]{:S(2)}) collective-permute-start(f32[7,8,128]{2,1,0:T(8,128)S(1)} %get-tuple-element.24), channel_id=1, source_target_pairs={{1,0},{2,1},{3,2},{4,3},{5,4},{6,5},{7,6},{8,7},{9,8},{10,9},{11,1... | collective-permute-start | bytes 86024 | tf_op jit(solution)/shard_map/ppermute | solution.py:544
  16.1 2.2 %collective-permute-start.3 = (f32[7,8,128]{2,1,0:T(8,128)S(1)}, f32[7,8,128]{2,1,0:T(8,128)S(1)}, u32[]{:S(2)}, u32[]{:S(2)}) collective-permute-start(f32[7,8,128]{2,1,0:T(8,128)S(1)} %get-tuple-element.25), channel_id=1, source_target_pairs={{0,1},{1,2},{2,3},{3,4},{4,5},{5,6},{6,7},{7,8},{8,9},{9,10},{10,1... | collective-permute-start | bytes 86024 | tf_op jit(solution)/shard_map/ppermute | solution.py:545
  18.3 0.0 collective-permute-done.2.from_right
  18.3 4.8 %collective-permute-done.3.from_left = f32[7,8,128]{2,1,0:T(8,128)S(1)} collective-permute-done((f32[7,8,128]{2,1,0:T(8,128)S(1)}, f32[7,8,128]{2,1,0:T(8,128)S(1)}, u32[]{:S(2)}, u32[]{:S(2)}) %collective-permute-start.3) | collective-permute-done | bytes 28704 | tf_op jit(solution)/shard_map/ppermute | solution.py:545
  23.1 0.0 collective-permute-done.ga
  23.1 0.0 collective-permute-done.1.gb
  23.1 0.0 copy-done.3
  23.1 0.0 copy-done.4
  23.1 0.0 copy-done.5
  23.1 2.4 %shard_map.69 = (f32[6,8,8,128]{3,2,1,0:T(8,128)S(1)}, f32[2,6,8,128]{3,2,1,0:T(8,128)S(1)}, f32[2,8,128]{2,1,0:T(8,128)S(1)}, f32[15,8,128]{2,1,0:T(8,128)S(1)}, f32[15,8,128]{2,1,0:T(8,128)S(1)}) custom-call(f32[3,6,6]{2,1,0:T(8,128)S(1)} %copy-done.3, s32[1,2]{1,0:T(1,128)S(1)} %copy-done.4, s32[1,2]{1,0:T(1,128)S(1)} %copy-done.5, ...), custom_call_target="tpu_custom_call" | custom-call | tf_op jit(solution)/shard_map/pallas_call | solution.py:507
  25.5 1.9 %collective-permute-start.4 = (f32[15,8,128]{2,1,0:T(8,128)S(1)}, f32[15,8,128]{2,1,0:T(8,128)S(1)}, u32[]{:S(2)}, u32[]{:S(2)}) collective-permute-start(f32[15,8,128]{2,1,0:T(8,128)S(1)} %get-tuple-element.30), channel_id=1, source_target_pairs={{0,12},{12,0},{24,36},{36,24},{48,60},{60,48},{72,84},{84,72},{96,... | collective-permute-start | bytes 184328 | tf_op jit(solution)/shard_map/ppermute | solution.py:528
  27.5 3.4 %collective-permute-start.5 = (f32[15,8,128]{2,1,0:T(8,128)S(1)}, f32[15,8,128]{2,1,0:T(8,128)S(1)}, u32[]{:S(2)}, u32[]{:S(2)}) collective-permute-start(f32[15,8,128]{2,1,0:T(8,128)S(1)} %get-tuple-element.31), channel_id=1, source_target_pairs={{0,756},{12,24},{24,12},{36,48},{48,36},{60,72},{72,60},{84,96},{9... | collective-permute-start | bytes 184328 | tf_op jit(solution)/shard_map/ppermute | solution.py:527
  30.8 0.0 collective-permute-done.4.ga
  30.9 5.5 %collective-permute-done.5.gb = f32[15,8,128]{2,1,0:T(8,128)S(1)} collective-permute-done((f32[15,8,128]{2,1,0:T(8,128)S(1)}, f32[15,8,128]{2,1,0:T(8,128)S(1)}, u32[]{:S(2)}, u32[]{:S(2)}) %collective-permute-start.5) | collective-permute-done | bytes 61472 | tf_op jit(solution)/shard_map/ppermute | solution.py:527
  36.3 0.0 copy-start.2
  36.3 2.2 %shard_map.70 = (f32[6,8,8,128]{3,2,1,0:T(8,128)S(1)}, f32[2,6,8,128]{3,2,1,0:T(8,128)S(1)}, f32[15,8,128]{2,1,0:T(8,128)S(1)}, f32[15,8,128]{2,1,0:T(8,128)S(1)}) custom-call(f32[3,6,6]{2,1,0:T(8,128)S(1)} %copy-done.3, s32[1,2]{1,0:T(1,128)S(1)} %copy-done.4, s32[1,2]{1,0:T(1,128)S(1)} %copy-done.5, f32[6,8,8,128]{3,2,1,0:T(8,128)S(1)} %copy-done, ...), custom_call_target="tpu_custom_call" | custom-call | tf_op jit(solution)/shard_map/pallas_call | solution.py:507
  38.5 1.9 %collective-permute-start.6 = (f32[15,8,128]{2,1,0:T(8,128)S(1)}, f32[15,8,128]{2,1,0:T(8,128)S(1)}, u32[]{:S(2)}, u32[]{:S(2)}) collective-permute-start(f32[15,8,128]{2,1,0:T(8,128)S(1)} %get-tuple-element.34), channel_id=1, source_target_pairs={{0,12},{12,0},{24,36},{36,24},{48,60},{60,48},{72,84},{84,72},{96,... | collective-permute-start | bytes 184328 | tf_op jit(solution)/shard_map/ppermute | solution.py:528
  40.4 3.4 %collective-permute-start.7 = (f32[15,8,128]{2,1,0:T(8,128)S(1)}, f32[15,8,128]{2,1,0:T(8,128)S(1)}, u32[]{:S(2)}, u32[]{:S(2)}) collective-permute-start(f32[15,8,128]{2,1,0:T(8,128)S(1)} %get-tuple-element.35), channel_id=1, source_target_pairs={{0,756},{12,24},{24,12},{36,48},{48,36},{60,72},{72,60},{84,96},{9... | collective-permute-start | bytes 184328 | tf_op jit(solution)/shard_map/ppermute | solution.py:527
  43.8 0.0 collective-permute-done.6.ga
  43.8 5.5 %collective-permute-done.7.gb = f32[15,8,128]{2,1,0:T(8,128)S(1)} collective-permute-done((f32[15,8,128]{2,1,0:T(8,128)S(1)}, f32[15,8,128]{2,1,0:T(8,128)S(1)}, u32[]{:S(2)}, u32[]{:S(2)}) %collective-permute-start.7) | collective-permute-done | bytes 61472 | tf_op jit(solution)/shard_map/ppermute | solution.py:527
  49.3 0.0 copy-done.2
  49.3 4.1 %shard_map.71 = (f32[6,8,8,128]{3,2,1,0:T(8,128)}, f32[2,6,8,128]{3,2,1,0:T(8,128)S(1)}, f32[6,4,8,128]{3,2,1,0:T(8,128)S(1)}, f32[6,4,8,128]{3,2,1,0:T(8,128)S(...) custom-call(f32[3,6,6]{2,1,0:T(8,128)S(1)} %copy-done.3, s32[1,2]{1,0:T(1,128)S(1)} %copy-done.4, ...), custom_call_target="tpu_custom_call" | custom-call | tf_op jit(solution)/shard_map/pallas_call | solution.py:507
  53.4 1.9 %collective-permute-start.8 = (f32[9,8,128]{2,1,0:T(8,128)S(1)}, f32[9,8,128]{2,1,0:T(8,128)S(1)}, u32[]{:S(2)}, u32[]{:S(2)}) collective-permute-start(f32[9,8,128]{2,1,0:T(8,128)S(1)} %get-tuple-element.39), channel_id=1, source_target_pairs={{0,12},{12,0},{24,36},{36,24},{48,60},{60,48},{72,84},{84,72},{96,... | collective-permute-start | bytes 110600 | tf_op jit(solution)/shard_map/ppermute | solution.py:528
  55.4 3.4 %collective-permute-start.9 = (f32[9,8,128]{2,1,0:T(8,128)S(1)}, f32[9,8,128]{2,1,0:T(8,128)S(1)}, u32[]{:S(2)}, u32[]{:S(2)}) collective-permute-start(f32[9,8,128]{2,1,0:T(8,128)S(1)} %get-tuple-element.40), channel_id=1, source_target_pairs={{0,756},{12,24},{24,12},{36,48},{48,36},{60,72},{72,60},{84,96},{9... | collective-permute-start | bytes 110600 | tf_op jit(solution)/shard_map/ppermute | solution.py:527
  58.7 0.0 collective-permute-done.8.ga
  58.7 5.2 %collective-permute-done.9.gb = f32[9,8,128]{2,1,0:T(8,128)S(1)} collective-permute-done((f32[9,8,128]{2,1,0:T(8,128)S(1)}, f32[9,8,128]{2,1,0:T(8,128)S(1)}, u32[]{:S(2)}, u32[]{:S(2)}) %collective-permute-start.9) | collective-permute-done | bytes 36896 | tf_op jit(solution)/shard_map/ppermute | solution.py:527
  64.0 5.0 %shard_map.72 = f32[6,8,8,128]{3,2,1,0:T(8,128)} custom-call(f32[3,6,6]{2,1,0:T(8,128)S(1)} %copy-done.3, s32[1,2]{1,0:T(1,128)S(1)} %copy-done.4, s32[1,2]{1,0:T(1,128)S(1)} %copy-done.5, f32[6,8,8,128]{3,2,1,0:T(8,128)S(1)} %get-tuple-element.32.t2_ref, f32[2,6,8,128]{3,2,1,0:T(8,128)S(1)} %get-tuple-element.36.h2_ref, ...), custom_call_target="tpu_custom_call" | custom-call | tf_op jit(solution)/shard_map/pallas_call | solution.py:507
Async XLA Ops:
  0.6 0.9 %copy-start = (f32[6,8,8,128]{3,2,1,0:T(8,128)S(1)}, f32[6,8,8,128]{3,2,1,0:T(8,128)}, u32[]{:S(2)}) copy-start(f32[6,8,8,128]{3,2,1,0:T(8,128)} %q_ref.3) | copy-start | bytes 589828
  1.6 0.8 %copy-start.1 = (f32[8,8,128]{2,1,0:T(8,128)S(1)}, f32[8,8,128]{2,1,0:T(8,128)}, u32[]{:S(2)}) copy-start(f32[8,8,128]{2,1,0:T(8,128)} %dt_ref.7) | copy-start | bytes 98308
  2.3 20.8 %copy-start.3 = (f32[3,6,6]{2,1,0:T(8,128)S(1)}, f32[3,6,6]{2,1,0:T(8,128)}, u32[]{:S(2)}) copy-start(f32[3,6,6]{2,1,0:T(8,128)} %a_ref.7) | copy-start | bytes 1300
  2.8 20.3 %collective-permute-start = (f32[12,8,128]{2,1,0:T(8,128)S(1)}, f32[12,8,128]{2,1,0:T(8,128)S(1)}, u32[]{:S(2)}, u32[]{:S(2)}) collective-permute-start(f32[12,8,128]{2,1,0:T(8,128)S(1)} %get-tuple-element.22), channel_id=1, source_target_pairs={{0,12},{12,0},{24,36},{36,24},{48,60},{60,48},{72,84},{84,72},{96,... | collective-permute-start | bytes 147464 | tf_op jit(solution)/shard_map/ppermute | solution.py:528
  4.7 18.4 %collective-permute-start.1 = (f32[12,8,128]{2,1,0:T(8,128)S(1)}, f32[12,8,128]{2,1,0:T(8,128)S(1)}, u32[]{:S(2)}, u32[]{:S(2)}) collective-permute-start(f32[12,8,128]{2,1,0:T(8,128)S(1)} %get-tuple-element.23), channel_id=1, source_target_pairs={{0,756},{12,24},{24,12},{36,48},{48,36},{60,72},{72,60},{84,96},{9... | collective-permute-start | bytes 147464 | tf_op jit(solution)/shard_map/ppermute | solution.py:527
  12.4 10.7 %copy-start.4 = (s32[1,2]{1,0:T(1,128)S(1)}, s32[1,2]{1,0:T(1,128)}, u32[]{:S(2)}) copy-start(s32[1,2]{1,0:T(1,128)} %type_ref.7) | copy-start | bytes 28
  12.4 10.7 %copy-start.5 = (s32[1,2]{1,0:T(1,128)S(1)}, s32[1,2]{1,0:T(1,128)}, u32[]{:S(2)}) copy-start(s32[1,2]{1,0:T(1,128)} %rot_ref.7) | copy-start | bytes 28
  12.4 5.9 %collective-permute-start.2 = (f32[7,8,128]{2,1,0:T(8,128)S(1)}, f32[7,8,128]{2,1,0:T(8,128)S(1)}, u32[]{:S(2)}, u32[]{:S(2)}) collective-permute-start(f32[7,8,128]{2,1,0:T(8,128)S(1)} %get-tuple-element.24), channel_id=1, source_target_pairs={{1,0},{2,1},{3,2},{4,3},{5,4},{6,5},{7,6},{8,7},{9,8},{10,9},{11,1... | collective-permute-start | bytes 86024 | tf_op jit(solution)/shard_map/ppermute | solution.py:544
  16.1 7.0 %collective-permute-start.3 = (f32[7,8,128]{2,1,0:T(8,128)S(1)}, f32[7,8,128]{2,1,0:T(8,128)S(1)}, u32[]{:S(2)}, u32[]{:S(2)}) collective-permute-start(f32[7,8,128]{2,1,0:T(8,128)S(1)} %get-tuple-element.25), channel_id=1, source_target_pairs={{0,1},{1,2},{2,3},{3,4},{4,5},{5,6},{6,7},{7,8},{8,9},{9,10},{10,1... | collective-permute-start | bytes 86024 | tf_op jit(solution)/shard_map/ppermute | solution.py:545
  25.5 5.3 %collective-permute-start.4 = (f32[15,8,128]{2,1,0:T(8,128)S(1)}, f32[15,8,128]{2,1,0:T(8,128)S(1)}, u32[]{:S(2)}, u32[]{:S(2)}) collective-permute-start(f32[15,8,128]{2,1,0:T(8,128)S(1)} %get-tuple-element.30), channel_id=1, source_target_pairs={{0,12},{12,0},{24,36},{36,24},{48,60},{60,48},{72,84},{84,72},{96,... | collective-permute-start | bytes 184328 | tf_op jit(solution)/shard_map/ppermute | solution.py:528
  27.5 8.9 %collective-permute-start.5 = (f32[15,8,128]{2,1,0:T(8,128)S(1)}, f32[15,8,128]{2,1,0:T(8,128)S(1)}, u32[]{:S(2)}, u32[]{:S(2)}) collective-permute-start(f32[15,8,128]{2,1,0:T(8,128)S(1)} %get-tuple-element.31), channel_id=1, source_target_pairs={{0,756},{12,24},{24,12},{36,48},{48,36},{60,72},{72,60},{84,96},{9... | collective-permute-start | bytes 184328 | tf_op jit(solution)/shard_map/ppermute | solution.py:527
  36.3 13.0 %copy-start.2 = (f32[8,8,128]{2,1,0:T(8,128)S(1)}, f32[8,8,128]{2,1,0:T(8,128)}, u32[]{:S(2)}) copy-start(f32[8,8,128]{2,1,0:T(8,128)} %dt_ref.7) | copy-start | bytes 98308
  38.5 5.3 %collective-permute-start.6 = (f32[15,8,128]{2,1,0:T(8,128)S(1)}, f32[15,8,128]{2,1,0:T(8,128)S(1)}, u32[]{:S(2)}, u32[]{:S(2)}) collective-permute-start(f32[15,8,128]{2,1,0:T(8,128)S(1)} %get-tuple-element.34), channel_id=1, source_target_pairs={{0,12},{12,0},{24,36},{36,24},{48,60},{60,48},{72,84},{84,72},{96,... | collective-permute-start | bytes 184328 | tf_op jit(solution)/shard_map/ppermute | solution.py:528
  40.4 8.9 %collective-permute-start.7 = (f32[15,8,128]{2,1,0:T(8,128)S(1)}, f32[15,8,128]{2,1,0:T(8,128)S(1)}, u32[]{:S(2)}, u32[]{:S(2)}) collective-permute-start(f32[15,8,128]{2,1,0:T(8,128)S(1)} %get-tuple-element.35), channel_id=1, source_target_pairs={{0,756},{12,24},{24,12},{36,48},{48,36},{60,72},{72,60},{84,96},{9... | collective-permute-start | bytes 184328 | tf_op jit(solution)/shard_map/ppermute | solution.py:527
  53.4 5.3 %collective-permute-start.8 = (f32[9,8,128]{2,1,0:T(8,128)S(1)}, f32[9,8,128]{2,1,0:T(8,128)S(1)}, u32[]{:S(2)}, u32[]{:S(2)}) collective-permute-start(f32[9,8,128]{2,1,0:T(8,128)S(1)} %get-tuple-element.39), channel_id=1, source_target_pairs={{0,12},{12,0},{24,36},{36,24},{48,60},{60,48},{72,84},{84,72},{96,... | collective-permute-start | bytes 110600 | tf_op jit(solution)/shard_map/ppermute | solution.py:528
  55.4 8.6 %collective-permute-start.9 = (f32[9,8,128]{2,1,0:T(8,128)S(1)}, f32[9,8,128]{2,1,0:T(8,128)S(1)}, u32[]{:S(2)}, u32[]{:S(2)}) collective-permute-start(f32[9,8,128]{2,1,0:T(8,128)S(1)} %get-tuple-element.40), channel_id=1, source_target_pairs={{0,756},{12,24},{24,12},{36,48},{48,36},{60,72},{72,60},{84,96},{9... | collective-permute-start | bytes 110600 | tf_op jit(solution)/shard_map/ppermute | solution.py:527

commit v3 on v2

--- a/solution.py
+++ b/solution.py
@@ -38,7 +38,7 @@
     return jnp.where(j % 2 == 0, rots(x, -1), rots(x, 1))
 
 
-def ghost_rows(own2, prev2, next2, kind, rot):
+def ghost_rows(own2, prev2, next2, kind, flip, turn):
     nearest = []
     for r in range(2):
         picked = []
@@ -47,18 +47,16 @@
             x = jnp.where(kind == 2, wall, 0.0)
             x = jnp.where(kind == 1, next2[r][v], x)
             x = jnp.where(kind == 0, prev2[r][v], x)
-            picked.append(jnp.where(rot % 2 == 1, reverse_j(x), x))
-        turn = rot // 2 % 2 == 1
+            picked.append(jnp.where(flip == 1, reverse_j(x), x))
         a, b = picked[2], picked[3]
-        picked[2], picked[3] = jnp.where(turn, -b, a), jnp.where(turn, a, b)
+        picked[2], picked[3] = jnp.where(turn == 1, -b, a), jnp.where(turn == 1, a, b)
         nearest.append(picked)
     return nearest
 
 
 def with_ghosts(rows, below, above, meta):
-    t_lo, t_hi, r_lo, r_hi = meta
-    lo = ghost_rows([rows[0], rows[1]], [below[1], below[0]], [above[0], above[1]], t_lo, r_lo)
-    hi = ghost_rows([rows[-1], rows[-2]], [above[0], above[1]], [below[1], below[0]], t_hi, r_hi)
+    lo = ghost_rows([rows[0], rows[1]], [below[1], below[0]], [above[0], above[1]], *meta[:3])
+    hi = ghost_rows([rows[-1], rows[-2]], [above[0], above[1]], [below[1], below[0]], *meta[3:])
     return [lo[1], lo[0]] + rows + [hi[0], hi[1]]
 
 
@@ -66,10 +64,10 @@
     half = 0.5 * q[1 + d]
     out = []
     for u in range(NV):
-        acc = (a[d][u][u] + half) * q[u]
+        acc = (a(d, u, u) + half) * q[u]
         for v in range(NV):
             if v != u:
-                acc = acc + a[d][u][v] * q[v]
+                acc = acc + a(d, u, v) * q[v]
         out.append(acc)
     return out
 
@@ -80,13 +78,13 @@
         even = None
         for v in range(NV):
             if v != 2:
-                term = a[1][u][v] * q[v]
+                term = a(1, u, v) * q[v]
                 even = term if even is None else even + term
         if u == 2:
             even = even + 0.5 * (q[2] * q[2])
-            odd = a[1][2][2] * q[2]
+            odd = a(1, 2, 2) * q[2]
         else:
-            odd = q[2] * (a[1][u][2] + 0.5 * q[u])
+            odd = q[2] * (a(1, u, 2) + 0.5 * q[u])
         out.append(even + odd)
         mirrored.append(even - odd)
     return out, mirrored
@@ -143,6 +141,10 @@
     for tile in halo:
         f = flux(tile, a, 2)
         edge.append([jnp.where(upper, f[u] + C1 * tile[u], f[u] - C1 * tile[u]) for u in range(NV)])
+    beside = []
+    for i in range(n):
+        g, first = unit * i // 4, unit * i % 4 * SEG + HALO
+        beside.append([(rotl(halo[g][u], -first), rotl(edge[g][u], -first)) for u in range(NV)])
     fi = {m: flux(padded[m], a, 0) for m in range(1, n + 3)}
     result = []
     for i in range(n):
@@ -150,11 +152,10 @@
         q = padded[m]
         fj, gj = flux_j(q, a)
         fk = flux(q, a, 2)
-        g, first = unit * i // 4, unit * i % 4 * SEG + HALO
         row = []
         for u in range(NV):
             x = q[u]
-            s, e = rotl(halo[g][u], -first), rotl(edge[g][u], -first)
+            s, e = beside[i][u]
             acc = second_index(fj, gj, q, u, unit, weights, ends)
             acc = acc + (fi[m + 1][u] - fi[m - 1][u])
             acc = acc + C1 * (padded[m + 1][u] + padded[m - 1][u]) + C2 * (padded[m + 2][u] + padded[m - 2][u])
@@ -220,7 +221,7 @@
 
 
 def halo_ghost(halo, below, above, meta):
-    t_lo, t_hi, r_lo, r_hi = meta
+    t_lo, flip_lo, turn_lo, t_hi, flip_hi, turn_hi = meta
     r = seg()
     high_side = r < 2
     even_part = r % 2 == 0
@@ -228,6 +229,7 @@
     def turned(x):
         return jnp.where(even_part, rotl(x, SEG), rotl(x, -SEG))
 
+    flip = jnp.where(high_side, flip_hi, flip_lo)
     picked = []
     for v in range(NV):
         wall_lo, wall_hi = turned(halo[0][v]), turned(halo[1][v])
@@ -240,9 +242,8 @@
         lo = jnp.where(t_lo == 1, turned(above[v]), lo)
         lo = jnp.where(t_lo == 0, below[v], lo)
         x = jnp.where(high_side, hi, lo)
-        code = jnp.where(high_side, r_hi, r_lo)
-        picked.append(jnp.where(code % 2 == 1, reverse_j(x), x))
-    turn = jnp.where(high_side, r_hi, r_lo) // 2 % 2 == 1
+        picked.append(jnp.where(flip == 1, reverse_j(x), x))
+    turn = jnp.where(high_side, turn_hi, turn_lo) == 1
     b, c = picked[2], picked[3]
     picked[2], picked[3] = jnp.where(turn, -c, b), jnp.where(turn, b, c)
     return picked
@@ -258,8 +259,10 @@
     return [[cell_mean(rows[2 * c][v] + rows[2 * c + 1][v]) for v in range(len(rows[0]))] for c in range(len(rows) // 2)]
 
 
-def halo_mean(x):
-    return cell_mean(x + jnp.where(seg() % 2 == 0, rotl(x, -SEG), rotl(x, SEG)))
+def halo_means(tiles):
+    even = seg() % 2 == 0
+    tiles = [x + jnp.where(even, rotl(x, -SEG), rotl(x, SEG)) for x in tiles]
+    return [cell_mean(x) for x in tiles]
 
 
 def load(ref, first, count):
@@ -282,12 +285,22 @@
             ref[g, v] = tiles[g][v]
 
 
-def coefficients(a_ref):
-    return [[[a_ref[d, u, v] for v in range(NV)] for u in range(NV)] for d in range(3)]
-
-
-def meta_of(type_ref, rot_ref):
-    return (type_ref[0, 0], type_ref[0, 1], rot_ref[0, 0], rot_ref[0, 1])
+def table_kernel(a_ref, type_ref, rot_ref, table_ref):
+    values = [a_ref[d, u, v] for d in range(3) for u in range(NV) for v in range(NV)]
+    for face in range(2):
+        kind, rot = type_ref[0, face], rot_ref[0, face]
+        values += [kind.astype(jnp.float32), (rot % 2).astype(jnp.float32), (rot // 2 % 2).astype(jnp.float32)]
+    for n, value in enumerate(values):
+        table_ref[n] = jnp.full((8, 128), value, jnp.float32)
+
+
+def coefficients(table_ref):
+    return lambda d, u, v: table_ref[(d * NV + u) * NV + v]
+
+
+def meta_of(table_ref):
+    first = 3 * NV * NV
+    return [table_ref[first + n] for n in range(6)]
 
 
 def masked(tiles):
@@ -370,17 +383,8 @@
     return fields
 
 
-def pack_kernel(q_hbm, dt_hbm, ends_ref, ma, mb, to_left, to_right, q_ref, dt_ref, sems):
-    copies = (
-        pltpu.make_async_copy(q_hbm, q_ref, sems.at[0]),
-        pltpu.make_async_copy(dt_hbm, dt_ref, sems.at[1]),
-    )
-    for copy in copies:
-        copy.start()
-    for copy in copies:
-        copy.wait()
+def pack_kernel(q_ref, dt_ref, ends_ref, ma, mb, to_left, to_right):
     rows = load(q_ref, 0, NI)
-    send_rows(ma, mb, 0, rows)
     ends = pack_ends(rows)
     store_tiles(ends_ref, ends)
     r, lower = seg(), place() < HALO
@@ -394,6 +398,7 @@
         x, y = tiles[2 * n], tiles[2 * n + 1]
         to_right[n] = jnp.where(lower, x, rotl(y, HALO))
         to_left[n] = jnp.where(lower, rotl(y, -HALO), x)
+    send_rows(ma, mb, 0, rows)
 
 
 def unpack(from_right, from_left):
@@ -411,8 +416,8 @@
     return [[start[i][v] - (0.5 * factor * dt[i]) * twice[i][v] for v in range(NV)] for i in range(len(start))]
 
 
-def first_kernel(a_ref, type_ref, rot_ref, q_ref, dt_ref, ga, gb, from_right, from_left, t1_ref, h0_ref, dth_ref, ma, mb):
-    a, meta = coefficients(a_ref), meta_of(type_ref, rot_ref)
+def first_kernel(table_ref, q_ref, dt_ref, ga, gb, from_right, from_left, t1_ref, h0_ref, dth_ref, ma, mb):
+    a, meta = coefficients(table_ref), meta_of(table_ref)
     h0, dth = unpack(from_right, from_left)
     store_tiles(h0_ref, h0)
     for g in range(2):
@@ -427,9 +432,9 @@
 
 
 def second_kernel(
-    a_ref, type_ref, rot_ref, q_ref, t1_ref, h0_ref, ends_ref, dt_ref, dth_ref, ga, gb, t2_ref, h1_ref, ma, mb
+    table_ref, q_ref, t1_ref, h0_ref, ends_ref, dt_ref, dth_ref, ga, gb, t2_ref, h1_ref, ma, mb
 ):
-    a, meta = coefficients(a_ref), meta_of(type_ref, rot_ref)
+    a, meta = coefficients(table_ref), meta_of(table_ref)
     h0 = load_tiles(h0_ref)
     below, above = receive_halo(ga, gb, 2 * NV)
     twice = halo_residual2(h0, halo_ghost(h0, below, above, meta), load_tiles(ends_ref), a)
@@ -445,9 +450,9 @@
 
 
 def third_kernel(
-    a_ref, type_ref, rot_ref, t1_ref, t2_ref, h0_ref, h1_ref, dt_ref, dth_ref, ga, gb, res_ref, h2_ref, c1_ref, mean_ref, ma, mb
+    table_ref, t1_ref, t2_ref, h0_ref, h1_ref, dt_ref, dth_ref, ga, gb, res_ref, h2_ref, c1_ref, mean_ref, ma, mb
 ):
-    a, meta = coefficients(a_ref), meta_of(type_ref, rot_ref)
+    a, meta = coefficients(table_ref), meta_of(table_ref)
     h0, h1 = load_tiles(h0_ref), load_tiles(h1_ref)
     below, above = receive_halo(ga, gb, 2 * NV)
     twice = halo_residual2(h1, halo_ghost(h1, below, above, meta), pack_ends(load(t1_ref, 0, NI)), a)
@@ -469,18 +474,19 @@
     send_coarse(ma, mb, 0, c1, start)
 
 
-def fourth_kernel(a_ref, type_ref, rot_ref, t2_ref, h2_ref, c1_ref, mean_ref, dt_ref, dth_ref, ga, gb, out_ref):
-    a, meta = coefficients(a_ref), meta_of(type_ref, rot_ref)
+def fourth_kernel(table_ref, t2_ref, h2_ref, c1_ref, mean_ref, dt_ref, dth_ref, res_ref, ga, gb, out_hbm, res_hbm, out_ref, sems):
+    a, meta = coefficients(table_ref), meta_of(table_ref)
     half = NI // 2
+    copies = [pltpu.make_async_copy(res_ref, res_hbm, sems.at[half])]
+    copies[0].start()
     h2, t2 = load_tiles(h2_ref), load(t2_ref, 0, NI)
     below, above = receive_halo(ga, gb, NV)
     twice = halo_residual2(h2, halo_ghost(h2, below, above, meta), pack_ends(t2), a)
-    start_h = [[halo_mean(x) for x in tile] for tile in h2]
-    c1_h = []
-    for g in range(2):
-        step = halo_mean(dth_ref[g])
-        c1_h.append([start_h[g][v] - (0.2 * step) * halo_mean(twice[g][v]) for v in range(NV)])
-    c1_h = masked(c1_h)
+    means = halo_means(h2[0] + h2[1] + [dth_ref[0], dth_ref[1]] + twice[0] + twice[1])
+    start_h, step_h, mean_h = means[: 2 * NV], means[2 * NV : 2 * NV + 2], means[2 * NV + 2 :]
+    c1_h = [start_h[t] - (0.2 * step_h[t // NV]) * mean_h[t] for t in range(2 * NV)]
+    start_h = [start_h[:NV], start_h[NV:]]
+    c1_h = masked([c1_h[:NV], c1_h[NV:]])
     start, c1 = restrict_rows(t2), load(c1_ref, 0, half)
     (below1, above1), (below0, above0) = receive_coarse(ga, gb, 0)
     twice0 = residual2(with_ghosts(start, below0, above0, meta), start_h, a, 2)
@@ -491,6 +497,12 @@
             change = -step * (0.5 * (twice1[c][v] - twice0[c][v]) + mean_ref[v, c])
             out_ref[v, 2 * c] = t2[2 * c][v] + change
             out_ref[v, 2 * c + 1] = t2[2 * c + 1][v] + change
+    for c in range(half):
+        rows = pl.ds(2 * c, 2)
+        copies.append(pltpu.make_async_copy(out_ref.at[:, rows], out_hbm.at[:, rows], sems.at[c]))
+        copies[-1].start()
+    for copy in copies:
+        copy.wait()
 
 
 def field(rows):
@@ -501,14 +513,13 @@
     return (*count, 8, 128)
 
 
-def call(kernel, scalars, arrays, outs, in_hbm=False, scratch=()):
+def call(kernel, arrays, outs, scalars=(), out_space=pltpu.VMEM, scratch=()):
     smem, vmem = pl.BlockSpec(memory_space=pltpu.SMEM), pl.BlockSpec(memory_space=pltpu.VMEM)
-    given = pl.BlockSpec(memory_space=pltpu.HBM) if in_hbm else vmem
     return pl.pallas_call(
         kernel,
         out_shape=[jax.ShapeDtypeStruct(shape, jnp.float32) for shape in outs],
-        in_specs=[smem] * len(scalars) + [given] * len(arrays),
-        out_specs=[vmem] * len(outs),
+        in_specs=[smem] * len(scalars) + [vmem] * len(arrays),
+        out_specs=[pl.BlockSpec(memory_space=out_space)] * len(outs),
         scratch_shapes=scratch,
         compiler_params=pltpu.CompilerParams(vmem_limit_bytes=VMEM_LIMIT),
     )(*scalars, *arrays)
@@ -520,7 +531,6 @@
     link = [(b, (b + 1) % blocks if b % 2 else (b - 1) % blocks) for b in range(blocks)]
     ahead = [(s, s + 1) for s in range(parts - 1)]
     back = [(s + 1, s) for s in range(parts - 1)]
-    scalars = (coupling, face_type, face_rot)
     pair = tiles_of(2, NV)
 
     def exchange(ma, mb):
@@ -528,17 +538,11 @@
         ga = lax.ppermute(ma, "blk", chip)
         return ga, gb
 
+    (table,) = call(table_kernel, (), (tiles_of(3 * NV * NV + 6),), (coupling, face_type, face_rot))
     ends, ma, mb, to_left, to_right = call(
         pack_kernel,
-        (),
         (flow_state, timestep),
         (pair, tiles_of(2 * NV), tiles_of(2 * NV), tiles_of(NV + 1), tiles_of(NV + 1)),
-        in_hbm=True,
-        scratch=(
-            pltpu.VMEM(field(NI), jnp.float32),
-            pltpu.VMEM(tiles_of(NI), jnp.float32),
-            pltpu.SemaphoreType.DMA((2,)),
-        ),
     )
     ga, gb = exchange(ma, mb)
     from_right = lax.ppermute(to_left, "sub", back)
@@ -547,16 +551,14 @@
     message = tiles_of(2 * NV + NV // 2)
     t1, h0, dth, ma, mb = call(
         first_kernel,
-        scalars,
-        (flow_state, timestep, ga, gb, from_right, from_left),
+        (table, flow_state, timestep, ga, gb, from_right, from_left),
         (field(NI), pair, tiles_of(2), message, message),
     )
     ga, gb = exchange(ma, mb)
 
     t2, h1, ma, mb = call(
         second_kernel,
-        scalars,
-        (flow_state, t1, h0, ends, timestep, dth, ga, gb),
+        (table, flow_state, t1, h0, ends, timestep, dth, ga, gb),
         (field(NI), pair, message, message),
     )
     ga, gb = exchange(ma, mb)
@@ -564,14 +566,17 @@
     message = tiles_of(NV + NV // 2)
     res, h2, c1, mean, ma, mb = call(
         third_kernel,
-        scalars,
-        (t1, t2, h0, h1, timestep, dth, ga, gb),
+        (table, t1, t2, h0, h1, timestep, dth, ga, gb),
         (field(NI), pair, field(NI // 2), field(NI // 2), message, message),
     )
     ga, gb = exchange(ma, mb)
 
-    (updated,) = call(
-        fourth_kernel, scalars, (t2, h2, c1, mean, timestep, dth, ga, gb), (field(NI),)
+    updated, res = call(
+        fourth_kernel,
+        (table, t2, h2, c1, mean, timestep, dth, res, ga, gb),
+        (field(NI), field(NI)),
+        out_space=pltpu.HBM,
+        scratch=(pltpu.VMEM(field(NI), jnp.float32), pltpu.SemaphoreType.DMA((NI // 2 + 1,))),
     )
     return (updated, res)
 

time: 69.4 us -> 60.5 us (0.87)
  Pallas kernels: 14.2 us -> 5.89 us
  waiting for transfers between devices: 21 us -> 20.1 us
    pallas_call x5 -> x6, Pallas kernels: 14.2 us -> 5.89 us  [call(): pl.pallas_call(kernel, out_shape=[jax.ShapeDtypeStruct(shape, jnp.float32...]
    ppermute x1, waiting for transfers between devices: 4.79 us -> 3.95 us  [cycle(): from_left = lax.ppermute(to_right, 'sub', ahead)]
    unnamed x12 -> x14, local copies, waits for them, and re-layouts: 1.7 us -> 1.71 us
  transfers between devices with their start and end apart: 10 -> 10, of which waited for: 4 -> 4; matrix products, arithmetic and copies ran while one was open for 0% -> 0% of each run, Pallas kernels for 0% -> 1%
where the time goes in v3:
time: 60.5 us; the launch traced here: 60 us
  starting transfers between devices  31.4 us (52%)
  waiting for transfers between devices  20.1 us (33%)
  Pallas kernels  5.89 us (10%)
  local copies, waits for them, and re-layouts  1.71 us (3%)
  between operations  0.85 us (1%)
    ppermute x4, starting transfers between devices, exchange(): gb = lax.ppermute(mb, 'blk', link)  17.8 us
    ppermute x4, waiting for transfers between devices, exchange(): gb = lax.ppermute(mb, 'blk', link)  16.2 us
    ppermute x4, starting transfers between devices, exchange(): ga = lax.ppermute(ma, 'blk', chip)  7.68 us
    pallas_call x6, Pallas kernels, call(): pl.pallas_call(kernel, out_shape=[jax.ShapeDtypeStruct(shape, jnp.float32...  5.89 us
    ppermute x1, waiting for transfers between devices, cycle(): from_left = lax.ppermute(to_right, 'sub', ahead)  3.95 us
    ppermute x1, starting transfers between devices, cycle(): from_right = lax.ppermute(to_left, 'sub', back)  3.67 us
    ppermute x1, starting transfers between devices, cycle(): from_left = lax.ppermute(to_right, 'sub', ahead)  2.3 us
    unnamed x14, local copies, waits for them, and re-layouts  1.71 us
  transfers between devices with their start and end apart: 10, of which 4 were waited for; matrix products, arithmetic and copies ran while one was open for 0% of the time, Pallas kernels for 1%

profile of v3, /device:TPU:512, one launch (start us, length us, event | category | flops | bytes accessed | tf_op | source)
XLA Modules:
  0.0 60.0 jit_solution(17748891530500134399)
XLA Ops:
  0.6 0.0 copy-start
  0.6 0.9 %copy-done = f32[6,8,8,128]{3,2,1,0:T(8,128)S(1)} copy-done((f32[6,8,8,128]{3,2,1,0:T(8,128)S(1)}, f32[6,8,8,128]{3,2,1,0:T(8,128)}, u32[]{:S(2)}) %copy-start) | copy-done | bytes 196632
  1.6 0.0 copy-start.2
  1.6 0.8 %copy-done.2 = f32[8,8,128]{2,1,0:T(8,128)S(1)} copy-done((f32[8,8,128]{2,1,0:T(8,128)S(1)}, f32[8,8,128]{2,1,0:T(8,128)}, u32[]{:S(2)}) %copy-start.2) | copy-done | bytes 32792
  2.3 0.0 copy-start.4
  2.3 0.2 shard_map.69
  2.5 1.9 %collective-permute-start = (f32[12,8,128]{2,1,0:T(8,128)S(1)}, f32[12,8,128]{2,1,0:T(8,128)S(1)}, u32[]{:S(2)}, u32[]{:S(2)}) collective-permute-start(f32[12,8,128]{2,1,0:T(8,128)S(1)} %get-tuple-element.22), channel_id=1, source_target_pairs={{0,12},{12,0},{24,36},{36,24},{48,60},{60,48},{72,84},{84,72},{96,... | collective-permute-start | bytes 147464 | tf_op jit(solution)/shard_map/ppermute | solution.py:538
  4.4 7.7 %collective-permute-start.1 = (f32[12,8,128]{2,1,0:T(8,128)S(1)}, f32[12,8,128]{2,1,0:T(8,128)S(1)}, u32[]{:S(2)}, u32[]{:S(2)}) collective-permute-start(f32[12,8,128]{2,1,0:T(8,128)S(1)} %get-tuple-element.23), channel_id=1, source_target_pairs={{0,756},{12,24},{24,12},{36,48},{48,36},{60,72},{72,60},{84,96},{9... | collective-permute-start | bytes 147464 | tf_op jit(solution)/shard_map/ppermute | solution.py:537
  12.1 0.0 copy-start.5
  12.1 0.0 copy-start.6
  12.1 3.7 %collective-permute-start.2 = (f32[7,8,128]{2,1,0:T(8,128)S(1)}, f32[7,8,128]{2,1,0:T(8,128)S(1)}, u32[]{:S(2)}, u32[]{:S(2)}) collective-permute-start(f32[7,8,128]{2,1,0:T(8,128)S(1)} %get-tuple-element.24), channel_id=1, source_target_pairs={{1,0},{2,1},{3,2},{4,3},{5,4},{6,5},{7,6},{8,7},{9,8},{10,9},{11,1... | collective-permute-start | bytes 86024 | tf_op jit(solution)/shard_map/ppermute | solution.py:548
  15.8 0.0 copy-start.1
  15.8 0.0 copy-start.3
  15.8 2.3 %collective-permute-start.3 = (f32[7,8,128]{2,1,0:T(8,128)S(1)}, f32[7,8,128]{2,1,0:T(8,128)S(1)}, u32[]{:S(2)}, u32[]{:S(2)}) collective-permute-start(f32[7,8,128]{2,1,0:T(8,128)S(1)} %get-tuple-element.25), channel_id=1, source_target_pairs={{0,1},{1,2},{2,3},{3,4},{4,5},{5,6},{6,7},{7,8},{8,9},{9,10},{10,1... | collective-permute-start | bytes 86024 | tf_op jit(solution)/shard_map/ppermute | solution.py:549
  18.1 0.0 copy-done.4
  18.2 0.0 copy-done.5
  18.2 0.0 copy-done.6
  18.2 0.8 %shard_map.68.table_ref = f32[114,8,128]{2,1,0:T(8,128)S(1)} custom-call(f32[3,6,6]{2,1,0:T(8,128)S(1)} %copy-done.4, s32[1,2]{1,0:T(1,128)S(1)} %copy-done.5, s32[1,2]{1,0:T(1,128)S(1)} %copy-done.6), custom_call_target="tpu_custom_call" | custom-call | tf_op jit(solution)/shard_map/pallas_call | solution.py:518
  19.0 0.0 collective-permute-done.2.from_right
  19.0 3.9 %collective-permute-done.3.from_left = f32[7,8,128]{2,1,0:T(8,128)S(1)} collective-permute-done((f32[7,8,128]{2,1,0:T(8,128)S(1)}, f32[7,8,128]{2,1,0:T(8,128)S(1)}, u32[]{:S(2)}, u32[]{:S(2)}) %collective-permute-start.3) | collective-permute-done | bytes 28704 | tf_op jit(solution)/shard_map/ppermute | solution.py:549
  22.9 0.0 collective-permute-done.ga
  22.9 0.0 collective-permute-done.1.gb
  22.9 0.0 copy-done.1
  23.0 0.0 copy-done.3
  23.0 0.8 %shard_map.70 = (f32[6,8,8,128]{3,2,1,0:T(8,128)S(1)}, f32[2,6,8,128]{3,2,1,0:T(8,128)S(1)}, f32[2,8,128]{2,1,0:T(8,128)S(1)}, f32[15,8,128]{2,1,0:T(8,128)S(1)}, f32[15,8,128]{2,1,0:T(8,128)S(1)}) custom-call(f32[114,8,128]{2,1,0:T(8,128)S(1)} %shard_map.68.table_ref, f32[6,8,8,128]{3,2,1,0:T(8,128)S(1)} %copy-done.1, f32[8,8,128]{2,1,0:T(8,128)S(1)} %copy-done.3, ...), custom_call_target="tpu_custom_call" | custom-call | tf_op jit(solution)/shard_map/pallas_call | solution.py:518
  23.7 1.9 %collective-permute-start.4 = (f32[15,8,128]{2,1,0:T(8,128)S(1)}, f32[15,8,128]{2,1,0:T(8,128)S(1)}, u32[]{:S(2)}, u32[]{:S(2)}) collective-permute-start(f32[15,8,128]{2,1,0:T(8,128)S(1)} %get-tuple-element.30), channel_id=1, source_target_pairs={{0,12},{12,0},{24,36},{36,24},{48,60},{60,48},{72,84},{84,72},{96,... | collective-permute-start | bytes 184328 | tf_op jit(solution)/shard_map/ppermute | solution.py:538
  25.7 3.4 %collective-permute-start.5 = (f32[15,8,128]{2,1,0:T(8,128)S(1)}, f32[15,8,128]{2,1,0:T(8,128)S(1)}, u32[]{:S(2)}, u32[]{:S(2)}) collective-permute-start(f32[15,8,128]{2,1,0:T(8,128)S(1)} %get-tuple-element.31), channel_id=1, source_target_pairs={{0,756},{12,24},{24,12},{36,48},{48,36},{60,72},{72,60},{84,96},{9... | collective-permute-start | bytes 184328 | tf_op jit(solution)/shard_map/ppermute | solution.py:537
  29.0 0.0 collective-permute-done.4.ga
  29.1 5.5 %collective-permute-done.5.gb = f32[15,8,128]{2,1,0:T(8,128)S(1)} collective-permute-done((f32[15,8,128]{2,1,0:T(8,128)S(1)}, f32[15,8,128]{2,1,0:T(8,128)S(1)}, u32[]{:S(2)}, u32[]{:S(2)}) %collective-permute-start.5) | collective-permute-done | bytes 61472 | tf_op jit(solution)/shard_map/ppermute | solution.py:537
  34.5 1.0 %shard_map.71 = (f32[6,8,8,128]{3,2,1,0:T(8,128)S(1)}, f32[2,6,8,128]{3,2,1,0:T(8,128)S(1)}, f32[15,8,128]{2,1,0:T(8,128)S(1)}, f32[15,8,128]{2,1,0:T(8,128)S(1)}) custom-call(f32[114,8,128]{2,1,0:T(8,128)S(1)} %shard_map.68.table_ref, f32[6,8,8,128]{3,2,1,0:T(8,128)S(1)} %copy-done.1, f32[6,8,8,128]{3,2,1,0:T(8,128)S(1)} %get-tuple-element.26.t1_ref, ...), custom_call_target="tpu_custom_call" | custom-call | tf_op jit(solution)/shard_map/pallas_call | solution.py:518
  35.5 1.9 %collective-permute-start.6 = (f32[15,8,128]{2,1,0:T(8,128)S(1)}, f32[15,8,128]{2,1,0:T(8,128)S(1)}, u32[]{:S(2)}, u32[]{:S(2)}) collective-permute-start(f32[15,8,128]{2,1,0:T(8,128)S(1)} %get-tuple-element.34), channel_id=1, source_target_pairs={{0,12},{12,0},{24,36},{36,24},{48,60},{60,48},{72,84},{84,72},{96,... | collective-permute-start | bytes 184328 | tf_op jit(solution)/shard_map/ppermute | solution.py:538
  37.5 3.4 %collective-permute-start.7 = (f32[15,8,128]{2,1,0:T(8,128)S(1)}, f32[15,8,128]{2,1,0:T(8,128)S(1)}, u32[]{:S(2)}, u32[]{:S(2)}) collective-permute-start(f32[15,8,128]{2,1,0:T(8,128)S(1)} %get-tuple-element.35), channel_id=1, source_target_pairs={{0,756},{12,24},{24,12},{36,48},{48,36},{60,72},{72,60},{84,96},{9... | collective-permute-start | bytes 184328 | tf_op jit(solution)/shard_map/ppermute | solution.py:537
  40.8 0.0 collective-permute-done.6.ga
  40.8 5.5 %collective-permute-done.7.gb = f32[15,8,128]{2,1,0:T(8,128)S(1)} collective-permute-done((f32[15,8,128]{2,1,0:T(8,128)S(1)}, f32[15,8,128]{2,1,0:T(8,128)S(1)}, u32[]{:S(2)}, u32[]{:S(2)}) %collective-permute-start.7) | collective-permute-done | bytes 61472 | tf_op jit(solution)/shard_map/ppermute | solution.py:537
  46.3 1.1 %shard_map.72 = (f32[6,8,8,128]{3,2,1,0:T(8,128)S(1)}, f32[2,6,8,128]{3,2,1,0:T(8,128)S(1)}, f32[6,4,8,128]{3,2,1,0:T(8,128)S(1)}, f32[6,4,8,128]{3,2,1,0:T(8,12...) custom-call(f32[114,8,128]{2,1,0:T(8,128)S(1)} %shard_map.68.table_ref, ...), custom_call_target="tpu_custom_call" | custom-call | tf_op jit(solution)/shard_map/pallas_call | solution.py:518
  47.5 1.9 %collective-permute-start.8 = (f32[9,8,128]{2,1,0:T(8,128)S(1)}, f32[9,8,128]{2,1,0:T(8,128)S(1)}, u32[]{:S(2)}, u32[]{:S(2)}) collective-permute-start(f32[9,8,128]{2,1,0:T(8,128)S(1)} %get-tuple-element.40), channel_id=1, source_target_pairs={{0,12},{12,0},{24,36},{36,24},{48,60},{60,48},{72,84},{84,72},{96,... | collective-permute-start | bytes 110600 | tf_op jit(solution)/shard_map/ppermute | solution.py:538
  49.4 3.4 %collective-permute-start.9 = (f32[9,8,128]{2,1,0:T(8,128)S(1)}, f32[9,8,128]{2,1,0:T(8,128)S(1)}, u32[]{:S(2)}, u32[]{:S(2)}) collective-permute-start(f32[9,8,128]{2,1,0:T(8,128)S(1)} %get-tuple-element.41), channel_id=1, source_target_pairs={{0,756},{12,24},{24,12},{36,48},{48,36},{60,72},{72,60},{84,96},{9... | collective-permute-start | bytes 110600 | tf_op jit(solution)/shard_map/ppermute | solution.py:537
  52.8 0.0 collective-permute-done.8.ga
  52.8 5.2 %collective-permute-done.9.gb = f32[9,8,128]{2,1,0:T(8,128)S(1)} collective-permute-done((f32[9,8,128]{2,1,0:T(8,128)S(1)}, f32[9,8,128]{2,1,0:T(8,128)S(1)}, u32[]{:S(2)}, u32[]{:S(2)}) %collective-permute-start.9) | collective-permute-done | bytes 36896 | tf_op jit(solution)/shard_map/ppermute | solution.py:537
  58.0 2.0 %shard_map.73 = (f32[6,8,8,128]{3,2,1,0:T(8,128)}, f32[6,8,8,128]{3,2,1,0:T(8,128)}) custom-call(f32[114,8,128]{2,1,0:T(8,128)S(1)} %shard_map.68.table_ref, f32[6,8,8,128]{3,2,1,0:T(8,128)S(1)} %get-tuple-element.32.t2_ref, f32[2,6,8,128]{3,2,1,0:T(8,128)S(1)} %get-tuple-element.36.h2_ref, f32[6,4,8,128]{3,2,1,0:T(8,128)S(1)} %get-tuple-element.37.c1_ref, ...), custom_call_target="tpu_custom_call" | custom-call | tf_op jit(solution)/shard_map/pallas_call | solution.py:518
Async XLA Ops:
  0.6 0.9 %copy-start = (f32[6,8,8,128]{3,2,1,0:T(8,128)S(1)}, f32[6,8,8,128]{3,2,1,0:T(8,128)}, u32[]{:S(2)}) copy-start(f32[6,8,8,128]{3,2,1,0:T(8,128)} %q_ref.5) | copy-start | bytes 589828
  1.6 0.8 %copy-start.2 = (f32[8,8,128]{2,1,0:T(8,128)S(1)}, f32[8,8,128]{2,1,0:T(8,128)}, u32[]{:S(2)}) copy-start(f32[8,8,128]{2,1,0:T(8,128)} %dt_ref.9) | copy-start | bytes 98308
  2.3 15.8 %copy-start.4 = (f32[3,6,6]{2,1,0:T(8,128)S(1)}, f32[3,6,6]{2,1,0:T(8,128)}, u32[]{:S(2)}) copy-start(f32[3,6,6]{2,1,0:T(8,128)} %a_ref.1) | copy-start | bytes 1300
  2.5 20.4 %collective-permute-start = (f32[12,8,128]{2,1,0:T(8,128)S(1)}, f32[12,8,128]{2,1,0:T(8,128)S(1)}, u32[]{:S(2)}, u32[]{:S(2)}) collective-permute-start(f32[12,8,128]{2,1,0:T(8,128)S(1)} %get-tuple-element.22), channel_id=1, source_target_pairs={{0,12},{12,0},{24,36},{36,24},{48,60},{60,48},{72,84},{84,72},{96,... | collective-permute-start | bytes 147464 | tf_op jit(solution)/shard_map/ppermute | solution.py:538
  4.4 18.5 %collective-permute-start.1 = (f32[12,8,128]{2,1,0:T(8,128)S(1)}, f32[12,8,128]{2,1,0:T(8,128)S(1)}, u32[]{:S(2)}, u32[]{:S(2)}) collective-permute-start(f32[12,8,128]{2,1,0:T(8,128)S(1)} %get-tuple-element.23), channel_id=1, source_target_pairs={{0,756},{12,24},{24,12},{36,48},{48,36},{60,72},{72,60},{84,96},{9... | collective-permute-start | bytes 147464 | tf_op jit(solution)/shard_map/ppermute | solution.py:537
  12.1 6.1 %copy-start.5 = (s32[1,2]{1,0:T(1,128)S(1)}, s32[1,2]{1,0:T(1,128)}, u32[]{:S(2)}) copy-start(s32[1,2]{1,0:T(1,128)} %type_ref.1) | copy-start | bytes 28
  12.1 6.0 %copy-start.6 = (s32[1,2]{1,0:T(1,128)S(1)}, s32[1,2]{1,0:T(1,128)}, u32[]{:S(2)}) copy-start(s32[1,2]{1,0:T(1,128)} %rot_ref.1) | copy-start | bytes 28
  12.1 6.9 %collective-permute-start.2 = (f32[7,8,128]{2,1,0:T(8,128)S(1)}, f32[7,8,128]{2,1,0:T(8,128)S(1)}, u32[]{:S(2)}, u32[]{:S(2)}) collective-permute-start(f32[7,8,128]{2,1,0:T(8,128)S(1)} %get-tuple-element.24), channel_id=1, source_target_pairs={{1,0},{2,1},{3,2},{4,3},{5,4},{6,5},{7,6},{8,7},{9,8},{10,9},{11,1... | collective-permute-start | bytes 86024 | tf_op jit(solution)/shard_map/ppermute | solution.py:548
  15.8 7.1 %copy-start.1 = (f32[6,8,8,128]{3,2,1,0:T(8,128)S(1)}, f32[6,8,8,128]{3,2,1,0:T(8,128)}, u32[]{:S(2)}) copy-start(f32[6,8,8,128]{3,2,1,0:T(8,128)} %q_ref.5) | copy-start | bytes 589828
  15.8 7.1 %copy-start.3 = (f32[8,8,128]{2,1,0:T(8,128)S(1)}, f32[8,8,128]{2,1,0:T(8,128)}, u32[]{:S(2)}) copy-start(f32[8,8,128]{2,1,0:T(8,128)} %dt_ref.9) | copy-start | bytes 98308
  15.8 7.1 %collective-permute-start.3 = (f32[7,8,128]{2,1,0:T(8,128)S(1)}, f32[7,8,128]{2,1,0:T(8,128)S(1)}, u32[]{:S(2)}, u32[]{:S(2)}) collective-permute-start(f32[7,8,128]{2,1,0:T(8,128)S(1)} %get-tuple-element.25), channel_id=1, source_target_pairs={{0,1},{1,2},{2,3},{3,4},{4,5},{5,6},{6,7},{7,8},{8,9},{9,10},{10,1... | collective-permute-start | bytes 86024 | tf_op jit(solution)/shard_map/ppermute | solution.py:549
  23.7 5.3 %collective-permute-start.4 = (f32[15,8,128]{2,1,0:T(8,128)S(1)}, f32[15,8,128]{2,1,0:T(8,128)S(1)}, u32[]{:S(2)}, u32[]{:S(2)}) collective-permute-start(f32[15,8,128]{2,1,0:T(8,128)S(1)} %get-tuple-element.30), channel_id=1, source_target_pairs={{0,12},{12,0},{24,36},{36,24},{48,60},{60,48},{72,84},{84,72},{96,... | collective-permute-start | bytes 184328 | tf_op jit(solution)/shard_map/ppermute | solution.py:538
  25.7 8.9 %collective-permute-start.5 = (f32[15,8,128]{2,1,0:T(8,128)S(1)}, f32[15,8,128]{2,1,0:T(8,128)S(1)}, u32[]{:S(2)}, u32[]{:S(2)}) collective-permute-start(f32[15,8,128]{2,1,0:T(8,128)S(1)} %get-tuple-element.31), channel_id=1, source_target_pairs={{0,756},{12,24},{24,12},{36,48},{48,36},{60,72},{72,60},{84,96},{9... | collective-permute-start | bytes 184328 | tf_op jit(solution)/shard_map/ppermute | solution.py:537
  35.5 5.3 %collective-permute-start.6 = (f32[15,8,128]{2,1,0:T(8,128)S(1)}, f32[15,8,128]{2,1,0:T(8,128)S(1)}, u32[]{:S(2)}, u32[]{:S(2)}) collective-permute-start(f32[15,8,128]{2,1,0:T(8,128)S(1)} %get-tuple-element.34), channel_id=1, source_target_pairs={{0,12},{12,0},{24,36},{36,24},{48,60},{60,48},{72,84},{84,72},{96,... | collective-permute-start | bytes 184328 | tf_op jit(solution)/shard_map/ppermute | solution.py:538
  37.5 8.9 %collective-permute-start.7 = (f32[15,8,128]{2,1,0:T(8,128)S(1)}, f32[15,8,128]{2,1,0:T(8,128)S(1)}, u32[]{:S(2)}, u32[]{:S(2)}) collective-permute-start(f32[15,8,128]{2,1,0:T(8,128)S(1)} %get-tuple-element.35), channel_id=1, source_target_pairs={{0,756},{12,24},{24,12},{36,48},{48,36},{60,72},{72,60},{84,96},{9... | collective-permute-start | bytes 184328 | tf_op jit(solution)/shard_map/ppermute | solution.py:537
  47.5 5.3 %collective-permute-start.8 = (f32[9,8,128]{2,1,0:T(8,128)S(1)}, f32[9,8,128]{2,1,0:T(8,128)S(1)}, u32[]{:S(2)}, u32[]{:S(2)}) collective-permute-start(f32[9,8,128]{2,1,0:T(8,128)S(1)} %get-tuple-element.40), channel_id=1, source_target_pairs={{0,12},{12,0},{24,36},{36,24},{48,60},{60,48},{72,84},{84,72},{96,... | collective-permute-start | bytes 110600 | tf_op jit(solution)/shard_map/ppermute | solution.py:538
  49.4 8.6 %collective-permute-start.9 = (f32[9,8,128]{2,1,0:T(8,128)S(1)}, f32[9,8,128]{2,1,0:T(8,128)S(1)}, u32[]{:S(2)}, u32[]{:S(2)}) collective-permute-start(f32[9,8,128]{2,1,0:T(8,128)S(1)} %get-tuple-element.41), channel_id=1, source_target_pairs={{0,756},{12,24},{24,12},{36,48},{48,36},{60,72},{72,60},{84,96},{9... | collective-permute-start | bytes 110600 | tf_op jit(solution)/shard_map/ppermute | solution.py:537

commit v4 on v3

--- a/solution.py
+++ b/solution.py
@@ -383,7 +383,11 @@
     return fields
 
 
-def pack_kernel(q_ref, dt_ref, ends_ref, ma, mb, to_left, to_right):
+def prime_kernel(out_ref):
+    out_ref[...] = jnp.zeros_like(out_ref)
+
+
+def pack_kernel(prime_ref, q_ref, dt_ref, ends_ref, ma, mb, to_left, to_right):
     rows = load(q_ref, 0, NI)
     ends = pack_ends(rows)
     store_tiles(ends_ref, ends)
@@ -539,9 +543,10 @@
         return ga, gb
 
     (table,) = call(table_kernel, (), (tiles_of(3 * NV * NV + 6),), (coupling, face_type, face_rot))
+    (prime,) = call(prime_kernel, (), (tiles_of(114),))
     ends, ma, mb, to_left, to_right = call(
         pack_kernel,
-        (flow_state, timestep),
+        (prime, flow_state, timestep),
         (pair, tiles_of(2 * NV), tiles_of(2 * NV), tiles_of(NV + 1), tiles_of(NV + 1)),
     )
     ga, gb = exchange(ma, mb)

time: 60.5 us -> 59.4 us (0.982)
  local copies, waits for them, and re-layouts: 1.71 us -> 0.91 us
    unnamed x14 -> x10, local copies, waits for them, and re-layouts: 1.71 us -> 0.91 us
    pallas_call x6 -> x7, Pallas kernels: 5.89 us -> 5.86 us  [call(): pl.pallas_call(kernel, out_shape=[jax.ShapeDtypeStruct(shape, jnp.float32...]
where the time goes in v4:
time: 59.4 us; the launch traced here: 59 us
  starting transfers between devices  31.3 us (53%)
  waiting for transfers between devices  20.1 us (34%)
  Pallas kernels  5.86 us (10%)
  local copies, waits for them, and re-layouts  0.91 us (2%)
  between operations  0.84 us (1%)
    ppermute x4, starting transfers between devices, exchange(): gb = lax.ppermute(mb, 'blk', link)  17.8 us
    ppermute x4, waiting for transfers between devices, exchange(): gb = lax.ppermute(mb, 'blk', link)  16.2 us
    ppermute x4, starting transfers between devices, exchange(): ga = lax.ppermute(ma, 'blk', chip)  7.68 us
    pallas_call x7, Pallas kernels, call(): pl.pallas_call(kernel, out_shape=[jax.ShapeDtypeStruct(shape, jnp.float32...  5.86 us
    ppermute x1, waiting for transfers between devices, cycle(): from_left = lax.ppermute(to_right, 'sub', ahead)  3.95 us
    ppermute x1, starting transfers between devices, cycle(): from_right = lax.ppermute(to_left, 'sub', back)  3.67 us
    ppermute x1, starting transfers between devices, cycle(): from_left = lax.ppermute(to_right, 'sub', ahead)  2.17 us
  transfers between devices with their start and end apart: 10, of which 4 were waited for; matrix products, arithmetic and copies ran while one was open for 0% of the time, Pallas kernels for 1%

profile of v4, /device:TPU:512, one launch (start us, length us, event | category | flops | bytes accessed | tf_op | source)
XLA Modules:
  0.0 59.0 jit_solution(9221548191865409741)
XLA Ops:
  0.6 0.0 copy-start.1
  0.6 0.0 copy-start
  0.7 0.7 %copy-done.1 = f32[8,8,128]{2,1,0:T(8,128)S(1)} copy-done((f32[8,8,128]{2,1,0:T(8,128)S(1)}, f32[8,8,128]{2,1,0:T(8,128)}, u32[]{:S(2)}) %copy-start.1) | copy-done | bytes 32792
  1.4 0.2 copy-done
  1.6 0.0 copy-start.2
  1.6 0.2 shard_map.70
  1.8 1.9 %collective-permute-start = (f32[12,8,128]{2,1,0:T(8,128)S(1)}, f32[12,8,128]{2,1,0:T(8,128)S(1)}, u32[]{:S(2)}, u32[]{:S(2)}) collective-permute-start(f32[12,8,128]{2,1,0:T(8,128)S(1)} %get-tuple-element.22), channel_id=1, source_target_pairs={{0,12},{12,0},{24,36},{36,24},{48,60},{60,48},{72,84},{84,72},{96,... | collective-permute-start | bytes 147464 | tf_op jit(solution)/shard_map/ppermute | solution.py:542
  3.7 7.7 %collective-permute-start.1 = (f32[12,8,128]{2,1,0:T(8,128)S(1)}, f32[12,8,128]{2,1,0:T(8,128)S(1)}, u32[]{:S(2)}, u32[]{:S(2)}) collective-permute-start(f32[12,8,128]{2,1,0:T(8,128)S(1)} %get-tuple-element.23), channel_id=1, source_target_pairs={{0,756},{12,24},{24,12},{36,48},{48,36},{60,72},{72,60},{84,96},{9... | collective-permute-start | bytes 147464 | tf_op jit(solution)/shard_map/ppermute | solution.py:541
  11.4 0.0 copy-start.3
  11.4 0.0 copy-start.4
  11.4 3.7 %collective-permute-start.2 = (f32[7,8,128]{2,1,0:T(8,128)S(1)}, f32[7,8,128]{2,1,0:T(8,128)S(1)}, u32[]{:S(2)}, u32[]{:S(2)}) collective-permute-start(f32[7,8,128]{2,1,0:T(8,128)S(1)} %get-tuple-element.24), channel_id=1, source_target_pairs={{1,0},{2,1},{3,2},{4,3},{5,4},{6,5},{7,6},{8,7},{9,8},{10,9},{11,1... | collective-permute-start | bytes 86024 | tf_op jit(solution)/shard_map/ppermute | solution.py:553
  15.1 2.2 %collective-permute-start.3 = (f32[7,8,128]{2,1,0:T(8,128)S(1)}, f32[7,8,128]{2,1,0:T(8,128)S(1)}, u32[]{:S(2)}, u32[]{:S(2)}) collective-permute-start(f32[7,8,128]{2,1,0:T(8,128)S(1)} %get-tuple-element.25), channel_id=1, source_target_pairs={{0,1},{1,2},{2,3},{3,4},{4,5},{5,6},{6,7},{7,8},{8,9},{9,10},{10,1... | collective-permute-start | bytes 86024 | tf_op jit(solution)/shard_map/ppermute | solution.py:554
  17.2 0.0 copy-done.2
  17.3 0.0 copy-done.3
  17.3 0.0 copy-done.4
  17.3 0.8 %shard_map.68.table_ref = f32[114,8,128]{2,1,0:T(8,128)S(1)} custom-call(f32[3,6,6]{2,1,0:T(8,128)S(1)} %copy-done.2, s32[1,2]{1,0:T(1,128)S(1)} %copy-done.3, s32[1,2]{1,0:T(1,128)S(1)} %copy-done.4), custom_call_target="tpu_custom_call" | custom-call | tf_op jit(solution)/shard_map/pallas_call | solution.py:522
  18.1 0.0 collective-permute-done.2.from_right
  18.1 3.9 %collective-permute-done.3.from_left = f32[7,8,128]{2,1,0:T(8,128)S(1)} collective-permute-done((f32[7,8,128]{2,1,0:T(8,128)S(1)}, f32[7,8,128]{2,1,0:T(8,128)S(1)}, u32[]{:S(2)}, u32[]{:S(2)}) %collective-permute-start.3) | collective-permute-done | bytes 28704 | tf_op jit(solution)/shard_map/ppermute | solution.py:554
  22.0 0.0 collective-permute-done.ga
  22.0 0.0 collective-permute-done.1.gb
  22.1 0.8 %shard_map.71 = (f32[6,8,8,128]{3,2,1,0:T(8,128)S(1)}, f32[2,6,8,128]{3,2,1,0:T(8,128)S(1)}, f32[2,8,128]{2,1,0:T(8,128)S(1)}, f32[15,8,128]{2,1,0:T(8,128)S(1)}, f32[15,8,128]{2,1,0:T(8,128)S(1)}) custom-call(f32[114,8,128]{2,1,0:T(8,128)S(1)} %shard_map.68.table_ref, f32[6,8,8,128]{3,2,1,0:T(8,128)S(1)} %copy-done, f32[8,8,128]{2,1,0:T(8,128)S(1)} %copy-done.1, ...), custom_call_target="tpu_custom_call" | custom-call | tf_op jit(solution)/shard_map/pallas_call | solution.py:522
  22.8 1.9 %collective-permute-start.4 = (f32[15,8,128]{2,1,0:T(8,128)S(1)}, f32[15,8,128]{2,1,0:T(8,128)S(1)}, u32[]{:S(2)}, u32[]{:S(2)}) collective-permute-start(f32[15,8,128]{2,1,0:T(8,128)S(1)} %get-tuple-element.30), channel_id=1, source_target_pairs={{0,12},{12,0},{24,36},{36,24},{48,60},{60,48},{72,84},{84,72},{96,... | collective-permute-start | bytes 184328 | tf_op jit(solution)/shard_map/ppermute | solution.py:542
  24.8 3.4 %collective-permute-start.5 = (f32[15,8,128]{2,1,0:T(8,128)S(1)}, f32[15,8,128]{2,1,0:T(8,128)S(1)}, u32[]{:S(2)}, u32[]{:S(2)}) collective-permute-start(f32[15,8,128]{2,1,0:T(8,128)S(1)} %get-tuple-element.31), channel_id=1, source_target_pairs={{0,756},{12,24},{24,12},{36,48},{48,36},{60,72},{72,60},{84,96},{9... | collective-permute-start | bytes 184328 | tf_op jit(solution)/shard_map/ppermute | solution.py:541
  28.1 0.0 collective-permute-done.4.ga
  28.1 5.5 %collective-permute-done.5.gb = f32[15,8,128]{2,1,0:T(8,128)S(1)} collective-permute-done((f32[15,8,128]{2,1,0:T(8,128)S(1)}, f32[15,8,128]{2,1,0:T(8,128)S(1)}, u32[]{:S(2)}, u32[]{:S(2)}) %collective-permute-start.5) | collective-permute-done | bytes 61472 | tf_op jit(solution)/shard_map/ppermute | solution.py:541
  33.6 1.0 %shard_map.72 = (f32[6,8,8,128]{3,2,1,0:T(8,128)S(1)}, f32[2,6,8,128]{3,2,1,0:T(8,128)S(1)}, f32[15,8,128]{2,1,0:T(8,128)S(1)}, f32[15,8,128]{2,1,0:T(8,128)S(1)}) custom-call(f32[114,8,128]{2,1,0:T(8,128)S(1)} %shard_map.68.table_ref, f32[6,8,8,128]{3,2,1,0:T(8,128)S(1)} %copy-done, f32[6,8,8,128]{3,2,1,0:T(8,128)S(1)} %get-tuple-element.26.t1_ref, ...), custom_call_target="tpu_custom_call" | custom-call | tf_op jit(solution)/shard_map/pallas_call | solution.py:522
  34.6 1.9 %collective-permute-start.6 = (f32[15,8,128]{2,1,0:T(8,128)S(1)}, f32[15,8,128]{2,1,0:T(8,128)S(1)}, u32[]{:S(2)}, u32[]{:S(2)}) collective-permute-start(f32[15,8,128]{2,1,0:T(8,128)S(1)} %get-tuple-element.34), channel_id=1, source_target_pairs={{0,12},{12,0},{24,36},{36,24},{48,60},{60,48},{72,84},{84,72},{96,... | collective-permute-start | bytes 184328 | tf_op jit(solution)/shard_map/ppermute | solution.py:542
  36.5 3.4 %collective-permute-start.7 = (f32[15,8,128]{2,1,0:T(8,128)S(1)}, f32[15,8,128]{2,1,0:T(8,128)S(1)}, u32[]{:S(2)}, u32[]{:S(2)}) collective-permute-start(f32[15,8,128]{2,1,0:T(8,128)S(1)} %get-tuple-element.35), channel_id=1, source_target_pairs={{0,756},{12,24},{24,12},{36,48},{48,36},{60,72},{72,60},{84,96},{9... | collective-permute-start | bytes 184328 | tf_op jit(solution)/shard_map/ppermute | solution.py:541
  39.9 0.0 collective-permute-done.6.ga
  39.9 5.5 %collective-permute-done.7.gb = f32[15,8,128]{2,1,0:T(8,128)S(1)} collective-permute-done((f32[15,8,128]{2,1,0:T(8,128)S(1)}, f32[15,8,128]{2,1,0:T(8,128)S(1)}, u32[]{:S(2)}, u32[]{:S(2)}) %collective-permute-start.7) | collective-permute-done | bytes 61472 | tf_op jit(solution)/shard_map/ppermute | solution.py:541
  45.4 1.1 %shard_map.73 = (f32[6,8,8,128]{3,2,1,0:T(8,128)S(1)}, f32[2,6,8,128]{3,2,1,0:T(8,128)S(1)}, f32[6,4,8,128]{3,2,1,0:T(8,128)S(1)}, f32[6,4,8,128]{3,2,1,0:T(8,12...) custom-call(f32[114,8,128]{2,1,0:T(8,128)S(1)} %shard_map.68.table_ref, ...), custom_call_target="tpu_custom_call" | custom-call | tf_op jit(solution)/shard_map/pallas_call | solution.py:522
  46.5 1.9 %collective-permute-start.8 = (f32[9,8,128]{2,1,0:T(8,128)S(1)}, f32[9,8,128]{2,1,0:T(8,128)S(1)}, u32[]{:S(2)}, u32[]{:S(2)}) collective-permute-start(f32[9,8,128]{2,1,0:T(8,128)S(1)} %get-tuple-element.40), channel_id=1, source_target_pairs={{0,12},{12,0},{24,36},{36,24},{48,60},{60,48},{72,84},{84,72},{96,... | collective-permute-start | bytes 110600 | tf_op jit(solution)/shard_map/ppermute | solution.py:542
  48.4 3.4 %collective-permute-start.9 = (f32[9,8,128]{2,1,0:T(8,128)S(1)}, f32[9,8,128]{2,1,0:T(8,128)S(1)}, u32[]{:S(2)}, u32[]{:S(2)}) collective-permute-start(f32[9,8,128]{2,1,0:T(8,128)S(1)} %get-tuple-element.41), channel_id=1, source_target_pairs={{0,756},{12,24},{24,12},{36,48},{48,36},{60,72},{72,60},{84,96},{9... | collective-permute-start | bytes 110600 | tf_op jit(solution)/shard_map/ppermute | solution.py:541
  51.8 0.0 collective-permute-done.8.ga
  51.8 5.2 %collective-permute-done.9.gb = f32[9,8,128]{2,1,0:T(8,128)S(1)} collective-permute-done((f32[9,8,128]{2,1,0:T(8,128)S(1)}, f32[9,8,128]{2,1,0:T(8,128)S(1)}, u32[]{:S(2)}, u32[]{:S(2)}) %collective-permute-start.9) | collective-permute-done | bytes 36896 | tf_op jit(solution)/shard_map/ppermute | solution.py:541
  57.0 2.0 %shard_map.74 = (f32[6,8,8,128]{3,2,1,0:T(8,128)}, f32[6,8,8,128]{3,2,1,0:T(8,128)}) custom-call(f32[114,8,128]{2,1,0:T(8,128)S(1)} %shard_map.68.table_ref, f32[6,8,8,128]{3,2,1,0:T(8,128)S(1)} %get-tuple-element.32.t2_ref, f32[2,6,8,128]{3,2,1,0:T(8,128)S(1)} %get-tuple-element.36.h2_ref, f32[6,4,8,128]{3,2,1,0:T(8,128)S(1)} %get-tuple-element.37.c1_ref, ...), custom_call_target="tpu_custom_call" | custom-call | tf_op jit(solution)/shard_map/pallas_call | solution.py:522
  (1 shorter events, 0.0 us)
Async XLA Ops:
  0.6 0.8 %copy-start.1 = (f32[8,8,128]{2,1,0:T(8,128)S(1)}, f32[8,8,128]{2,1,0:T(8,128)}, u32[]{:S(2)}) copy-start(f32[8,8,128]{2,1,0:T(8,128)} %dt_ref.9) | copy-start | bytes 98308
  0.6 0.9 %copy-start = (f32[6,8,8,128]{3,2,1,0:T(8,128)S(1)}, f32[6,8,8,128]{3,2,1,0:T(8,128)}, u32[]{:S(2)}) copy-start(f32[6,8,8,128]{3,2,1,0:T(8,128)} %q_ref.5) | copy-start | bytes 589828
  1.6 15.7 %copy-start.2 = (f32[3,6,6]{2,1,0:T(8,128)S(1)}, f32[3,6,6]{2,1,0:T(8,128)}, u32[]{:S(2)}) copy-start(f32[3,6,6]{2,1,0:T(8,128)} %a_ref.1) | copy-start | bytes 1300
  1.8 20.3 %collective-permute-start = (f32[12,8,128]{2,1,0:T(8,128)S(1)}, f32[12,8,128]{2,1,0:T(8,128)S(1)}, u32[]{:S(2)}, u32[]{:S(2)}) collective-permute-start(f32[12,8,128]{2,1,0:T(8,128)S(1)} %get-tuple-element.22), channel_id=1, source_target_pairs={{0,12},{12,0},{24,36},{36,24},{48,60},{60,48},{72,84},{84,72},{96,... | collective-permute-start | bytes 147464 | tf_op jit(solution)/shard_map/ppermute | solution.py:542
  3.7 18.4 %collective-permute-start.1 = (f32[12,8,128]{2,1,0:T(8,128)S(1)}, f32[12,8,128]{2,1,0:T(8,128)S(1)}, u32[]{:S(2)}, u32[]{:S(2)}) collective-permute-start(f32[12,8,128]{2,1,0:T(8,128)S(1)} %get-tuple-element.23), channel_id=1, source_target_pairs={{0,756},{12,24},{24,12},{36,48},{48,36},{60,72},{72,60},{84,96},{9... | collective-permute-start | bytes 147464 | tf_op jit(solution)/shard_map/ppermute | solution.py:541
  11.4 5.9 %copy-start.3 = (s32[1,2]{1,0:T(1,128)S(1)}, s32[1,2]{1,0:T(1,128)}, u32[]{:S(2)}) copy-start(s32[1,2]{1,0:T(1,128)} %type_ref.1) | copy-start | bytes 28
  11.4 5.9 %copy-start.4 = (s32[1,2]{1,0:T(1,128)S(1)}, s32[1,2]{1,0:T(1,128)}, u32[]{:S(2)}) copy-start(s32[1,2]{1,0:T(1,128)} %rot_ref.1) | copy-start | bytes 28
  11.4 6.7 %collective-permute-start.2 = (f32[7,8,128]{2,1,0:T(8,128)S(1)}, f32[7,8,128]{2,1,0:T(8,128)S(1)}, u32[]{:S(2)}, u32[]{:S(2)}) collective-permute-start(f32[7,8,128]{2,1,0:T(8,128)S(1)} %get-tuple-element.24), channel_id=1, source_target_pairs={{1,0},{2,1},{3,2},{4,3},{5,4},{6,5},{7,6},{8,7},{9,8},{10,9},{11,1... | collective-permute-start | bytes 86024 | tf_op jit(solution)/shard_map/ppermute | solution.py:553
  15.1 7.0 %collective-permute-start.3 = (f32[7,8,128]{2,1,0:T(8,128)S(1)}, f32[7,8,128]{2,1,0:T(8,128)S(1)}, u32[]{:S(2)}, u32[]{:S(2)}) collective-permute-start(f32[7,8,128]{2,1,0:T(8,128)S(1)} %get-tuple-element.25), channel_id=1, source_target_pairs={{0,1},{1,2},{2,3},{3,4},{4,5},{5,6},{6,7},{7,8},{8,9},{9,10},{10,1... | collective-permute-start | bytes 86024 | tf_op jit(solution)/shard_map/ppermute | solution.py:554
  22.8 5.3 %collective-permute-start.4 = (f32[15,8,128]{2,1,0:T(8,128)S(1)}, f32[15,8,128]{2,1,0:T(8,128)S(1)}, u32[]{:S(2)}, u32[]{:S(2)}) collective-permute-start(f32[15,8,128]{2,1,0:T(8,128)S(1)} %get-tuple-element.30), channel_id=1, source_target_pairs={{0,12},{12,0},{24,36},{36,24},{48,60},{60,48},{72,84},{84,72},{96,... | collective-permute-start | bytes 184328 | tf_op jit(solution)/shard_map/ppermute | solution.py:542
  24.8 8.9 %collective-permute-start.5 = (f32[15,8,128]{2,1,0:T(8,128)S(1)}, f32[15,8,128]{2,1,0:T(8,128)S(1)}, u32[]{:S(2)}, u32[]{:S(2)}) collective-permute-start(f32[15,8,128]{2,1,0:T(8,128)S(1)} %get-tuple-element.31), channel_id=1, source_target_pairs={{0,756},{12,24},{24,12},{36,48},{48,36},{60,72},{72,60},{84,96},{9... | collective-permute-start | bytes 184328 | tf_op jit(solution)/shard_map/ppermute | solution.py:541
  34.6 5.3 %collective-permute-start.6 = (f32[15,8,128]{2,1,0:T(8,128)S(1)}, f32[15,8,128]{2,1,0:T(8,128)S(1)}, u32[]{:S(2)}, u32[]{:S(2)}) collective-permute-start(f32[15,8,128]{2,1,0:T(8,128)S(1)} %get-tuple-element.34), channel_id=1, source_target_pairs={{0,12},{12,0},{24,36},{36,24},{48,60},{60,48},{72,84},{84,72},{96,... | collective-permute-start | bytes 184328 | tf_op jit(solution)/shard_map/ppermute | solution.py:542
  36.5 8.9 %collective-permute-start.7 = (f32[15,8,128]{2,1,0:T(8,128)S(1)}, f32[15,8,128]{2,1,0:T(8,128)S(1)}, u32[]{:S(2)}, u32[]{:S(2)}) collective-permute-start(f32[15,8,128]{2,1,0:T(8,128)S(1)} %get-tuple-element.35), channel_id=1, source_target_pairs={{0,756},{12,24},{24,12},{36,48},{48,36},{60,72},{72,60},{84,96},{9... | collective-permute-start | bytes 184328 | tf_op jit(solution)/shard_map/ppermute | solution.py:541
  46.5 5.3 %collective-permute-start.8 = (f32[9,8,128]{2,1,0:T(8,128)S(1)}, f32[9,8,128]{2,1,0:T(8,128)S(1)}, u32[]{:S(2)}, u32[]{:S(2)}) collective-permute-start(f32[9,8,128]{2,1,0:T(8,128)S(1)} %get-tuple-element.40), channel_id=1, source_target_pairs={{0,12},{12,0},{24,36},{36,24},{48,60},{60,48},{72,84},{84,72},{96,... | collective-permute-start | bytes 110600 | tf_op jit(solution)/shard_map/ppermute | solution.py:542
  48.4 8.6 %collective-permute-start.9 = (f32[9,8,128]{2,1,0:T(8,128)S(1)}, f32[9,8,128]{2,1,0:T(8,128)S(1)}, u32[]{:S(2)}, u32[]{:S(2)}) collective-permute-start(f32[9,8,128]{2,1,0:T(8,128)S(1)} %get-tuple-element.41), channel_id=1, source_target_pairs={{0,756},{12,24},{24,12},{36,48},{48,36},{60,72},{72,60},{84,96},{9... | collective-permute-start | bytes 110600 | tf_op jit(solution)/shard_map/ppermute | solution.py:541

commit v5 on v4

--- a/solution.py
+++ b/solution.py
@@ -54,10 +54,17 @@
     return nearest
 
 
+def low_ghosts(rows, below, above, meta):
+    lo = ghost_rows([rows[0], rows[1]], [below[1], below[0]], [above[0], above[1]], *meta[:3])
+    return [lo[1], lo[0]]
+
+
+def high_ghosts(rows, below, above, meta):
+    return ghost_rows([rows[-1], rows[-2]], [above[0], above[1]], [below[1], below[0]], *meta[3:])
+
+
 def with_ghosts(rows, below, above, meta):
-    lo = ghost_rows([rows[0], rows[1]], [below[1], below[0]], [above[0], above[1]], *meta[:3])
-    hi = ghost_rows([rows[-1], rows[-2]], [above[0], above[1]], [below[1], below[0]], *meta[3:])
-    return [lo[1], lo[0]] + rows + [hi[0], hi[1]]
+    return low_ghosts(rows, below, above, meta) + rows + high_ghosts(rows, below, above, meta)
 
 
 def flux(q, a, d):
@@ -129,7 +136,7 @@
     return acc + (up - down)
 
 
-def residual2(padded, halo, a, unit):
+def residual2(padded, halo, a, unit, start=0):
     n = len(padded) - 4
     k, j = iota_k(), iota_j()
     weights = j_weights(unit)
@@ -143,7 +150,7 @@
         edge.append([jnp.where(upper, f[u] + C1 * tile[u], f[u] - C1 * tile[u]) for u in range(NV)])
     beside = []
     for i in range(n):
-        g, first = unit * i // 4, unit * i % 4 * SEG + HALO
+        g, first = unit * (start + i) // 4, unit * (start + i) % 4 * SEG + HALO
         beside.append([(rotl(halo[g][u], -first), rotl(edge[g][u], -first)) for u in range(NV)])
     fi = {m: flux(padded[m], a, 0) for m in range(1, n + 3)}
     result = []
@@ -319,7 +326,19 @@
     even = is_even()
     for n, (lo, hi) in enumerate(zip(first, last)):
         ma[at + n] = jnp.where(even, hi, lo)
-        mb[at + n] = jnp.where(even, lo, hi)
+        if mb is not None:
+            mb[at + n] = jnp.where(even, lo, hi)
+
+
+def at_link(work):
+    even = is_even()
+    pl.when(even)(lambda: work(True))
+    pl.when(jnp.logical_not(even))(lambda: work(False))
+
+
+def put(ref, at, tiles):
+    for n, x in enumerate(tiles):
+        ref[at + n] = x
 
 
 def receive(ga, gb, at, count):
@@ -341,11 +360,18 @@
     return [below[:NV], below[NV:]], [above[:NV], above[NV:]]
 
 
-def send_halo(ma, mb, at, halo):
+def halo_first(halo):
     low = seg() < 2
-    first = [jnp.where(low, halo[0][p], rotl(halo[0][p + 1], 64)) for p in range(0, NV, 2)]
-    last = [jnp.where(low, rotl(halo[1][p + 1], 64), halo[1][p]) for p in range(0, NV, 2)]
-    send(ma, mb, at, first, last)
+    return [jnp.where(low, halo[0][p], rotl(halo[0][p + 1], 64)) for p in range(0, NV, 2)]
+
+
+def halo_last(halo):
+    low = seg() < 2
+    return [jnp.where(low, rotl(halo[1][p + 1], 64), halo[1][p]) for p in range(0, NV, 2)]
+
+
+def send_halo(ma, at, halo):
+    send(ma, None, at, halo_first(halo), halo_last(halo))
 
 
 def receive_halo(ga, gb, at):
@@ -357,17 +383,13 @@
     return spread(below), spread(above)
 
 
-def send_coarse(ma, mb, at, first, second):
+def joined(first, second):
     j_even, k_even = iota_j() % 2 == 0, iota_k() % 2 == 0
-
-    def joined(r0, r1):
-        out = []
-        for v in range(NV):
-            x, y = (jnp.where(j_even, first[r][v], second[r][v]) for r in (r0, r1))
-            out.append(jnp.where(k_even, x, y))
-        return out
-
-    send(ma, mb, at, joined(0, 1), joined(-2, -1))
+    out = []
+    for v in range(NV):
+        x, y = (jnp.where(j_even, first[r][v], second[r][v]) for r in range(2))
+        out.append(jnp.where(k_even, x, y))
+    return out
 
 
 def receive_coarse(ga, gb, at):
@@ -420,62 +442,123 @@
     return [[start[i][v] - (0.5 * factor * dt[i]) * twice[i][v] for v in range(NV)] for i in range(len(start))]
 
 
-def first_kernel(table_ref, q_ref, dt_ref, ga, gb, from_right, from_left, t1_ref, h0_ref, dth_ref, ma, mb):
+def link_rows(rows, below, above, meta, count, lower):
+    if lower:
+        return low_ghosts(rows, below, above, meta) + rows[: count + 2]
+    return rows[-count - 2 :] + high_ghosts(rows, below, above, meta)
+
+
+def at_end(rows, count, lower):
+    return rows[:count] if lower else rows[-count:]
+
+
+def first_link_kernel(table_ref, q_ref, dt_ref, ga, gb, from_right, from_left, h0_ref, dth_ref, mb):
     a, meta = coefficients(table_ref), meta_of(table_ref)
     h0, dth = unpack(from_right, from_left)
     store_tiles(h0_ref, h0)
-    for g in range(2):
-        dth_ref[g] = dth[g]
-    send_halo(ma, mb, 2 * NV, h0)
+    put(dth_ref, 0, dth)
+
+    def work(lower):
+        rows = load(q_ref, 0, NI)
+        below, above = receive_rows(ga, gb, 0)
+        padded = link_rows(rows, below, above, meta, 2, lower)
+        twice = residual2(padded, h0, a, 1, 0 if lower else NI - 2)
+        dt = at_end([dt_ref[i] for i in range(NI)], 2, lower)
+        done = advance(at_end(rows, 2, lower), dt, twice, 0.4)
+        put(mb, 0, done[0] + done[1])
+        put(mb, 2 * NV, halo_first(h0) if lower else halo_last(h0))
+
+    at_link(work)
+
+
+def first_kernel(table_ref, q_ref, dt_ref, ga, gb, h0_ref, t1_ref, ma):
+    a, meta = coefficients(table_ref), meta_of(table_ref)
+    h0 = load_tiles(h0_ref)
+    send_halo(ma, 2 * NV, h0)
     t0 = load(q_ref, 0, NI)
     below, above = receive_rows(ga, gb, 0)
     twice = residual2(with_ghosts(t0, below, above, meta), h0, a, 1)
     t1 = advance(t0, [dt_ref[i] for i in range(NI)], twice, 0.4)
     store(t1_ref, 0, t1)
-    send_rows(ma, mb, 0, t1)
-
-
-def second_kernel(
-    table_ref, q_ref, t1_ref, h0_ref, ends_ref, dt_ref, dth_ref, ga, gb, t2_ref, h1_ref, ma, mb
-):
+    send_rows(ma, None, 0, t1)
+
+
+def second_link_kernel(table_ref, q_ref, t1_ref, h0_ref, ends_ref, dt_ref, dth_ref, ga, gb, h1_ref, mb):
     a, meta = coefficients(table_ref), meta_of(table_ref)
     h0 = load_tiles(h0_ref)
     below, above = receive_halo(ga, gb, 2 * NV)
     twice = halo_residual2(h0, halo_ghost(h0, below, above, meta), load_tiles(ends_ref), a)
     h1 = masked(advance(h0, [dth_ref[g] for g in range(2)], twice, 0.4))
     store_tiles(h1_ref, h1)
-    send_halo(ma, mb, 2 * NV, h1)
+
+    def work(lower):
+        rows = load(t1_ref, 0, NI)
+        below, above = receive_rows(ga, gb, 0)
+        padded = link_rows(rows, below, above, meta, 2, lower)
+        twice = residual2(padded, h1, a, 1, 0 if lower else NI - 2)
+        dt = at_end([dt_ref[i] for i in range(NI)], 2, lower)
+        done = advance(at_end(load(q_ref, 0, NI), 2, lower), dt, twice, 1.0)
+        put(mb, 0, done[0] + done[1])
+        put(mb, 2 * NV, halo_first(h1) if lower else halo_last(h1))
+
+    at_link(work)
+
+
+def second_kernel(table_ref, q_ref, t1_ref, h1_ref, dt_ref, ga, gb, t2_ref, ma):
+    a, meta = coefficients(table_ref), meta_of(table_ref)
+    h1 = load_tiles(h1_ref)
+    send_halo(ma, 2 * NV, h1)
     t0, t1 = load(q_ref, 0, NI), load(t1_ref, 0, NI)
     below, above = receive_rows(ga, gb, 0)
     twice = residual2(with_ghosts(t1, below, above, meta), h1, a, 1)
     t2 = advance(t0, [dt_ref[i] for i in range(NI)], twice, 1.0)
     store(t2_ref, 0, t2)
-    send_rows(ma, mb, 0, t2)
-
-
-def third_kernel(
-    table_ref, t1_ref, t2_ref, h0_ref, h1_ref, dt_ref, dth_ref, ga, gb, res_ref, h2_ref, c1_ref, mean_ref, ma, mb
-):
+    send_rows(ma, None, 0, t2)
+
+
+def first_section(rows, res, dt):
+    start, mean = restrict_rows(rows), restrict_rows(res)
+    c1 = []
+    for c in range(len(start)):
+        step = cell_mean(dt[2 * c] + dt[2 * c + 1])
+        c1.append([start[c][v] - (0.4 * step) * mean[c][v] for v in range(NV)])
+    return start, mean, c1
+
+
+def third_link_kernel(table_ref, t1_ref, t2_ref, h0_ref, h1_ref, dt_ref, dth_ref, ga, gb, h2_ref, mb):
     a, meta = coefficients(table_ref), meta_of(table_ref)
     h0, h1 = load_tiles(h0_ref), load_tiles(h1_ref)
     below, above = receive_halo(ga, gb, 2 * NV)
     twice = halo_residual2(h1, halo_ghost(h1, below, above, meta), pack_ends(load(t1_ref, 0, NI)), a)
     h2 = masked(advance(h0, [dth_ref[g] for g in range(2)], twice, 1.0))
     store_tiles(h2_ref, h2)
-    send_halo(ma, mb, NV, h2)
-    t2 = load(t2_ref, 0, NI)
+
+    def work(lower):
+        rows = load(t2_ref, 0, NI)
+        below, above = receive_rows(ga, gb, 0)
+        padded = link_rows(rows, below, above, meta, 4, lower)
+        twice = residual2(padded, h2, a, 1, 0 if lower else NI - 4)
+        res = [[0.5 * x for x in row] for row in twice]
+        dt = at_end([dt_ref[i] for i in range(NI)], 4, lower)
+        start, _, c1 = first_section(at_end(rows, 4, lower), res, dt)
+        put(mb, 0, joined(c1, start))
+        put(mb, NV, halo_first(h2) if lower else halo_last(h2))
+
+    at_link(work)
+
+
+def third_kernel(table_ref, t2_ref, h2_ref, dt_ref, ga, gb, res_ref, c1_ref, mean_ref, ma):
+    a, meta = coefficients(table_ref), meta_of(table_ref)
+    h2, t2 = load_tiles(h2_ref), load(t2_ref, 0, NI)
+    send_halo(ma, NV, h2)
     below, above = receive_rows(ga, gb, 0)
     twice = residual2(with_ghosts(t2, below, above, meta), h2, a, 1)
     res = [[0.5 * x for x in row] for row in twice]
     store(res_ref, 0, res)
-    start, mean = restrict_rows(t2), restrict_rows(res)
+    start, mean, c1 = first_section(t2, res, [dt_ref[i] for i in range(NI)])
     store(mean_ref, 0, mean)
-    c1 = []
-    for c in range(NI // 2):
-        step = cell_mean(dt_ref[2 * c] + dt_ref[2 * c + 1])
-        c1.append([start[c][v] - (0.4 * step) * mean[c][v] for v in range(NV)])
     store(c1_ref, 0, c1)
-    send_coarse(ma, mb, 0, c1, start)
+    send(ma, None, 0, joined(c1[:2], start[:2]), joined(c1[2:], start[2:]))
 
 
 def fourth_kernel(table_ref, t2_ref, h2_ref, c1_ref, mean_ref, dt_ref, dth_ref, res_ref, ga, gb, out_hbm, res_hbm, out_ref, sems):
@@ -554,25 +637,26 @@
     from_left = lax.ppermute(to_right, "sub", ahead)
 
     message = tiles_of(2 * NV + NV // 2)
-    t1, h0, dth, ma, mb = call(
-        first_kernel,
+    h0, dth, mb = call(
+        first_link_kernel,
         (table, flow_state, timestep, ga, gb, from_right, from_left),
-        (field(NI), pair, tiles_of(2), message, message),
+        (pair, tiles_of(2), message),
     )
+    t1, ma = call(first_kernel, (table, flow_state, timestep, ga, gb, h0), (field(NI), message))
     ga, gb = exchange(ma, mb)
 
-    t2, h1, ma, mb = call(
-        second_kernel,
-        (table, flow_state, t1, h0, ends, timestep, dth, ga, gb),
-        (field(NI), pair, message, message),
+    h1, mb = call(
+        second_link_kernel, (table, flow_state, t1, h0, ends, timestep, dth, ga, gb), (pair, message)
     )
+    t2, ma = call(second_kernel, (table, flow_state, t1, h1, timestep, ga, gb), (field(NI), message))
     ga, gb = exchange(ma, mb)
 
     message = tiles_of(NV + NV // 2)
-    res, h2, c1, mean, ma, mb = call(
+    h2, mb = call(third_link_kernel, (table, t1, t2, h0, h1, timestep, dth, ga, gb), (pair, message))
+    res, c1, mean, ma = call(
         third_kernel,
-        (table, t1, t2, h0, h1, timestep, dth, ga, gb),
-        (field(NI), pair, field(NI // 2), field(NI // 2), message, message),
+        (table, t2, h2, timestep, ga, gb),
+        (field(NI), field(NI // 2), field(NI // 2), message),
     )
     ga, gb = exchange(ma, mb)
 

time: 59.4 us -> 54.8 us (0.923)
  the two profiles are of different devices: /device:TPU:512 before, /device:TPU:1 now
where the time goes in v5:
time: 54.8 us; the launch traced here: 54.4 us
  starting transfers between devices  43 us (78%)
  Pallas kernels  6.96 us (13%)
  waiting for transfers between devices  2.7 us (5%)
  local copies, waits for them, and re-layouts  0.91 us (2%)
  between operations  0.86 us (2%)
    ppermute x4, starting transfers between devices, exchange(): ga = lax.ppermute(ma, 'blk', chip)  27.1 us
    ppermute x4, starting transfers between devices, exchange(): gb = lax.ppermute(mb, 'blk', link)  10.5 us
    pallas_call x10, Pallas kernels, call(): pl.pallas_call(kernel, out_shape=[jax.ShapeDtypeStruct(shape, jnp.float32...  6.96 us
    ppermute x1, starting transfers between devices, cycle(): from_left = lax.ppermute(to_right, 'sub', ahead)  3.99 us
    ppermute x4, waiting for transfers between devices, exchange(): ga = lax.ppermute(ma, 'blk', chip)  2.56 us
    ppermute x1, starting transfers between devices, cycle(): from_right = lax.ppermute(to_left, 'sub', back)  1.29 us
  transfers between devices with their start and end apart: 10, of which 4 were waited for; matrix products, arithmetic and copies ran while one was open for 0% of the time, Pallas kernels for 6%

profile of v5, /device:TPU:1, one launch (start us, length us, event | category | flops | bytes accessed | tf_op | source)
XLA Modules:
  0.0 54.4 jit_solution(8056913819411095311)
XLA Ops:
  0.6 0.0 copy-start.1
  0.6 0.0 copy-start
  0.7 0.7 %copy-done.1 = f32[8,8,128]{2,1,0:T(8,128)S(1)} copy-done((f32[8,8,128]{2,1,0:T(8,128)S(1)}, f32[8,8,128]{2,1,0:T(8,128)}, u32[]{:S(2)}) %copy-start.1) | copy-done | bytes 32792
  1.4 0.2 copy-done
  1.6 0.0 copy-start.2
  1.6 0.2 shard_map.70
  1.8 12.4 %collective-permute-start = (f32[12,8,128]{2,1,0:T(8,128)S(1)}, f32[12,8,128]{2,1,0:T(8,128)S(1)}, u32[]{:S(2)}, u32[]{:S(2)}) collective-permute-start(f32[12,8,128]{2,1,0:T(8,128)S(1)} %get-tuple-element.22), channel_id=1, source_target_pairs={{0,12},{12,0},{24,36},{36,24},{48,60},{60,48},{72,84},{84,72},{96,... | collective-permute-start | bytes 147464 | tf_op jit(solution)/shard_map/ppermute | solution.py:625
  14.1 1.9 %collective-permute-start.1 = (f32[12,8,128]{2,1,0:T(8,128)S(1)}, f32[12,8,128]{2,1,0:T(8,128)S(1)}, u32[]{:S(2)}, u32[]{:S(2)}) collective-permute-start(f32[12,8,128]{2,1,0:T(8,128)S(1)} %get-tuple-element.23), channel_id=1, source_target_pairs={{0,756},{12,24},{24,12},{36,48},{48,36},{60,72},{72,60},{84,96},{9... | collective-permute-start | bytes 147464 | tf_op jit(solution)/shard_map/ppermute | solution.py:624
  16.1 0.0 copy-start.3
  16.1 0.0 copy-start.4
  16.1 1.3 %collective-permute-start.2 = (f32[7,8,128]{2,1,0:T(8,128)S(1)}, f32[7,8,128]{2,1,0:T(8,128)S(1)}, u32[]{:S(2)}, u32[]{:S(2)}) collective-permute-start(f32[7,8,128]{2,1,0:T(8,128)S(1)} %get-tuple-element.24), channel_id=1, source_target_pairs={{1,0},{2,1},{3,2},{4,3},{5,4},{6,5},{7,6},{8,7},{9,8},{10,9},{11,1... | collective-permute-start | bytes 86024 | tf_op jit(solution)/shard_map/ppermute | solution.py:636
  17.4 4.0 %collective-permute-start.3 = (f32[7,8,128]{2,1,0:T(8,128)S(1)}, f32[7,8,128]{2,1,0:T(8,128)S(1)}, u32[]{:S(2)}, u32[]{:S(2)}) collective-permute-start(f32[7,8,128]{2,1,0:T(8,128)S(1)} %get-tuple-element.25), channel_id=1, source_target_pairs={{0,1},{1,2},{2,3},{3,4},{4,5},{5,6},{6,7},{7,8},{8,9},{9,10},{10,1... | collective-permute-start | bytes 86024 | tf_op jit(solution)/shard_map/ppermute | solution.py:637
  21.4 0.0 copy-done.2
  21.4 0.0 copy-done.3
  21.4 0.0 copy-done.4
  21.4 0.8 %shard_map.68.table_ref = f32[114,8,128]{2,1,0:T(8,128)S(1)} custom-call(f32[3,6,6]{2,1,0:T(8,128)S(1)} %copy-done.2, s32[1,2]{1,0:T(1,128)S(1)} %copy-done.3, s32[1,2]{1,0:T(1,128)S(1)} %copy-done.4), custom_call_target="tpu_custom_call" | custom-call | tf_op jit(solution)/shard_map/pallas_call | solution.py:605
  22.2 0.0 collective-permute-done.2.from_right
  22.2 0.1 collective-permute-done.3.from_left
  22.4 0.0 collective-permute-done.ga
  22.4 0.0 collective-permute-done.1.gb
  22.4 0.3 shard_map.71
  22.7 4.8 %collective-permute-start.5 = (f32[15,8,128]{2,1,0:T(8,128)S(1)}, f32[15,8,128]{2,1,0:T(8,128)S(1)}, u32[]{:S(2)}, u32[]{:S(2)}) collective-permute-start(f32[15,8,128]{2,1,0:T(8,128)S(1)} %get-tuple-element.31), channel_id=1, source_target_pairs={{0,756},{12,24},{24,12},{36,48},{48,36},{60,72},{72,60},{84,96},{9... | collective-permute-start | bytes 184328 | tf_op jit(solution)/shard_map/ppermute | solution.py:624
  27.5 0.7 %shard_map.72 = (f32[6,8,8,128]{3,2,1,0:T(8,128)S(1)}, f32[15,8,128]{2,1,0:T(8,128)S(1)}) custom-call(f32[114,8,128]{2,1,0:T(8,128)S(1)} %shard_map.68.table_ref, f32[6,8,8,128]{3,2,1,0:T(8,128)S(1)} %copy-done, f32[8,8,128]{2,1,0:T(8,128)S(1)} %copy-done.1, f32[12,8,128]{2,1,0:T(8,128)S(1)} %collective-permute-done.ga, ...), custom_call_target="tpu_custom_call" | custom-call | tf_op jit(solution)/shard_map/pallas_call | solution.py:605
  28.2 4.1 %collective-permute-start.4 = (f32[15,8,128]{2,1,0:T(8,128)S(1)}, f32[15,8,128]{2,1,0:T(8,128)S(1)}, u32[]{:S(2)}, u32[]{:S(2)}) collective-permute-start(f32[15,8,128]{2,1,0:T(8,128)S(1)} %get-tuple-element.30), channel_id=1, source_target_pairs={{0,12},{12,0},{24,36},{36,24},{48,60},{60,48},{72,84},{84,72},{96,... | collective-permute-start | bytes 184328 | tf_op jit(solution)/shard_map/ppermute | solution.py:625
  32.3 0.0 collective-permute-done.5.gb
  32.4 0.9 %collective-permute-done.4.ga = f32[15,8,128]{2,1,0:T(8,128)S(1)} collective-permute-done((f32[15,8,128]{2,1,0:T(8,128)S(1)}, f32[15,8,128]{2,1,0:T(8,128)S(1)}, u32[]{:S(2)}, u32[]{:S(2)}) %collective-permute-start.4) | collective-permute-done | bytes 61472 | tf_op jit(solution)/shard_map/ppermute | solution.py:625
  33.2 0.5 shard_map.73
  33.8 1.9 %collective-permute-start.7 = (f32[15,8,128]{2,1,0:T(8,128)S(1)}, f32[15,8,128]{2,1,0:T(8,128)S(1)}, u32[]{:S(2)}, u32[]{:S(2)}) collective-permute-start(f32[15,8,128]{2,1,0:T(8,128)S(1)} %get-tuple-element.35), channel_id=1, source_target_pairs={{0,756},{12,24},{24,12},{36,48},{48,36},{60,72},{72,60},{84,96},{9... | collective-permute-start | bytes 184328 | tf_op jit(solution)/shard_map/ppermute | solution.py:624
  35.7 0.7 %shard_map.74 = (f32[6,8,8,128]{3,2,1,0:T(8,128)S(1)}, f32[15,8,128]{2,1,0:T(8,128)S(1)}) custom-call(f32[114,8,128]{2,1,0:T(8,128)S(1)} %shard_map.68.table_ref, f32[6,8,8,128]{3,2,1,0:T(8,128)S(1)} %copy-done, f32[6,8,8,128]{3,2,1,0:T(8,128)S(1)} %get-tuple-element.27.t1_ref, f32[2,6,8,128]{3,2,1,0:T(8,128)S(1)} %get-tuple-element.32.h1_ref, ...), custom_call_target="tpu_custom_call" | custom-call | tf_op jit(solution)/shard_map/pallas_call | solution.py:605
  36.4 5.3 %collective-permute-start.6 = (f32[15,8,128]{2,1,0:T(8,128)S(1)}, f32[15,8,128]{2,1,0:T(8,128)S(1)}, u32[]{:S(2)}, u32[]{:S(2)}) collective-permute-start(f32[15,8,128]{2,1,0:T(8,128)S(1)} %get-tuple-element.34), channel_id=1, source_target_pairs={{0,12},{12,0},{24,36},{36,24},{48,60},{60,48},{72,84},{84,72},{96,... | collective-permute-start | bytes 184328 | tf_op jit(solution)/shard_map/ppermute | solution.py:625
  41.7 0.0 collective-permute-done.7.gb
  41.8 0.9 %collective-permute-done.6.ga = f32[15,8,128]{2,1,0:T(8,128)S(1)} collective-permute-done((f32[15,8,128]{2,1,0:T(8,128)S(1)}, f32[15,8,128]{2,1,0:T(8,128)S(1)}, u32[]{:S(2)}, u32[]{:S(2)}) %collective-permute-start.6) | collective-permute-done | bytes 61472 | tf_op jit(solution)/shard_map/ppermute | solution.py:625
  42.6 0.8 %shard_map.75 = (f32[2,6,8,128]{3,2,1,0:T(8,128)S(1)}, f32[9,8,128]{2,1,0:T(8,128)S(1)}) custom-call(f32[114,8,128]{2,1,0:T(8,128)S(1)} %shard_map.68.table_ref, f32[6,8,8,128]{3,2,1,0:T(8,128)S(1)} %get-tuple-element.27.t1_ref, f32[6,8,8,128]{3,2,1,0:T(8,128)S(1)} %get-tuple-element.33.t2_ref, f32[2,6,8,128]{3,2,1,0:T(8,128)S(1)} %get-tuple-element.26.h0_ref, ...), custom_call_target="tpu_custom_call" | custom-call | tf_op jit(solution)/shard_map/pallas_call | solution.py:605
  43.4 1.9 %collective-permute-start.9 = (f32[9,8,128]{2,1,0:T(8,128)S(1)}, f32[9,8,128]{2,1,0:T(8,128)S(1)}, u32[]{:S(2)}, u32[]{:S(2)}) collective-permute-start(f32[9,8,128]{2,1,0:T(8,128)S(1)} %get-tuple-element.41), channel_id=1, source_target_pairs={{0,756},{12,24},{24,12},{36,48},{48,36},{60,72},{72,60},{84,96},{9... | collective-permute-start | bytes 110600 | tf_op jit(solution)/shard_map/ppermute | solution.py:624
  45.3 0.8 %shard_map.76 = (f32[6,8,8,128]{3,2,1,0:T(8,128)S(1)}, f32[6,4,8,128]{3,2,1,0:T(8,128)S(1)}, f32[6,4,8,128]{3,2,1,0:T(8,128)S(1)}, f32[9,8,128]{2,1,0:T(8,128)S(1)}) custom-call(f32[114,8,128]{2,1,0:T(8,128)S(1)} %shard_map.68.table_ref, f32[6,8,8,128]{3,2,1,0:T(8,128)S(1)} %get-tuple-element.33.t2_ref, f32[2,6,8,128]{3,2,1,0:T(8,128)S(1)} %get-tuple-element.36.h2_ref, ...), custom_call_target="tpu_custom_call" | custom-call | tf_op jit(solution)/shard_map/pallas_call | solution.py:605
  46.2 5.3 %collective-permute-start.8 = (f32[9,8,128]{2,1,0:T(8,128)S(1)}, f32[9,8,128]{2,1,0:T(8,128)S(1)}, u32[]{:S(2)}, u32[]{:S(2)}) collective-permute-start(f32[9,8,128]{2,1,0:T(8,128)S(1)} %get-tuple-element.40), channel_id=1, source_target_pairs={{0,12},{12,0},{24,36},{36,24},{48,60},{60,48},{72,84},{84,72},{96,... | collective-permute-start | bytes 110600 | tf_op jit(solution)/shard_map/ppermute | solution.py:625
  51.5 0.0 collective-permute-done.9.gb
  51.5 0.8 %collective-permute-done.8.ga = f32[9,8,128]{2,1,0:T(8,128)S(1)} collective-permute-done((f32[9,8,128]{2,1,0:T(8,128)S(1)}, f32[9,8,128]{2,1,0:T(8,128)S(1)}, u32[]{:S(2)}, u32[]{:S(2)}) %collective-permute-start.8) | collective-permute-done | bytes 36896 | tf_op jit(solution)/shard_map/ppermute | solution.py:625
  52.4 2.0 %shard_map.77 = (f32[6,8,8,128]{3,2,1,0:T(8,128)}, f32[6,8,8,128]{3,2,1,0:T(8,128)}) custom-call(f32[114,8,128]{2,1,0:T(8,128)S(1)} %shard_map.68.table_ref, f32[6,8,8,128]{3,2,1,0:T(8,128)S(1)} %get-tuple-element.33.t2_ref, f32[2,6,8,128]{3,2,1,0:T(8,128)S(1)} %get-tuple-element.36.h2_ref, f32[6,4,8,128]{3,2,1,0:T(8,128)S(1)} %get-tuple-element.37.c1_ref, ...), custom_call_target="tpu_custom_call" | custom-call | tf_op jit(solution)/shard_map/pallas_call | solution.py:605
  (1 shorter events, 0.0 us)
Async XLA Ops:
  0.6 0.8 %copy-start.1 = (f32[8,8,128]{2,1,0:T(8,128)S(1)}, f32[8,8,128]{2,1,0:T(8,128)}, u32[]{:S(2)}) copy-start(f32[8,8,128]{2,1,0:T(8,128)} %dt_ref.15) | copy-start | bytes 98308
  0.6 0.9 %copy-start = (f32[6,8,8,128]{3,2,1,0:T(8,128)S(1)}, f32[6,8,8,128]{3,2,1,0:T(8,128)}, u32[]{:S(2)}) copy-start(f32[6,8,8,128]{3,2,1,0:T(8,128)} %q_ref.9) | copy-start | bytes 589828
  1.6 19.8 %copy-start.2 = (f32[3,6,6]{2,1,0:T(8,128)S(1)}, f32[3,6,6]{2,1,0:T(8,128)}, u32[]{:S(2)}) copy-start(f32[3,6,6]{2,1,0:T(8,128)} %a_ref.1) | copy-start | bytes 1300
  1.8 20.6 %collective-permute-start = (f32[12,8,128]{2,1,0:T(8,128)S(1)}, f32[12,8,128]{2,1,0:T(8,128)S(1)}, u32[]{:S(2)}, u32[]{:S(2)}) collective-permute-start(f32[12,8,128]{2,1,0:T(8,128)S(1)} %get-tuple-element.22), channel_id=1, source_target_pairs={{0,12},{12,0},{24,36},{36,24},{48,60},{60,48},{72,84},{84,72},{96,... | collective-permute-start | bytes 147464 | tf_op jit(solution)/shard_map/ppermute | solution.py:625
  14.1 8.2 %collective-permute-start.1 = (f32[12,8,128]{2,1,0:T(8,128)S(1)}, f32[12,8,128]{2,1,0:T(8,128)S(1)}, u32[]{:S(2)}, u32[]{:S(2)}) collective-permute-start(f32[12,8,128]{2,1,0:T(8,128)S(1)} %get-tuple-element.23), channel_id=1, source_target_pairs={{0,756},{12,24},{24,12},{36,48},{48,36},{60,72},{72,60},{84,96},{9... | collective-permute-start | bytes 147464 | tf_op jit(solution)/shard_map/ppermute | solution.py:624
  16.1 5.3 %copy-start.3 = (s32[1,2]{1,0:T(1,128)S(1)}, s32[1,2]{1,0:T(1,128)}, u32[]{:S(2)}) copy-start(s32[1,2]{1,0:T(1,128)} %type_ref.1) | copy-start | bytes 28
  16.1 5.3 %copy-start.4 = (s32[1,2]{1,0:T(1,128)S(1)}, s32[1,2]{1,0:T(1,128)}, u32[]{:S(2)}) copy-start(s32[1,2]{1,0:T(1,128)} %rot_ref.1) | copy-start | bytes 28
  16.1 6.1 %collective-permute-start.2 = (f32[7,8,128]{2,1,0:T(8,128)S(1)}, f32[7,8,128]{2,1,0:T(8,128)S(1)}, u32[]{:S(2)}, u32[]{:S(2)}) collective-permute-start(f32[7,8,128]{2,1,0:T(8,128)S(1)} %get-tuple-element.24), channel_id=1, source_target_pairs={{1,0},{2,1},{3,2},{4,3},{5,4},{6,5},{7,6},{8,7},{9,8},{10,9},{11,1... | collective-permute-start | bytes 86024 | tf_op jit(solution)/shard_map/ppermute | solution.py:636
  17.4 5.0 %collective-permute-start.3 = (f32[7,8,128]{2,1,0:T(8,128)S(1)}, f32[7,8,128]{2,1,0:T(8,128)S(1)}, u32[]{:S(2)}, u32[]{:S(2)}) collective-permute-start(f32[7,8,128]{2,1,0:T(8,128)S(1)} %get-tuple-element.25), channel_id=1, source_target_pairs={{0,1},{1,2},{2,3},{3,4},{4,5},{5,6},{6,7},{7,8},{8,9},{9,10},{10,1... | collective-permute-start | bytes 86024 | tf_op jit(solution)/shard_map/ppermute | solution.py:637
  22.7 9.6 %collective-permute-start.5 = (f32[15,8,128]{2,1,0:T(8,128)S(1)}, f32[15,8,128]{2,1,0:T(8,128)S(1)}, u32[]{:S(2)}, u32[]{:S(2)}) collective-permute-start(f32[15,8,128]{2,1,0:T(8,128)S(1)} %get-tuple-element.31), channel_id=1, source_target_pairs={{0,756},{12,24},{24,12},{36,48},{48,36},{60,72},{72,60},{84,96},{9... | collective-permute-start | bytes 184328 | tf_op jit(solution)/shard_map/ppermute | solution.py:624
  28.2 5.0 %collective-permute-start.4 = (f32[15,8,128]{2,1,0:T(8,128)S(1)}, f32[15,8,128]{2,1,0:T(8,128)S(1)}, u32[]{:S(2)}, u32[]{:S(2)}) collective-permute-start(f32[15,8,128]{2,1,0:T(8,128)S(1)} %get-tuple-element.30), channel_id=1, source_target_pairs={{0,12},{12,0},{24,36},{36,24},{48,60},{60,48},{72,84},{84,72},{96,... | collective-permute-start | bytes 184328 | tf_op jit(solution)/shard_map/ppermute | solution.py:625
  33.8 8.0 %collective-permute-start.7 = (f32[15,8,128]{2,1,0:T(8,128)S(1)}, f32[15,8,128]{2,1,0:T(8,128)S(1)}, u32[]{:S(2)}, u32[]{:S(2)}) collective-permute-start(f32[15,8,128]{2,1,0:T(8,128)S(1)} %get-tuple-element.35), channel_id=1, source_target_pairs={{0,756},{12,24},{24,12},{36,48},{48,36},{60,72},{72,60},{84,96},{9... | collective-permute-start | bytes 184328 | tf_op jit(solution)/shard_map/ppermute | solution.py:624
  36.4 6.2 %collective-permute-start.6 = (f32[15,8,128]{2,1,0:T(8,128)S(1)}, f32[15,8,128]{2,1,0:T(8,128)S(1)}, u32[]{:S(2)}, u32[]{:S(2)}) collective-permute-start(f32[15,8,128]{2,1,0:T(8,128)S(1)} %get-tuple-element.34), channel_id=1, source_target_pairs={{0,12},{12,0},{24,36},{36,24},{48,60},{60,48},{72,84},{84,72},{96,... | collective-permute-start | bytes 184328 | tf_op jit(solution)/shard_map/ppermute | solution.py:625
  43.4 8.1 %collective-permute-start.9 = (f32[9,8,128]{2,1,0:T(8,128)S(1)}, f32[9,8,128]{2,1,0:T(8,128)S(1)}, u32[]{:S(2)}, u32[]{:S(2)}) collective-permute-start(f32[9,8,128]{2,1,0:T(8,128)S(1)} %get-tuple-element.41), channel_id=1, source_target_pairs={{0,756},{12,24},{24,12},{36,48},{48,36},{60,72},{72,60},{84,96},{9... | collective-permute-start | bytes 110600 | tf_op jit(solution)/shard_map/ppermute | solution.py:624
  46.2 6.2 %collective-permute-start.8 = (f32[9,8,128]{2,1,0:T(8,128)S(1)}, f32[9,8,128]{2,1,0:T(8,128)S(1)}, u32[]{:S(2)}, u32[]{:S(2)}) collective-permute-start(f32[9,8,128]{2,1,0:T(8,128)S(1)} %get-tuple-element.40), channel_id=1, source_target_pairs={{0,12},{12,0},{24,36},{36,24},{48,60},{60,48},{72,84},{84,72},{96,... | collective-permute-start | bytes 110600 | tf_op jit(solution)/shard_map/ppermute | solution.py:625

commit v6 on v5

--- a/solution.py
+++ b/solution.py
@@ -145,11 +145,11 @@
     high1, high2 = k >= 128 - unit, k >= 128 - 2 * unit
     upper = place() >= HALO
     edge = []
-    for tile in halo:
+    for tile in halo or ():
         f = flux(tile, a, 2)
         edge.append([jnp.where(upper, f[u] + C1 * tile[u], f[u] - C1 * tile[u]) for u in range(NV)])
     beside = []
-    for i in range(n):
+    for i in range(n if halo else 0):
         g, first = unit * (start + i) // 4, unit * (start + i) % 4 * SEG + HALO
         beside.append([(rotl(halo[g][u], -first), rotl(edge[g][u], -first)) for u in range(NV)])
     fi = {m: flux(padded[m], a, 0) for m in range(1, n + 3)}
@@ -162,7 +162,7 @@
         row = []
         for u in range(NV):
             x = q[u]
-            s, e = beside[i][u]
+            s, e = beside[i][u] if halo else (0.0, 0.0)
             acc = second_index(fj, gj, q, u, unit, weights, ends)
             acc = acc + (fi[m + 1][u] - fi[m - 1][u])
             acc = acc + C1 * (padded[m + 1][u] + padded[m - 1][u]) + C2 * (padded[m + 2][u] + padded[m - 2][u])
@@ -452,35 +452,29 @@
     return rows[:count] if lower else rows[-count:]
 
 
-def first_link_kernel(table_ref, q_ref, dt_ref, ga, gb, from_right, from_left, h0_ref, dth_ref, mb):
+def first_ends_kernel(table_ref, q_ref, dt_ref, ga, gb, from_right, from_left, h0_ref, dth_ref, ma, mb):
     a, meta = coefficients(table_ref), meta_of(table_ref)
     h0, dth = unpack(from_right, from_left)
     store_tiles(h0_ref, h0)
     put(dth_ref, 0, dth)
-
-    def work(lower):
-        rows = load(q_ref, 0, NI)
-        below, above = receive_rows(ga, gb, 0)
+    send(ma, mb, 2 * NV, halo_first(h0), halo_last(h0))
+    rows = load(q_ref, 0, NI)
+    below, above = receive_rows(ga, gb, 0)
+    ends = []
+    for lower in (True, False):
         padded = link_rows(rows, below, above, meta, 2, lower)
         twice = residual2(padded, h0, a, 1, 0 if lower else NI - 2)
         dt = at_end([dt_ref[i] for i in range(NI)], 2, lower)
-        done = advance(at_end(rows, 2, lower), dt, twice, 0.4)
-        put(mb, 0, done[0] + done[1])
-        put(mb, 2 * NV, halo_first(h0) if lower else halo_last(h0))
-
-    at_link(work)
-
-
-def first_kernel(table_ref, q_ref, dt_ref, ga, gb, h0_ref, t1_ref, ma):
+        ends += advance(at_end(rows, 2, lower), dt, twice, 0.4)
+    send_rows(ma, mb, 0, ends)
+
+
+def first_kernel(table_ref, q_ref, dt_ref, ga, gb, h0_ref, t1_ref):
     a, meta = coefficients(table_ref), meta_of(table_ref)
-    h0 = load_tiles(h0_ref)
-    send_halo(ma, 2 * NV, h0)
     t0 = load(q_ref, 0, NI)
     below, above = receive_rows(ga, gb, 0)
-    twice = residual2(with_ghosts(t0, below, above, meta), h0, a, 1)
-    t1 = advance(t0, [dt_ref[i] for i in range(NI)], twice, 0.4)
-    store(t1_ref, 0, t1)
-    send_rows(ma, None, 0, t1)
+    twice = residual2(with_ghosts(t0, below, above, meta), load_tiles(h0_ref), a, 1)
+    store(t1_ref, 0, advance(t0, [dt_ref[i] for i in range(NI)], twice, 0.4))
 
 
 def second_link_kernel(table_ref, q_ref, t1_ref, h0_ref, ends_ref, dt_ref, dth_ref, ga, gb, h1_ref, mb):
@@ -547,7 +541,7 @@
     at_link(work)
 
 
-def third_kernel(table_ref, t2_ref, h2_ref, dt_ref, ga, gb, res_ref, c1_ref, mean_ref, ma):
+def third_kernel(table_ref, t2_ref, h2_ref, dt_ref, ga, gb, res_ref, start_ref, c1_ref, mean_ref, ma):
     a, meta = coefficients(table_ref), meta_of(table_ref)
     h2, t2 = load_tiles(h2_ref), load(t2_ref, 0, NI)
     send_halo(ma, NV, h2)
@@ -556,12 +550,58 @@
     res = [[0.5 * x for x in row] for row in twice]
     store(res_ref, 0, res)
     start, mean, c1 = first_section(t2, res, [dt_ref[i] for i in range(NI)])
+    store(start_ref, 0, start)
     store(mean_ref, 0, mean)
     store(c1_ref, 0, c1)
     send(ma, None, 0, joined(c1[:2], start[:2]), joined(c1[2:], start[2:]))
 
 
-def fourth_kernel(table_ref, t2_ref, h2_ref, c1_ref, mean_ref, dt_ref, dth_ref, res_ref, ga, gb, out_hbm, res_hbm, out_ref, sems):
+def early_kernel(table_ref, start_ref, c1_ref, h2_ref, part_ref):
+    a = coefficients(table_ref)
+    half = NI // 2
+    h2 = load_tiles(h2_ref)
+    start_h = halo_means(h2[0] + h2[1])
+    ghost = [[jnp.zeros((8, 128), jnp.float32)] * NV] * 2
+    twice0 = residual2(ghost + load(start_ref, 0, half) + ghost, [start_h[:NV], start_h[NV:]], a, 2)
+    twice1 = residual2(ghost + load(c1_ref, 0, half) + ghost, None, a, 2)
+    store(part_ref, 0, [[twice1[c][v] - twice0[c][v] for v in range(NV)] for c in range(half)])
+
+
+def halo_part(halo, a):
+    o, k = place(), iota_k()
+    high1, low1 = (o == HALO - 2) | (o == HALO - 1), (o == HALO) | (o == HALO + 1)
+    high2, low2 = (o >= HALO - 4) & (o < HALO), (o >= HALO) & (o < HALO + 4)
+    spread = []
+    for tile in halo:
+        f = flux(tile, a, 2)
+        row = []
+        for u in range(NV):
+            x = tile[u]
+            w = jnp.where(high1, rotl(f[u] + C1 * x, -2), 0.0) - jnp.where(low1, rotl(f[u] - C1 * x, 2), 0.0)
+            row.append(w + C2 * (jnp.where(high2, rotl(x, -4), 0.0) + jnp.where(low2, rotl(x, 4), 0.0)))
+        spread.append(row)
+    near = (k < 4) | (k >= 124)
+    out = []
+    for c in range(NI // 2):
+        g, first = 2 * c // 4, 2 * c % 4 * SEG + HALO
+        out.append([jnp.where(near, rotl(spread[g][u], -first), 0.0) for u in range(NV)])
+    return out
+
+
+def ghost_part(low, high, a):
+    fl, fh = flux(low[1], a, 0), flux(high[0], a, 0)
+    rows = ([], [], [], [])
+    for u in range(NV):
+        rows[0].append(C1 * low[1][u] + C2 * low[0][u] - fl[u])
+        rows[1].append(C2 * low[1][u])
+        rows[2].append(C2 * high[0][u])
+        rows[3].append(C1 * high[0][u] + C2 * high[1][u] + fh[u])
+    return rows
+
+
+def fourth_kernel(
+    table_ref, t2_ref, h2_ref, start_ref, c1_ref, mean_ref, part_ref, dt_ref, dth_ref, res_ref, ga, gb, out_hbm, res_hbm, out_ref, sems
+):
     a, meta = coefficients(table_ref), meta_of(table_ref)
     half = NI // 2
     copies = [pltpu.make_async_copy(res_ref, res_hbm, sems.at[half])]
@@ -572,16 +612,16 @@
     means = halo_means(h2[0] + h2[1] + [dth_ref[0], dth_ref[1]] + twice[0] + twice[1])
     start_h, step_h, mean_h = means[: 2 * NV], means[2 * NV : 2 * NV + 2], means[2 * NV + 2 :]
     c1_h = [start_h[t] - (0.2 * step_h[t // NV]) * mean_h[t] for t in range(2 * NV)]
-    start_h = [start_h[:NV], start_h[NV:]]
-    c1_h = masked([c1_h[:NV], c1_h[NV:]])
-    start, c1 = restrict_rows(t2), load(c1_ref, 0, half)
-    (below1, above1), (below0, above0) = receive_coarse(ga, gb, 0)
-    twice0 = residual2(with_ghosts(start, below0, above0, meta), start_h, a, 2)
-    twice1 = residual2(with_ghosts(c1, below1, above1, meta), c1_h, a, 2)
+    halo = halo_part(masked([c1_h[:NV], c1_h[NV:]]), a)
+    ghosts = []
+    for ref, (below, above) in zip((c1_ref, start_ref), receive_coarse(ga, gb, 0)):
+        rows = load(ref, 0, half)
+        ghosts.append(ghost_part(low_ghosts(rows, below, above, meta), high_ghosts(rows, below, above, meta), a))
     for c in range(half):
         step = cell_mean(dt_ref[2 * c] + dt_ref[2 * c + 1])
         for v in range(NV):
-            change = -step * (0.5 * (twice1[c][v] - twice0[c][v]) + mean_ref[v, c])
+            twice_change = part_ref[v, c] + (ghosts[0][c][v] - ghosts[1][c][v]) + halo[c][v]
+            change = -step * (0.5 * twice_change + mean_ref[v, c])
             out_ref[v, 2 * c] = t2[2 * c][v] + change
             out_ref[v, 2 * c + 1] = t2[2 * c + 1][v] + change
     for c in range(half):
@@ -637,12 +677,12 @@
     from_left = lax.ppermute(to_right, "sub", ahead)
 
     message = tiles_of(2 * NV + NV // 2)
-    h0, dth, mb = call(
-        first_link_kernel,
+    h0, dth, ma, mb = call(
+        first_ends_kernel,
         (table, flow_state, timestep, ga, gb, from_right, from_left),
-        (pair, tiles_of(2), message),
+        (pair, tiles_of(2), message, message),
     )
-    t1, ma = call(first_kernel, (table, flow_state, timestep, ga, gb, h0), (field(NI), message))
+    (t1,) = call(first_kernel, (table, flow_state, timestep, ga, gb, h0), (field(NI),))
     ga, gb = exchange(ma, mb)
 
     h1, mb = call(
@@ -653,16 +693,17 @@
 
     message = tiles_of(NV + NV // 2)
     h2, mb = call(third_link_kernel, (table, t1, t2, h0, h1, timestep, dth, ga, gb), (pair, message))
-    res, c1, mean, ma = call(
+    res, start, c1, mean, ma = call(
         third_kernel,
         (table, t2, h2, timestep, ga, gb),
-        (field(NI), field(NI // 2), field(NI // 2), message),
+        (field(NI), field(NI // 2), field(NI // 2), field(NI // 2), message),
     )
+    (part,) = call(early_kernel, (table, start, c1, h2), (field(NI // 2),))
     ga, gb = exchange(ma, mb)
 
     updated, res = call(
         fourth_kernel,
-        (table, t2, h2, c1, mean, timestep, dth, res, ga, gb),
+        (table, t2, h2, start, c1, mean, part, timestep, dth, res, ga, gb),
         (field(NI), field(NI)),
         out_space=pltpu.HBM,
         scratch=(pltpu.VMEM(field(NI), jnp.float32), pltpu.SemaphoreType.DMA((NI // 2 + 1,))),

time: 54.8 us -> 56.3 us (1.027)
  starting transfers between devices: 43 us -> 44.6 us
    ppermute x4, waiting for transfers between devices: 2.56 us -> 1.01 us  [exchange(): ga = lax.ppermute(ma, 'blk', chip)]
    ppermute x4, waiting for transfers between devices: 0.01 us -> 1.17 us  [exchange(): gb = lax.ppermute(mb, 'blk', link)]
    ppermute x4, starting transfers between devices: 27.1 us -> 28.2 us  [exchange(): ga = lax.ppermute(ma, 'blk', chip)]
    ppermute x4, starting transfers between devices: 10.5 us -> 11.1 us  [exchange(): gb = lax.ppermute(mb, 'blk', link)]
    pallas_call x10 -> x11, Pallas kernels: 6.96 us -> 7.18 us  [call(): pl.pallas_call(kernel, out_shape=[jax.ShapeDtypeStruct(shape, jnp.float32...]
  transfers between devices with their start and end apart: 10 -> 10, of which waited for: 4 -> 4; matrix products, arithmetic and copies ran while one was open for 0% -> 0% of each run, Pallas kernels for 6% -> 7%
where the time goes in v6:
time: 56.3 us; the launch traced here: 55.9 us
  starting transfers between devices  44.6 us (79%)
  Pallas kernels  7.18 us (13%)
  waiting for transfers between devices  2.3 us (4%)
  local copies, waits for them, and re-layouts  0.91 us (2%)
  between operations  0.87 us (2%)
    ppermute x4, starting transfers between devices, exchange(): ga = lax.ppermute(ma, 'blk', chip)  28.2 us
    ppermute x4, starting transfers between devices, exchange(): gb = lax.ppermute(mb, 'blk', link)  11.1 us
    pallas_call x11, Pallas kernels, call(): pl.pallas_call(kernel, out_shape=[jax.ShapeDtypeStruct(shape, jnp.float32...  7.18 us
    ppermute x1, starting transfers between devices, cycle(): from_left = lax.ppermute(to_right, 'sub', ahead)  3.99 us
    ppermute x1, starting transfers between devices, cycle(): from_right = lax.ppermute(to_left, 'sub', back)  1.29 us
    ppermute x4, waiting for transfers between devices, exchange(): gb = lax.ppermute(mb, 'blk', link)  1.17 us
  transfers between devices with their start and end apart: 10, of which 4 were waited for; matrix products, arithmetic and copies ran while one was open for 0% of the time, Pallas kernels for 7%

profile of v6, /device:TPU:1, one launch (start us, length us, event | category | flops | bytes accessed | tf_op | source)
XLA Modules:
  0.0 55.9 jit_solution(8541085353546101404)
XLA Ops:
  0.6 0.0 copy-start.1
  0.6 0.0 copy-start
  0.7 0.7 %copy-done.1 = f32[8,8,128]{2,1,0:T(8,128)S(1)} copy-done((f32[8,8,128]{2,1,0:T(8,128)S(1)}, f32[8,8,128]{2,1,0:T(8,128)}, u32[]{:S(2)}) %copy-start.1) | copy-done | bytes 32792
  1.4 0.2 copy-done
  1.6 0.0 copy-start.2
  1.6 0.2 shard_map.70
  1.8 12.4 %collective-permute-start = (f32[12,8,128]{2,1,0:T(8,128)S(1)}, f32[12,8,128]{2,1,0:T(8,128)S(1)}, u32[]{:S(2)}, u32[]{:S(2)}) collective-permute-start(f32[12,8,128]{2,1,0:T(8,128)S(1)} %get-tuple-element.22), channel_id=1, source_target_pairs={{0,12},{12,0},{24,36},{36,24},{48,60},{60,48},{72,84},{84,72},{96,... | collective-permute-start | bytes 147464 | tf_op jit(solution)/shard_map/ppermute | solution.py:665
  14.1 1.9 %collective-permute-start.1 = (f32[12,8,128]{2,1,0:T(8,128)S(1)}, f32[12,8,128]{2,1,0:T(8,128)S(1)}, u32[]{:S(2)}, u32[]{:S(2)}) collective-permute-start(f32[12,8,128]{2,1,0:T(8,128)S(1)} %get-tuple-element.23), channel_id=1, source_target_pairs={{0,756},{12,24},{24,12},{36,48},{48,36},{60,72},{72,60},{84,96},{9... | collective-permute-start | bytes 147464 | tf_op jit(solution)/shard_map/ppermute | solution.py:664
  16.1 0.0 copy-start.3
  16.1 0.0 copy-start.4
  16.1 1.3 %collective-permute-start.2 = (f32[7,8,128]{2,1,0:T(8,128)S(1)}, f32[7,8,128]{2,1,0:T(8,128)S(1)}, u32[]{:S(2)}, u32[]{:S(2)}) collective-permute-start(f32[7,8,128]{2,1,0:T(8,128)S(1)} %get-tuple-element.24), channel_id=1, source_target_pairs={{1,0},{2,1},{3,2},{4,3},{5,4},{6,5},{7,6},{8,7},{9,8},{10,9},{11,1... | collective-permute-start | bytes 86024 | tf_op jit(solution)/shard_map/ppermute | solution.py:676
  17.4 4.0 %collective-permute-start.3 = (f32[7,8,128]{2,1,0:T(8,128)S(1)}, f32[7,8,128]{2,1,0:T(8,128)S(1)}, u32[]{:S(2)}, u32[]{:S(2)}) collective-permute-start(f32[7,8,128]{2,1,0:T(8,128)S(1)} %get-tuple-element.25), channel_id=1, source_target_pairs={{0,1},{1,2},{2,3},{3,4},{4,5},{5,6},{6,7},{7,8},{8,9},{9,10},{10,1... | collective-permute-start | bytes 86024 | tf_op jit(solution)/shard_map/ppermute | solution.py:677
  21.4 0.0 copy-done.2
  21.4 0.0 copy-done.3
  21.4 0.0 copy-done.4
  21.4 0.8 %shard_map.68.table_ref = f32[114,8,128]{2,1,0:T(8,128)S(1)} custom-call(f32[3,6,6]{2,1,0:T(8,128)S(1)} %copy-done.2, s32[1,2]{1,0:T(1,128)S(1)} %copy-done.3, s32[1,2]{1,0:T(1,128)S(1)} %copy-done.4), custom_call_target="tpu_custom_call" | custom-call | tf_op jit(solution)/shard_map/pallas_call | solution.py:645
  22.2 0.0 collective-permute-done.2.from_right
  22.2 0.1 collective-permute-done.3.from_left
  22.4 0.0 collective-permute-done.ga
  22.4 0.0 collective-permute-done.1.gb
  22.4 0.5 shard_map.71
  22.9 3.1 %collective-permute-start.4 = (f32[15,8,128]{2,1,0:T(8,128)S(1)}, f32[15,8,128]{2,1,0:T(8,128)S(1)}, u32[]{:S(2)}, u32[]{:S(2)}) collective-permute-start(f32[15,8,128]{2,1,0:T(8,128)S(1)} %get-tuple-element.29), channel_id=1, source_target_pairs={{0,12},{12,0},{24,36},{36,24},{48,60},{60,48},{72,84},{84,72},{96,... | collective-permute-start | bytes 184328 | tf_op jit(solution)/shard_map/ppermute | solution.py:665
  25.9 3.6 %collective-permute-start.5 = (f32[15,8,128]{2,1,0:T(8,128)S(1)}, f32[15,8,128]{2,1,0:T(8,128)S(1)}, u32[]{:S(2)}, u32[]{:S(2)}) collective-permute-start(f32[15,8,128]{2,1,0:T(8,128)S(1)} %get-tuple-element.30), channel_id=1, source_target_pairs={{0,756},{12,24},{24,12},{36,48},{48,36},{60,72},{72,60},{84,96},{9... | collective-permute-start | bytes 184328 | tf_op jit(solution)/shard_map/ppermute | solution.py:664
  29.6 0.7 %shard_map.72.t1_ref = f32[6,8,8,128]{3,2,1,0:T(8,128)S(1)} custom-call(f32[114,8,128]{2,1,0:T(8,128)S(1)} %shard_map.68.table_ref, f32[6,8,8,128]{3,2,1,0:T(8,128)S(1)} %copy-done, f32[8,8,128]{2,1,0:T(8,128)S(1)} %copy-done.1, f32[12,8,128]{2,1,0:T(8,128)S(1)} %collective-permute-done.ga, f32[12,8,128]{2,1,0:T(8,128)S(1)} %collective-permute-done.1.gb, ...), custom_call_target="tpu_custom_call" | custom-call | tf_op jit(solution)/shard_map/pallas_call | solution.py:645
  30.3 0.0 collective-permute-done.4.ga
  30.3 1.2 %collective-permute-done.5.gb = f32[15,8,128]{2,1,0:T(8,128)S(1)} collective-permute-done((f32[15,8,128]{2,1,0:T(8,128)S(1)}, f32[15,8,128]{2,1,0:T(8,128)S(1)}, u32[]{:S(2)}, u32[]{:S(2)}) %collective-permute-start.5) | collective-permute-done | bytes 61472 | tf_op jit(solution)/shard_map/ppermute | solution.py:664
  31.5 0.5 shard_map.73
  32.0 3.6 %collective-permute-start.7 = (f32[15,8,128]{2,1,0:T(8,128)S(1)}, f32[15,8,128]{2,1,0:T(8,128)S(1)}, u32[]{:S(2)}, u32[]{:S(2)}) collective-permute-start(f32[15,8,128]{2,1,0:T(8,128)S(1)} %get-tuple-element.34), channel_id=1, source_target_pairs={{0,756},{12,24},{24,12},{36,48},{48,36},{60,72},{72,60},{84,96},{9... | collective-permute-start | bytes 184328 | tf_op jit(solution)/shard_map/ppermute | solution.py:664
  35.7 0.7 %shard_map.74 = (f32[6,8,8,128]{3,2,1,0:T(8,128)S(1)}, f32[15,8,128]{2,1,0:T(8,128)S(1)}) custom-call(f32[114,8,128]{2,1,0:T(8,128)S(1)} %shard_map.68.table_ref, f32[6,8,8,128]{3,2,1,0:T(8,128)S(1)} %copy-done, f32[6,8,8,128]{3,2,1,0:T(8,128)S(1)} %shard_map.72.t1_ref, f32[2,6,8,128]{3,2,1,0:T(8,128)S(1)} %get-tuple-element.31.h1_ref, ...), custom_call_target="tpu_custom_call" | custom-call | tf_op jit(solution)/shard_map/pallas_call | solution.py:645
  36.4 7.4 %collective-permute-start.6 = (f32[15,8,128]{2,1,0:T(8,128)S(1)}, f32[15,8,128]{2,1,0:T(8,128)S(1)}, u32[]{:S(2)}, u32[]{:S(2)}) collective-permute-start(f32[15,8,128]{2,1,0:T(8,128)S(1)} %get-tuple-element.33), channel_id=1, source_target_pairs={{0,12},{12,0},{24,36},{36,24},{48,60},{60,48},{72,84},{84,72},{96,... | collective-permute-start | bytes 184328 | tf_op jit(solution)/shard_map/ppermute | solution.py:665
  43.8 0.0 collective-permute-done.7.gb
  43.8 0.9 %collective-permute-done.6.ga = f32[15,8,128]{2,1,0:T(8,128)S(1)} collective-permute-done((f32[15,8,128]{2,1,0:T(8,128)S(1)}, f32[15,8,128]{2,1,0:T(8,128)S(1)}, u32[]{:S(2)}, u32[]{:S(2)}) %collective-permute-start.6) | collective-permute-done | bytes 61472 | tf_op jit(solution)/shard_map/ppermute | solution.py:665
  44.7 0.8 %shard_map.75 = (f32[2,6,8,128]{3,2,1,0:T(8,128)S(1)}, f32[9,8,128]{2,1,0:T(8,128)S(1)}) custom-call(f32[114,8,128]{2,1,0:T(8,128)S(1)} %shard_map.68.table_ref, f32[6,8,8,128]{3,2,1,0:T(8,128)S(1)} %shard_map.72.t1_ref, f32[6,8,8,128]{3,2,1,0:T(8,128)S(1)} %get-tuple-element.32.t2_ref, f32[2,6,8,128]{3,2,1,0:T(8,128)S(1)} %get-tuple-element.26.h0_ref, ...), custom_call_target="tpu_custom_call" | custom-call | tf_op jit(solution)/shard_map/pallas_call | solution.py:645
  45.5 1.9 %collective-permute-start.9 = (f32[9,8,128]{2,1,0:T(8,128)S(1)}, f32[9,8,128]{2,1,0:T(8,128)S(1)}, u32[]{:S(2)}, u32[]{:S(2)}) collective-permute-start(f32[9,8,128]{2,1,0:T(8,128)S(1)} %get-tuple-element.41), channel_id=1, source_target_pairs={{0,756},{12,24},{24,12},{36,48},{48,36},{60,72},{72,60},{84,96},{9... | collective-permute-start | bytes 110600 | tf_op jit(solution)/shard_map/ppermute | solution.py:664
  47.4 0.8 %shard_map.76 = (f32[6,8,8,128]{3,2,1,0:T(8,128)S(1)}, f32[6,4,8,128]{3,2,1,0:T(8,128)S(1)}, f32[6,4,8,128]{3,2,1,0:T(8,128)S(1)}, f32[6,4,8,128]{3,2,1,0:T(8,128)S(1)}, f32[9,8,128]{2,1,0:T(8,128)S(1)}) custom-call(f32[114,8,128]{2,1,0:T(8,128)S(1)} %shard_map.68.table_ref, f32[6,8,8,128]{3,2,1,0:T(8,128)S(1)} %get-tuple-element.32.t2_ref, ...), custom_call_target="tpu_custom_call" | custom-call | tf_op jit(solution)/shard_map/pallas_call | solution.py:645
  48.3 5.3 %collective-permute-start.8 = (f32[9,8,128]{2,1,0:T(8,128)S(1)}, f32[9,8,128]{2,1,0:T(8,128)S(1)}, u32[]{:S(2)}, u32[]{:S(2)}) collective-permute-start(f32[9,8,128]{2,1,0:T(8,128)S(1)} %get-tuple-element.40), channel_id=1, source_target_pairs={{0,12},{12,0},{24,36},{36,24},{48,60},{60,48},{72,84},{84,72},{96,... | collective-permute-start | bytes 110600 | tf_op jit(solution)/shard_map/ppermute | solution.py:665
  53.6 0.7 %shard_map.77.part_ref = f32[6,4,8,128]{3,2,1,0:T(8,128)S(1)} custom-call(f32[114,8,128]{2,1,0:T(8,128)S(1)} %shard_map.68.table_ref, f32[6,4,8,128]{3,2,1,0:T(8,128)S(1)} %get-tuple-element.36.start_ref, f32[6,4,8,128]{3,2,1,0:T(8,128)S(1)} %get-tuple-element.37.c1_ref, f32[2,6,8,128]{3,2,1,0:T(8,128)S(1)} %get-tuple-element.35.h2_ref), custom_call_target="tpu_custom_call" | custom-call | tf_op jit(solution)/shard_map/pallas_call | solution.py:645
  54.3 0.0 collective-permute-done.9.gb
  54.3 0.1 collective-permute-done.8.ga
  54.5 1.4 %shard_map.78 = (f32[6,8,8,128]{3,2,1,0:T(8,128)}, f32[6,8,8,128]{3,2,1,0:T(8,128)}) custom-call(f32[114,8,128]{2,1,0:T(8,128)S(1)} %shard_map.68.table_ref, f32[6,8,8,128]{3,2,1,0:T(8,128)S(1)} %get-tuple-element.32.t2_ref, f32[2,6,8,128]{3,2,1,0:T(8,128)S(1)} %get-tuple-element.35.h2_ref, f32[6,4,8,128]{3,2,1,0:T(8,128)S(1)} %get-tuple-element.36.start_ref, ...), custom_call_target="tpu_custom_call" | custom-call | tf_op jit(solution)/shard_map/pallas_call | solution.py:645
  (1 shorter events, 0.0 us)
Async XLA Ops:
  0.6 0.8 %copy-start.1 = (f32[8,8,128]{2,1,0:T(8,128)S(1)}, f32[8,8,128]{2,1,0:T(8,128)}, u32[]{:S(2)}) copy-start(f32[8,8,128]{2,1,0:T(8,128)} %dt_ref.15) | copy-start | bytes 98308
  0.6 0.9 %copy-start = (f32[6,8,8,128]{3,2,1,0:T(8,128)S(1)}, f32[6,8,8,128]{3,2,1,0:T(8,128)}, u32[]{:S(2)}) copy-start(f32[6,8,8,128]{3,2,1,0:T(8,128)} %q_ref.9) | copy-start | bytes 589828
  1.6 19.8 %copy-start.2 = (f32[3,6,6]{2,1,0:T(8,128)S(1)}, f32[3,6,6]{2,1,0:T(8,128)}, u32[]{:S(2)}) copy-start(f32[3,6,6]{2,1,0:T(8,128)} %a_ref.1) | copy-start | bytes 1300
  1.8 20.6 %collective-permute-start = (f32[12,8,128]{2,1,0:T(8,128)S(1)}, f32[12,8,128]{2,1,0:T(8,128)S(1)}, u32[]{:S(2)}, u32[]{:S(2)}) collective-permute-start(f32[12,8,128]{2,1,0:T(8,128)S(1)} %get-tuple-element.22), channel_id=1, source_target_pairs={{0,12},{12,0},{24,36},{36,24},{48,60},{60,48},{72,84},{84,72},{96,... | collective-permute-start | bytes 147464 | tf_op jit(solution)/shard_map/ppermute | solution.py:665
  14.1 8.2 %collective-permute-start.1 = (f32[12,8,128]{2,1,0:T(8,128)S(1)}, f32[12,8,128]{2,1,0:T(8,128)S(1)}, u32[]{:S(2)}, u32[]{:S(2)}) collective-permute-start(f32[12,8,128]{2,1,0:T(8,128)S(1)} %get-tuple-element.23), channel_id=1, source_target_pairs={{0,756},{12,24},{24,12},{36,48},{48,36},{60,72},{72,60},{84,96},{9... | collective-permute-start | bytes 147464 | tf_op jit(solution)/shard_map/ppermute | solution.py:664
  16.1 5.3 %copy-start.3 = (s32[1,2]{1,0:T(1,128)S(1)}, s32[1,2]{1,0:T(1,128)}, u32[]{:S(2)}) copy-start(s32[1,2]{1,0:T(1,128)} %type_ref.1) | copy-start | bytes 28
  16.1 5.3 %copy-start.4 = (s32[1,2]{1,0:T(1,128)S(1)}, s32[1,2]{1,0:T(1,128)}, u32[]{:S(2)}) copy-start(s32[1,2]{1,0:T(1,128)} %rot_ref.1) | copy-start | bytes 28
  16.1 6.1 %collective-permute-start.2 = (f32[7,8,128]{2,1,0:T(8,128)S(1)}, f32[7,8,128]{2,1,0:T(8,128)S(1)}, u32[]{:S(2)}, u32[]{:S(2)}) collective-permute-start(f32[7,8,128]{2,1,0:T(8,128)S(1)} %get-tuple-element.24), channel_id=1, source_target_pairs={{1,0},{2,1},{3,2},{4,3},{5,4},{6,5},{7,6},{8,7},{9,8},{10,9},{11,1... | collective-permute-start | bytes 86024 | tf_op jit(solution)/shard_map/ppermute | solution.py:676
  17.4 5.0 %collective-permute-start.3 = (f32[7,8,128]{2,1,0:T(8,128)S(1)}, f32[7,8,128]{2,1,0:T(8,128)S(1)}, u32[]{:S(2)}, u32[]{:S(2)}) collective-permute-start(f32[7,8,128]{2,1,0:T(8,128)S(1)} %get-tuple-element.25), channel_id=1, source_target_pairs={{0,1},{1,2},{2,3},{3,4},{4,5},{5,6},{6,7},{7,8},{8,9},{9,10},{10,1... | collective-permute-start | bytes 86024 | tf_op jit(solution)/shard_map/ppermute | solution.py:677
  22.9 7.4 %collective-permute-start.4 = (f32[15,8,128]{2,1,0:T(8,128)S(1)}, f32[15,8,128]{2,1,0:T(8,128)S(1)}, u32[]{:S(2)}, u32[]{:S(2)}) collective-permute-start(f32[15,8,128]{2,1,0:T(8,128)S(1)} %get-tuple-element.29), channel_id=1, source_target_pairs={{0,12},{12,0},{24,36},{36,24},{48,60},{60,48},{72,84},{84,72},{96,... | collective-permute-start | bytes 184328 | tf_op jit(solution)/shard_map/ppermute | solution.py:665
  25.9 5.5 %collective-permute-start.5 = (f32[15,8,128]{2,1,0:T(8,128)S(1)}, f32[15,8,128]{2,1,0:T(8,128)S(1)}, u32[]{:S(2)}, u32[]{:S(2)}) collective-permute-start(f32[15,8,128]{2,1,0:T(8,128)S(1)} %get-tuple-element.30), channel_id=1, source_target_pairs={{0,756},{12,24},{24,12},{36,48},{48,36},{60,72},{72,60},{84,96},{9... | collective-permute-start | bytes 184328 | tf_op jit(solution)/shard_map/ppermute | solution.py:664
  32.0 11.8 %collective-permute-start.7 = (f32[15,8,128]{2,1,0:T(8,128)S(1)}, f32[15,8,128]{2,1,0:T(8,128)S(1)}, u32[]{:S(2)}, u32[]{:S(2)}) collective-permute-start(f32[15,8,128]{2,1,0:T(8,128)S(1)} %get-tuple-element.34), channel_id=1, source_target_pairs={{0,756},{12,24},{24,12},{36,48},{48,36},{60,72},{72,60},{84,96},{9... | collective-permute-start | bytes 184328 | tf_op jit(solution)/shard_map/ppermute | solution.py:664
  36.4 8.3 %collective-permute-start.6 = (f32[15,8,128]{2,1,0:T(8,128)S(1)}, f32[15,8,128]{2,1,0:T(8,128)S(1)}, u32[]{:S(2)}, u32[]{:S(2)}) collective-permute-start(f32[15,8,128]{2,1,0:T(8,128)S(1)} %get-tuple-element.33), channel_id=1, source_target_pairs={{0,12},{12,0},{24,36},{36,24},{48,60},{60,48},{72,84},{84,72},{96,... | collective-permute-start | bytes 184328 | tf_op jit(solution)/shard_map/ppermute | solution.py:665
  45.5 8.8 %collective-permute-start.9 = (f32[9,8,128]{2,1,0:T(8,128)S(1)}, f32[9,8,128]{2,1,0:T(8,128)S(1)}, u32[]{:S(2)}, u32[]{:S(2)}) collective-permute-start(f32[9,8,128]{2,1,0:T(8,128)S(1)} %get-tuple-element.41), channel_id=1, source_target_pairs={{0,756},{12,24},{24,12},{36,48},{48,36},{60,72},{72,60},{84,96},{9... | collective-permute-start | bytes 110600 | tf_op jit(solution)/shard_map/ppermute | solution.py:664
  48.3 6.2 %collective-permute-start.8 = (f32[9,8,128]{2,1,0:T(8,128)S(1)}, f32[9,8,128]{2,1,0:T(8,128)S(1)}, u32[]{:S(2)}, u32[]{:S(2)}) collective-permute-start(f32[9,8,128]{2,1,0:T(8,128)S(1)} %get-tuple-element.40), channel_id=1, source_target_pairs={{0,12},{12,0},{24,36},{36,24},{48,60},{60,48},{72,84},{84,72},{96,... | collective-permute-start | bytes 110600 | tf_op jit(solution)/shard_map/ppermute | solution.py:665
